TPU v7x, 32 devices: a whole 2x2x4 slice. The times are simulated.
32 devices in a mesh: row: 4 (over x, core), col: 8 (over z, y).
Axes of the slice: x: 2, y: 2, z: 4, core: 2. Of those that a mesh axis runs over, the one named last changes fastest.
Arguments:
- inputs: bfloat16 [8, 512, 2048], P('col', 'row'), may hold values from -6 to 6
- segment_ids: int32 [8, 512], P('col'), may hold values from 0 to 2, never falling along the last dimension, each value on 1 to 256 neighbouring positions
- routes: int32 [8, 512, 6], P('col', 'row'), may hold values from 0 to 63, all different within a row; in each aligned block of 128 rows (0 to 127, 128 to 255, ..., all dimensions but the last counted through in order) at most 16 rows name the same one
- first_gain: float32 [2048], replicated, may hold values from 0.5 to 1.5
- query_weight: bfloat16 [2048, 3072], P('col', 'row'), may hold values from -0.13258252 to 0.13258252
- latent_down: bfloat16 [2048, 576], P('col'), may hold values from -0.13258252 to 0.13258252
- latent_gain: float32 [512], replicated, may hold values from 0.5 to 1.5
- latent_up: bfloat16 [512, 4096], P('col', 'row'), may hold values from -0.25 to 0.25
- output_weight: bfloat16 [2048, 2048], P('row', 'col'), may hold values from -0.375 to 0.375
- second_gain: float32 [2048], replicated, may hold values from 0.5 to 1.5
- router_weight: bfloat16 [2048, 64], replicated, may hold values from -0.25 to 0.25
- shared_gate: bfloat16 [2048, 2816], P('col', 'row'), may hold values from -0.125 to 0.125
- shared_up: bfloat16 [2048, 2816], P('col', 'row'), may hold values from -0.125 to 0.125
- shared_down: bfloat16 [2816, 2048], P('row', 'col'), may hold values from -0.15625 to 0.15625
- expert_gate: bfloat16 [64, 2048, 1408], P('col', None, 'row'), may hold values from -0.125 to 0.125
- expert_up: bfloat16 [64, 2048, 1408], P('col', None, 'row'), may hold values from -0.125 to 0.125
- expert_down: bfloat16 [64, 1408, 2048], P('col', 'row'), may hold values from -0.21875 to 0.21875
- cotangent: float32 [8, 512, 2048], P('col', 'row'), may hold values from -6 to 6
Outputs:
- layer_out: bfloat16 [8, 512, 2048], P('col', 'row')
- input_grad: float32 [8, 512, 2048], P('col', 'row')
- first_gain_grad: float32 [2048], replicated
- query_grad: float32 [2048, 3072], P('col', 'row')
- latent_down_grad: float32 [2048, 576], P('col')
- latent_gain_grad: float32 [512], replicated
- latent_up_grad: float32 [512, 4096], P('col', 'row')
- output_grad: float32 [2048, 2048], P('row', 'col')
- second_gain_grad: float32 [2048], replicated
- router_grad: float32 [2048, 64], replicated
- shared_gate_grad: float32 [2048, 2816], P('col', 'row')
- shared_up_grad: float32 [2048, 2816], P('col', 'row')
- shared_down_grad: float32 [2816, 2048], P('row', 'col')
- expert_gate_grad: float32 [64, 2048, 1408], P('col', None, 'row')
- expert_up_grad: float32 [64, 2048, 1408], P('col', None, 'row')
- expert_down_grad: float32 [64, 1408, 2048], P('col', 'row')
Inputs may be any that keep to these rules, and one draw needn't show every extreme that they name: `segment_ids`: within a sequence the segment numbers never fall; a segment spans at most one half of 512 positions, and some segment spans exactly that many. `routes`: each token names 6 different experts. Among the 128 tokens of one device no expert is named more than 16 times, a bound that some block reaches.
All inputs are finite; a program needn't handle non-finite values.
Results may differ from a plain program's by a relative error of at most 0.03.
Values may be sent and summed in bfloat16 or wider, within the bound.
A program may use at most 448 MiB of HBM per device.

v0:
```python
import jax
import jax.numpy as jnp
from jax import lax
from jax.sharding import PartitionSpec as P

NOPE = 128
ROPE = 64
LATENT = 512
VD = 128
TOPK = 6


EPS = 1e-06
ROWS_CONTRACT = (((0,), (0,)), ((), ()))
COLS_CONTRACT = (((1,), (1,)), ((), ()))


def matmul(left_side, right_side):
    return jnp.dot(left_side, right_side, preferred_element_type=jnp.float32)


def inner_rows(left_side, right_side):
    return lax.dot_general(left_side, right_side, ROWS_CONTRACT, preferred_element_type=jnp.float32)


def outer_cols(left_side, right_side):
    return lax.dot_general(left_side, right_side, COLS_CONTRACT, preferred_element_type=jnp.float32)


def rms_scale(values):
    return lax.rsqrt(jnp.mean(values * values, axis=-1, keepdims=True) + EPS)


def rms_back(values, scaling, gradient):
    return scaling * gradient - values * scaling**3 * jnp.mean(
        gradient * values, axis=-1, keepdims=True
    )


def silu_parts(preact):
    logistic = jax.nn.sigmoid(preact)
    return (preact * logistic, logistic * (1.0 + preact * (1.0 - logistic)))


def angle_tables(length):
    halfway = ROPE // 2
    frequency = 10000.0 ** (-2.0 * jnp.arange(halfway, dtype=jnp.float32) / ROPE)
    angles = jnp.arange(length, dtype=jnp.float32)[:, None] * frequency[None, :]
    return (jnp.cos(angles), jnp.sin(angles))


def rotate(values, cosine_in, sine_in):
    halfway = values.shape[-1] // 2
    leading = values[..., :halfway]
    trailing = values[..., halfway:]
    return jnp.concatenate(
        [leading * cosine_in - trailing * sine_in, leading * sine_in + trailing * cosine_in],
        axis=-1,
    )


def unrotate(values, cosine_in, sine_in):
    halfway = values.shape[-1] // 2
    leading = values[..., :halfway]
    trailing = values[..., halfway:]
    return jnp.concatenate(
        [leading * cosine_in + trailing * sine_in, trailing * cosine_in - leading * sine_in],
        axis=-1,
    )


def token_rows(values):
    return lax.all_gather(values, "row", axis=0, tiled=True)


def row_total(term_fn, row_count):
    return lax.psum_scatter(
        term_fn(jnp.int32(0), lax.axis_size("row") * row_count).astype(jnp.bfloat16),
        "row",
        scatter_dimension=0,
        tiled=True,
    ).astype(jnp.float32)


def to_experts(buffer):
    arrived = lax.all_to_all(buffer, "col", split_axis=0, concat_axis=0, tiled=True)
    return lax.all_gather(arrived, "row", axis=0, tiled=True)


def from_experts(partial_value):
    summed = lax.psum_scatter(
        partial_value.astype(jnp.bfloat16), "row", scatter_dimension=0, tiled=True
    )
    return lax.all_to_all(summed, "col", split_axis=0, concat_axis=0, tiled=True)


def masked_scores(queries, attn_keys, allowed, softmax_scale):
    scores = (
        jnp.einsum("qhd,khd->hqk", queries, attn_keys, preferred_element_type=jnp.float32)
        * softmax_scale
    )
    return jnp.where(allowed[None], scores, -1e30)


def on_device(
    inputs,
    segment_ids,
    routes,
    first_gain,
    query_weight,
    latent_down,
    latent_gain,
    latent_up,
    output_weight,
    second_gain,
    router_weight,
    shared_gate,
    shared_up,
    shared_down,
    expert_gate,
    expert_up,
    expert_down,
    cotangent,
):
    own_rows = inputs.shape[1]
    width = inputs.shape[2]
    experts = router_weight.shape[1]
    local_experts = expert_gate.shape[0]
    capacity = max(2, own_rows // 8)
    stream = inputs.reshape(own_rows, width).astype(jnp.float32)
    grad_out = cotangent.reshape(own_rows, width)
    own_routes = routes.reshape(own_rows, TOPK)
    segments = segment_ids.reshape(-1)
    length = segments.shape[0]
    own_start = lax.axis_index("row") * own_rows
    qk_dim = NOPE + ROPE
    softmax_scale = qk_dim ** (-0.5)
    cosine_table, sine_table = angle_tables(length)
    scale_one = rms_scale(stream)
    normed_one = (stream * scale_one * first_gain).astype(jnp.bfloat16)
    seq_normed = token_rows(normed_one)
    query_all, down_all, expand_all, output_all, gating_all, linear_all, project_all = (
        lax.all_gather(query_weight, "col", axis=0, tiled=True),
        lax.all_gather(latent_down, "col", axis=0, tiled=True),
        lax.all_gather(latent_up, "col", axis=0, tiled=True),
        lax.all_gather(output_weight, "col", axis=1, tiled=True),
        lax.all_gather(shared_gate, "col", axis=0, tiled=True),
        lax.all_gather(shared_up, "col", axis=0, tiled=True),
        lax.all_gather(shared_down, "col", axis=1, tiled=True),
    )
    heads_local = query_all.shape[1] // qk_dim
    gate_block, up_block, down_block = (expert_gate, expert_up, expert_down)
    query_raw = matmul(seq_normed, query_all).reshape(length, heads_local, qk_dim)
    queries = jnp.concatenate(
        [
            query_raw[..., :NOPE],
            rotate(query_raw[..., NOPE:], cosine_table[:, None, :], sine_table[:, None, :]),
        ],
        axis=-1,
    ).astype(jnp.bfloat16)
    latent_all = matmul(seq_normed, down_all)
    latent = latent_all[:, :LATENT]
    scale_latent = rms_scale(latent)
    latent_normed = (latent * scale_latent * latent_gain).astype(jnp.bfloat16)
    keyval = matmul(latent_normed, expand_all).reshape(length, heads_local, NOPE + VD)
    key_rope = rotate(latent_all[:, LATENT:], cosine_table, sine_table)
    attn_keys = jnp.concatenate(
        [keyval[..., :NOPE], jnp.broadcast_to(key_rope[:, None, :], (length, heads_local, ROPE))],
        axis=-1,
    ).astype(jnp.bfloat16)
    values = keyval[..., NOPE:].astype(jnp.bfloat16)
    positions = jnp.arange(length)
    allowed = (positions[:, None] >= positions[None, :]) & (segments[:, None] == segments[None, :])
    scores = masked_scores(queries, attn_keys, allowed, softmax_scale)
    highest = jnp.max(scores, axis=-1, keepdims=True)
    log_total = highest + jnp.log(jnp.sum(jnp.exp(scores - highest), axis=-1, keepdims=True))
    attn_probs = jnp.exp(scores - log_total).astype(jnp.bfloat16)
    heads_out = (
        jnp.einsum("hqk,khd->qhd", attn_probs, values, preferred_element_type=jnp.float32)
        .astype(jnp.bfloat16)
        .reshape(length, heads_local * VD)
    )

    def attn_term(first_row, row_count):
        return matmul(heads_out, output_all)

    residual = stream + row_total(attn_term, own_rows)
    scale_two = rms_scale(residual)
    normed_two = (residual * scale_two * second_gain).astype(jnp.bfloat16)
    logits = matmul(normed_two, router_weight)
    expert_ids = jnp.arange(experts)
    chosen = own_routes[:, :, None] == expert_ids[None, None, :]
    picked = jnp.sum(jnp.where(chosen, logits[:, None, :], 0.0), axis=-1)
    gate_probs = jax.nn.softmax(picked, axis=-1)
    seq_two = token_rows(normed_two)
    shared_pre = matmul(seq_two, gating_all)
    shared_lin = matmul(seq_two, linear_all)
    shared_act, shared_slope = silu_parts(shared_pre)
    shared_hidden = (shared_act * shared_lin).astype(jnp.bfloat16)

    def shared_term(first_row, row_count):
        return matmul(shared_hidden, project_all)

    shared_own = row_total(shared_term, own_rows)
    per_token = jnp.sum(chosen.astype(jnp.int32), axis=1)
    earlier = jnp.cumsum(per_token, axis=0) - per_token
    slot_rank = jnp.sum(jnp.where(chosen, earlier[:, None, :], 0), axis=-1)
    target = own_routes * capacity + slot_rank
    selector = (target[:, :, None] == jnp.arange(experts * capacity)[None, None, :]).astype(
        jnp.bfloat16
    )
    placement = jnp.max(selector, axis=1)
    selector = selector.reshape(own_rows * TOPK, experts * capacity)
    send_rows = (
        inner_rows(placement, normed_two).astype(jnp.bfloat16).reshape(experts, capacity, width)
    )
    arrived = to_experts(send_rows).reshape(-1, local_experts, capacity, width)
    gate_pre = jnp.einsum("sjcd,jdf->sjcf", arrived, gate_block, preferred_element_type=jnp.float32)
    up_lin = jnp.einsum("sjcd,jdf->sjcf", arrived, up_block, preferred_element_type=jnp.float32)
    expert_act, expert_slope = silu_parts(gate_pre)
    expert_hidden = (expert_act * up_lin).astype(jnp.bfloat16)
    partial_out = jnp.einsum(
        "sjcf,jfd->sjcd", expert_hidden, down_block, preferred_element_type=jnp.float32
    )
    returned = from_experts(partial_out.reshape(-1, capacity, width)).reshape(
        experts * capacity, width
    )
    chosen_out = matmul(selector, returned).reshape(own_rows, TOPK, width)
    routed = jnp.sum(gate_probs[:, :, None] * chosen_out, axis=1)
    result = residual + shared_own + routed
    layer_out = result.astype(jnp.bfloat16).reshape(1, own_rows, width)
    gate_grad = jnp.sum(grad_out[:, None, :] * chosen_out, axis=-1)
    picked_grad = gate_probs * (gate_grad - jnp.sum(gate_probs * gate_grad, axis=-1, keepdims=True))
    logit_grad = jnp.sum(jnp.where(chosen, picked_grad[:, :, None], 0.0), axis=1).astype(
        jnp.bfloat16
    )
    router_part = inner_rows(normed_two, logit_grad)
    scaled_grad = (
        (gate_probs[:, :, None] * grad_out[:, None, :])
        .astype(jnp.bfloat16)
        .reshape(own_rows * TOPK, width)
    )
    send_grads = (
        inner_rows(selector, scaled_grad).astype(jnp.bfloat16).reshape(experts, capacity, width)
    )
    arrived_grad = to_experts(send_grads).reshape(-1, local_experts, capacity, width)
    hidden_grad = jnp.einsum(
        "sjcd,jfd->sjcf", arrived_grad, down_block, preferred_element_type=jnp.float32
    )
    expert_down_part = jnp.einsum(
        "sjcf,sjcd->jfd", expert_hidden, arrived_grad, preferred_element_type=jnp.float32
    )
    pre_grad = (hidden_grad * up_lin * expert_slope).astype(jnp.bfloat16)
    lin_grad = (hidden_grad * expert_act).astype(jnp.bfloat16)
    expert_gate_part = jnp.einsum(
        "sjcd,sjcf->jdf", arrived, pre_grad, preferred_element_type=jnp.float32
    )
    expert_up_part = jnp.einsum(
        "sjcd,sjcf->jdf", arrived, lin_grad, preferred_element_type=jnp.float32
    )
    rows_grad = jnp.einsum(
        "sjcf,jdf->sjcd", pre_grad, gate_block, preferred_element_type=jnp.float32
    ) + jnp.einsum("sjcf,jdf->sjcd", lin_grad, up_block, preferred_element_type=jnp.float32)
    returned_grad = from_experts(rows_grad.reshape(-1, capacity, width)).reshape(
        experts * capacity, width
    )
    routed_grad = jnp.sum(matmul(selector, returned_grad).reshape(own_rows, TOPK, width), axis=1)
    expert_gate_grad, expert_up_grad, expert_down_grad = (
        expert_gate_part,
        expert_up_part,
        expert_down_part,
    )
    query_all, down_all, expand_all, output_all, gating_all, linear_all, project_all = (
        lax.all_gather(query_weight, "col", axis=0, tiled=True),
        lax.all_gather(latent_down, "col", axis=0, tiled=True),
        lax.all_gather(latent_up, "col", axis=0, tiled=True),
        lax.all_gather(output_weight, "col", axis=1, tiled=True),
        lax.all_gather(shared_gate, "col", axis=0, tiled=True),
        lax.all_gather(shared_up, "col", axis=0, tiled=True),
        lax.all_gather(shared_down, "col", axis=1, tiled=True),
    )
    seq_grad = token_rows(grad_out.astype(jnp.bfloat16))
    shared_down_part = inner_rows(shared_hidden, seq_grad)
    shared_hidden_grad = outer_cols(seq_grad, project_all)
    shared_pre_grad = (shared_hidden_grad * shared_lin * shared_slope).astype(jnp.bfloat16)
    shared_lin_grad = (shared_hidden_grad * shared_act).astype(jnp.bfloat16)
    shared_gate_part = inner_rows(seq_two, shared_pre_grad)
    shared_up_part = inner_rows(seq_two, shared_lin_grad)

    def shared_back(first_row, row_count):
        return outer_cols(shared_pre_grad, gating_all) + outer_cols(shared_lin_grad, linear_all)

    normed_two_grad = (
        row_total(shared_back, own_rows) + routed_grad + outer_cols(logit_grad, router_weight)
    )
    second_gain_part = jnp.sum(normed_two_grad * residual * scale_two, axis=0)
    residual_grad = grad_out + rms_back(residual, scale_two, normed_two_grad * second_gain)
    seq_resid = token_rows(residual_grad.astype(jnp.bfloat16))
    output_part = inner_rows(heads_out, seq_resid)
    heads_grad = (
        outer_cols(seq_resid, output_all).astype(jnp.bfloat16).reshape(length, heads_local, VD)
    )
    recomputed = jnp.exp(masked_scores(queries, attn_keys, allowed, softmax_scale) - log_total)
    delta_rows = jnp.sum(
        heads_grad.astype(jnp.float32)
        * heads_out.reshape(length, heads_local, VD).astype(jnp.float32),
        axis=-1,
    )
    prob_grad = jnp.einsum("qhd,khd->hqk", heads_grad, values, preferred_element_type=jnp.float32)
    score_grad = (recomputed * (prob_grad - delta_rows.T[:, :, None]) * softmax_scale).astype(
        jnp.bfloat16
    )
    queries_grad = jnp.einsum(
        "hqk,khd->qhd", score_grad, attn_keys, preferred_element_type=jnp.float32
    )
    key_grad = jnp.einsum("hqk,qhd->khd", score_grad, queries, preferred_element_type=jnp.float32)
    value_grad = jnp.einsum(
        "hqk,qhd->khd",
        recomputed.astype(jnp.bfloat16),
        heads_grad,
        preferred_element_type=jnp.float32,
    )
    query_full = (
        jnp.concatenate(
            [
                queries_grad[..., :NOPE],
                unrotate(
                    queries_grad[..., NOPE:], cosine_table[:, None, :], sine_table[:, None, :]
                ),
            ],
            axis=-1,
        )
        .astype(jnp.bfloat16)
        .reshape(length, heads_local * qk_dim)
    )
    query_part = inner_rows(seq_normed, query_full)
    keyval_grad = (
        jnp.concatenate([key_grad[..., :NOPE], value_grad], axis=-1)
        .astype(jnp.bfloat16)
        .reshape(length, heads_local * (NOPE + VD))
    )
    expand_part = inner_rows(latent_normed, keyval_grad)
    latent_normed_part = outer_cols(keyval_grad, expand_all)
    rope_part = jnp.sum(key_grad[..., NOPE:], axis=1)
    latent_normed_grad, rope_raw = (
        lax.psum(latent_normed_part.astype(jnp.bfloat16), "row").astype(jnp.float32),
        lax.psum(rope_part.astype(jnp.bfloat16), "row").astype(jnp.float32),
    )
    rope_grad = unrotate(rope_raw, cosine_table, sine_table)
    latent_gain_part = jnp.sum(
        lax.dynamic_slice_in_dim(
            latent_normed_grad * latent * scale_latent, own_start, own_rows, 0
        ),
        axis=0,
    )
    latent_grad = rms_back(latent, scale_latent, latent_normed_grad * latent_gain)
    down_grad_in = jnp.concatenate([latent_grad, rope_grad], axis=-1).astype(jnp.bfloat16)
    down_part = inner_rows(seq_normed, down_grad_in)

    def input_back(first_row, row_count):
        return outer_cols(query_full, query_all)

    normed_one_grad = row_total(input_back, own_rows) + outer_cols(
        lax.dynamic_slice_in_dim(down_grad_in, own_start, own_rows, 0), down_all
    )
    first_gain_part = jnp.sum(normed_one_grad * stream * scale_one, axis=0)
    input_grad = (
        residual_grad + rms_back(stream, scale_one, normed_one_grad * first_gain)
    ).reshape(1, own_rows, width)
    (
        query_grad,
        latent_down_grad,
        latent_up_grad,
        output_grad,
        shared_gate_grad,
        shared_up_grad,
        shared_down_grad,
    ) = (
        lax.psum_scatter(
            query_part.astype(jnp.bfloat16), "col", scatter_dimension=0, tiled=True
        ).astype(jnp.float32),
        lax.psum_scatter(
            down_part.astype(jnp.bfloat16), "col", scatter_dimension=0, tiled=True
        ).astype(jnp.float32),
        lax.psum_scatter(
            expand_part.astype(jnp.bfloat16), "col", scatter_dimension=0, tiled=True
        ).astype(jnp.float32),
        lax.psum_scatter(
            output_part.astype(jnp.bfloat16), "col", scatter_dimension=1, tiled=True
        ).astype(jnp.float32),
        lax.psum_scatter(
            shared_gate_part.astype(jnp.bfloat16), "col", scatter_dimension=0, tiled=True
        ).astype(jnp.float32),
        lax.psum_scatter(
            shared_up_part.astype(jnp.bfloat16), "col", scatter_dimension=0, tiled=True
        ).astype(jnp.float32),
        lax.psum_scatter(
            shared_down_part.astype(jnp.bfloat16), "col", scatter_dimension=1, tiled=True
        ).astype(jnp.float32),
    )
    first_gain_grad, latent_gain_grad, second_gain_grad, router_grad = lax.psum(
        (first_gain_part, latent_gain_part, second_gain_part, router_part), ("row", "col")
    )
    return (
        layer_out,
        input_grad,
        first_gain_grad,
        query_grad,
        latent_down_grad,
        latent_gain_grad,
        latent_up_grad,
        output_grad,
        second_gain_grad,
        router_grad,
        shared_gate_grad,
        shared_up_grad,
        shared_down_grad,
        expert_gate_grad,
        expert_up_grad,
        expert_down_grad,
    )


def solution(mesh):
    return jax.shard_map(
        on_device,
        mesh=mesh,
        in_specs=(
            P("col", "row", None),
            P("col", None),
            P("col", "row", None),
            P(),
            P("col", "row"),
            P("col", None),
            P(),
            P("col", "row"),
            P("row", "col"),
            P(),
            P(),
            P("col", "row"),
            P("col", "row"),
            P("row", "col"),
            P("col", None, "row"),
            P("col", None, "row"),
            P("col", "row", None),
            P("col", "row", None),
        ),
        out_specs=(
            P("col", "row", None),
            P("col", "row", None),
            P(),
            P("col", "row"),
            P("col", None),
            P(),
            P("col", "row"),
            P("row", "col"),
            P(),
            P(),
            P("col", "row"),
            P("col", "row"),
            P("row", "col"),
            P("col", None, "row"),
            P("col", None, "row"),
            P("col", "row", None),
        ),
        check_vma=False,
    )
```

profile of v0, /device:TPU:8, one launch (start us, length us, event | category | flops | bytes accessed | tf_op | source)
XLA Modules:
  0.0 2063.2 jit_solution(14342955601362016614)
XLA Ops:
  14.9 20.6 all-gather.14.cloned.1.call-done
  35.5 53.7 %all-gather.16.cloned.1.call-done = bf16[2048,576]{0,1:T(8,128)(2,1)} async-done(((bf16[256,576]{0,1:T(8,128)(2,1)}), bf16[2048,576]{0,1:T(8,128)(2,1)}) %all-gather.16.cloned.1.call-update) | async-done | bytes 2359312 | tf_op jit(solution)/shard_map/all_gather | solution.py:144
  89.2 3.7 fusion.86
  94.8 35.7 %all-gather.18.cloned.1.call-done = bf16[512,1024]{1,0:T(8,128)(2,1)} async-done(((bf16[64,1024]{1,0:T(8,128)(2,1)}), bf16[512,1024]{1,0:T(8,128)(2,1)}) %all-gather.18.cloned.1.call-update) | async-done | bytes 1048592 | tf_op jit(solution)/shard_map/all_gather | solution.py:145
  130.5 3.0 convolution_convert_fusion.11
  135.5 57.0 %all-gather.20.cloned.1.call-done = bf16[2048,768]{1,0:T(8,128)(2,1)} async-done(((bf16[256,768]{1,0:T(8,128)(2,1)}), bf16[2048,768]{1,0:T(8,128)(2,1)}) %all-gather.20.cloned.1.call-update) | async-done | bytes 3145744 | tf_op jit(solution)/shard_map/all_gather | solution.py:143
  192.5 4.3 fusion.87
  202.3 39.2 %all-gather.22.cloned.1.call-done = bf16[512,2048]{1,0:T(8,128)(2,1)} async-done(((bf16[512,256]{1,0:T(8,128)(2,1)}), bf16[512,2048]{1,0:T(8,128)(2,1)}) %all-gather.22.cloned.1.call-update) | async-done | bytes 2097168 | tf_op jit(solution)/shard_map/all_gather | solution.py:146
  241.6 4.4 convolution_convert_fusion.9
  247.1 30.2 %reduce-scatter.14.cloned.1.call-done = bf16[128,2048]{1,0:T(8,128)(2,1)} async-done(((bf16[512,2048]{1,0:T(8,128)(2,1)}), bf16[128,2048]{1,0:T(8,128)(2,1)}) %reduce-scatter.14.cloned.1.call-update) | async-done | bytes 524304 | tf_op jit(solution)/shard_map/reduce_scatter | solution.py:77
  281.7 98.1 %all_to_all.20 = bf16[64,16,2048]{2,1,0:T(8,128)(2,1)} all-to-all(bf16[64,16,2048]{2,1,0:T(8,128)(2,1)S(1)} %bitcast.205), channel_id=1, replica_groups=mesh['row'=4,'col'=8] {'col'}, dimensions={0} | all-to-all | bytes 8388608 | tf_op jit(solution)/shard_map/all_to_all | solution.py:86
  381.0 3.8 bitcast_convert_fusion
  384.8 96.3 %all_to_all.21 = bf16[64,16,2048]{2,1,0:T(8,128)(2,1)} all-to-all(bf16[64,16,2048]{2,1,0:T(8,128)(2,1)S(1)} %bitcast.206), channel_id=1, replica_groups=mesh['row'=4,'col'=8] {'col'}, dimensions={0} | all-to-all | bytes 8388608 | tf_op jit(solution)/shard_map/all_to_all | solution.py:86
  481.2 3.1 all-gather.32.cloned.1.call-done
  484.3 15.9 fusion.4
  500.2 17.9 fusion.6
  518.1 73.7 %all-gather.36.cloned.1.call-done = bf16[256,16,2048]{2,1,0:T(8,128)(2,1)} async-done(((bf16[64,16,2048]{2,1,0:T(8,128)(2,1)}), bf16[256,16,2048]{2,1,0:T(8,128)(2,1)}) %all-gather.36.cloned.1.call-update) | async-done | bytes 16777232 | tf_op jit(solution)/shard_map/all_gather | solution.py:87
  591.8 23.6 %fusion.23 = (bf16[32,8,16,352]{3,2,0,1:T(8,128)(2,1)S(1)}, bf16[32,8,16,352]{3,2,0,1:T(8,128)(2,1)}, bf16[32,8,16,352]{3,2,0,1:T(8,128)(2,1)}) fusion(f32[8,32,16,352]{3,2,1,0:T(8,128)} %fusion.6, f32[8,32,16,352]{3,2,1,0:T(8,128)} %fusion.4, bf16[8,352,2048]{2,1,0:T(8,128)(2,1)} %param.34, bf16[32,8,16,2048]{3,2,1,0:T(8,128)(2,1)} %bitcast.223), kind=kOutput, calls=%fused_computation.26 | convolution fusion | flops 5927206912 | bytes 48496640 | tf_op jit(solution)/shard_map/sjcd,jfd->sjcf/dot_general | solution.py:247
  615.4 18.3 convert_bitcast_fusion
  633.7 14.2 copy.112
  652.6 25.6 %fusion.10 = f32[8,32,16,2048]{3,2,1,0:T(8,128)} fusion(bf16[32,8,16,352]{3,2,0,1:T(8,128)(2,1)} %get-tuple-element.30, bf16[8,2048,352]{1,2,0:T(8,128)(2,1)} %param.32), kind=kOutput, calls=%fused_computation.12 | convolution fusion | flops 5905580032 | bytes 47972352 | tf_op jit(solution)/shard_map/sjcf,jdf->sjcd/dot_general | solution.py:261
  678.2 23.3 %fusion.15 = bf16[32,8,16,2048]{3,2,0,1:T(8,128)(2,1)} fusion(f32[8,32,16,2048]{3,2,1,0:T(8,128)} %fusion.10, bf16[32,8,16,352]{3,2,0,1:T(8,128)(2,1)S(1)} %get-tuple-element.29, bf16[8,2048,352]{1,2,0:T(8,128)(2,1)} %param.33), kind=kOutput, calls=%fused_computation.17 | convolution fusion | flops 5922357248 | bytes 64749568 | tf_op jit(solution)/shard_map/sjcf,jdf->sjcd/dot_general | solution.py:263
  701.5 14.3 copy.114
  715.8 57.3 %reduce-scatter.18.cloned.1.call-done = bf16[64,16,2048]{2,1,0:T(8,128)(2,1)} async-done(((bf16[256,16,2048]{2,1,0:T(8,128)(2,1)}), bf16[64,16,2048]{2,1,0:T(8,128)(2,1)}) %reduce-scatter.18.cloned.1.call-update) | async-done | bytes 4194320 | tf_op jit(solution)/shard_map/reduce_scatter | solution.py:91
  773.1 6.3 all-to-all-start.1
  779.4 115.6 %all-gather.26.cloned.1.call-done = bf16[2048,704]{0,1:T(8,128)(2,1)} async-done(((bf16[256,704]{0,1:T(8,128)(2,1)}), bf16[2048,704]{0,1:T(8,128)(2,1)}) %all-gather.26.cloned.1.call-update) | async-done | bytes 2883600 | tf_op jit(solution)/shard_map/all_gather | solution.py:147
  895.0 24.7 %all-gather.24.cloned.1.call-done = bf16[512,2048]{1,0:T(8,128)(2,1)} async-done(((bf16[128,2048]{1,0:T(8,128)(2,1)}), bf16[512,2048]{1,0:T(8,128)(2,1)}) %all-gather.24.cloned.1.call-update) | async-done | bytes 2097168 | tf_op jit(solution)/shard_map/all_gather | solution.py:73
  919.7 5.4 fusion.88
  925.0 54.3 %all-gather.28.cloned.1.call-done = bf16[2048,704]{0,1:T(8,128)(2,1)} async-done(((bf16[256,704]{0,1:T(8,128)(2,1)}), bf16[2048,704]{0,1:T(8,128)(2,1)}) %all-gather.28.cloned.1.call-update) | async-done | bytes 2883600 | tf_op jit(solution)/shard_map/all_gather | solution.py:148
  979.3 4.6 fusion.89
  983.9 20.1 all-gather.34.cloned.1.call-done
  1004.0 59.7 %all-gather.30.cloned.1.call-done = bf16[704,2048]{1,0:T(8,128)(2,1)} async-done(((bf16[704,256]{1,0:T(8,128)(2,1)}), bf16[704,2048]{1,0:T(8,128)(2,1)}) %all-gather.30.cloned.1.call-update) | async-done | bytes 2883600 | tf_op jit(solution)/shard_map/all_gather | solution.py:149
  1063.7 6.5 multiply_convert_fusion.3
  1071.1 3.9 fusion.91
  1075.0 116.8 %reduce-scatter.22.cloned.1.call-done = bf16[64,16,2048]{2,1,0:T(8,128)(2,1)} async-done(((bf16[256,16,2048]{2,1,0:T(8,128)(2,1)}), bf16[64,16,2048]{2,1,0:T(8,128)(2,1)}) %reduce-scatter.22.cloned.1.call-update) | async-done | bytes 4194320 | tf_op jit(solution)/shard_map/reduce_scatter | solution.py:91
  1191.8 6.1 all-to-all-start.3
  1197.9 5.6 add_convert_fusion.1
  1203.5 5.3 convolution_convert_fusion.8
  1208.9 7.8 multiply_reduce_fusion
  1216.8 71.6 %all-to-all-done.3 = bf16[64,16,2048]{2,1,0:T(8,128)(2,1)} async-done(((bf16[64,16,2048]{2,1,0:T(8,128)(2,1)}), bf16[64,16,2048]{2,1,0:T(8,128)(2,1)}, u32[]{:S(2)}, u32[]{:S(2)}) %all-to-all-start.3) | async-done | bytes 4194336 | tf_op jit(solution)/shard_map/all_to_all | solution.py:94
  1288.4 7.1 fusion.42
  1298.1 3.2 fusion.84
  1301.4 22.8 %all-gather.38.cloned.1.call-done = bf16[512,2048]{1,0:T(8,128)(2,1)} async-done(((bf16[128,2048]{1,0:T(8,128)(2,1)}), bf16[512,2048]{1,0:T(8,128)(2,1)}) %all-gather.38.cloned.1.call-update) | async-done | bytes 2097168 | tf_op jit(solution)/shard_map/all_gather | solution.py:73
  1324.2 3.7 multiply_reduce_fusion.4
  1335.5 4.8 convolution_convert_fusion.3
  1340.8 5.1 convolution_convert_fusion.2
  1346.0 5.1 convolution_convert_fusion.4
  1357.3 3.2 convolution_convert_fusion.7
  1360.5 3.7 convolution_convert_fusion.6
  1364.3 5.2 all-reduce.7.cloned.1.call-done
  1377.1 68.7 %reduce-scatter.34.cloned.1.call-done = bf16[256,704]{0,1:T(8,128)(2,1)} async-done(((bf16[2048,704]{0,1:T(8,128)(2,1)}), bf16[256,704]{0,1:T(8,128)(2,1)}) %reduce-scatter.34.cloned.1.call-update) | async-done | bytes 360464 | tf_op jit(solution)/shard_map/reduce_scatter | solution.py:391
  1447.7 74.4 %reduce-scatter.36.cloned.1.call-done = bf16[256,704]{0,1:T(8,128)(2,1)} async-done(((bf16[2048,704]{0,1:T(8,128)(2,1)}), bf16[256,704]{0,1:T(8,128)(2,1)}) %reduce-scatter.36.cloned.1.call-update) | async-done | bytes 360464 | tf_op jit(solution)/shard_map/reduce_scatter | solution.py:394
  1524.0 74.4 %reduce-scatter.38.cloned.1.call-done = bf16[704,256]{1,0:T(8,128)(2,1)} async-done(((bf16[704,2048]{1,0:T(8,128)(2,1)}), bf16[704,256]{1,0:T(8,128)(2,1)}) %reduce-scatter.38.cloned.1.call-update) | async-done | bytes 360464 | tf_op jit(solution)/shard_map/reduce_scatter | solution.py:397
  1600.3 14.8 convolution_bitcast_fusion
  1615.1 15.4 convolution_bitcast_fusion.1
  1630.6 3.5 convolution_convert_fusion.1
  1634.5 16.0 fusion.18
  1652.9 12.6 reduce-scatter.30.cloned.1.call-done
  1667.2 31.2 %reduce-scatter.24.cloned.1.call-done = bf16[128,2048]{1,0:T(8,128)(2,1)} async-done(((bf16[512,2048]{1,0:T(8,128)(2,1)}), bf16[128,2048]{1,0:T(8,128)(2,1)}) %reduce-scatter.24.cloned.1.call-update) | async-done | bytes 524304 | tf_op jit(solution)/shard_map/reduce_scatter | solution.py:77
  1702.5 67.7 %reduce-scatter.32.cloned.1.call-done = bf16[512,256]{1,0:T(8,128)(2,1)} async-done(((bf16[512,2048]{1,0:T(8,128)(2,1)}), bf16[512,256]{1,0:T(8,128)(2,1)}) %reduce-scatter.32.cloned.1.call-update) | async-done | bytes 262160 | tf_op jit(solution)/shard_map/reduce_scatter | solution.py:388
  1772.0 40.2 %all-reduce = (f32[2048]{0:T(1024)}, f32[512]{0:T(512)}, f32[2048]{0:T(1024)}) all-reduce(f32[2048]{0:T(1024)S(1)} %get-tuple-element.20, f32[512]{0:T(512)S(1)} %fusion.67, f32[2048]{0:T(1024)S(1)} %copy-done.52), channel_id=1, replica_groups=mesh['row'=4,'col'=8] {'row','col'}, use_global_device_ids=true, to_apply=%region_31.32 | all-reduce | flops 4608 | bytes 36864 | tf_op jit(solution)/shard_map/psum | solution.py:401
  1812.2 31.1 %reduce-scatter.28.cloned.1.call-done = bf16[256,576]{0,1:T(8,128)(2,1)} async-done(((bf16[2048,576]{0,1:T(8,128)(2,1)}), bf16[256,576]{0,1:T(8,128)(2,1)}) %reduce-scatter.28.cloned.1.call-update) | async-done | bytes 294928 | tf_op jit(solution)/shard_map/reduce_scatter | solution.py:382
  1845.2 75.3 %reduce-scatter.26.cloned.1.call-done = bf16[256,768]{1,0:T(8,128)(2,1)} async-done(((bf16[2048,768]{1,0:T(8,128)(2,1)}), bf16[256,768]{1,0:T(8,128)(2,1)}) %reduce-scatter.26.cloned.1.call-update) | async-done | bytes 393232 | tf_op jit(solution)/shard_map/reduce_scatter | solution.py:379
  1922.4 131.9 %all-reduce.5.cloned.1.call-done = f32[2048,64]{0,1:T(8,128)} async-done(((f32[2048,64]{0,1:T(8,128)}), f32[2048,64]{0,1:T(8,128)}) %all-reduce.5.cloned.1.call-update) | async-done | bytes 524304 | tf_op jit(solution)/shard_map/psum | solution.py:401
  (306 shorter events, 74.9 us)
Async XLA Ops:
  7.2 372.7 %copy-start = (bf16[2048,64]{0,1:T(8,128)(2,1)S(1)}, bf16[2048,64]{0,1:T(8,128)(2,1)}, u32[]{:S(2)}) copy-start(bf16[2048,64]{0,1:T(8,128)(2,1)} %param.28) | copy-start | bytes 786436
  7.2 28.3 %all-gather.14.cloned.1.call-start = ((), (), s32[]{:S(2)}) async-start(), calls=%async_computation.17 | async-start | bytes 2621440 | tf_op jit(solution)/shard_map/all_gather | solution.py:73
  11.6 77.6 %all-gather.16.cloned.1.call-start = ((), (), s32[]{:S(2)}) async-start(), calls=%async_computation.18 | async-start | bytes 2654208 | tf_op jit(solution)/shard_map/all_gather | solution.py:144
  12.4 118.2 %all-gather.18.cloned.1.call-start = ((), (), s32[]{:S(2)}) async-start(), calls=%async_computation.19 | async-start | bytes 1179648 | tf_op jit(solution)/shard_map/all_gather | solution.py:145
  13.1 179.4 %all-gather.20.cloned.1.call-start = ((), (), s32[]{:S(2)}) async-start(), calls=%async_computation.20 | async-start | bytes 3538944 | tf_op jit(solution)/shard_map/all_gather | solution.py:143
  13.7 227.9 %all-gather.22.cloned.1.call-start = ((), (), s32[]{:S(2)}) async-start(), calls=%async_computation.21 | async-start | bytes 2359296 | tf_op jit(solution)/shard_map/all_gather | solution.py:146
  14.3 263.1 %reduce-scatter.14.cloned.1.call-start = ((), (), s32[]{:S(2)}) async-start(), calls=%async_computation.22 | async-start | bytes 2621440 | tf_op jit(solution)/shard_map/reduce_scatter | solution.py:77
  14.3 120.8 %copy-start.68 = (f32[32]{0:T(128)}, f32[32]{0:T(128)S(1)}, u32[]{:S(2)}) copy-start(f32[32]{0:T(128)S(1)} %multiply_power_fusion) | copy-start | bytes 388
  14.6 182.3 %copy-start.35 = (f32[512,32]{0,1:T(8,128)}, f32[512,32]{0,1:T(8,128)S(1)}, u32[]{:S(2)}) copy-start(f32[512,32]{0,1:T(8,128)S(1)} %get-tuple-element.52) | copy-start | bytes 196612
  14.7 182.3 %copy-start.37 = (f32[512,32]{0,1:T(8,128)}, f32[512,32]{0,1:T(8,128)S(1)}, u32[]{:S(2)}) copy-start(f32[512,32]{0,1:T(8,128)S(1)} %get-tuple-element.53) | copy-start | bytes 196612
  14.9 184.2 %copy-start.29 = (pred[512,512]{0,1:T(8,128)(4,1)}, pred[512,512]{0,1:T(8,128)(4,1)S(1)}, u32[]{:S(2)}) copy-start(pred[512,512]{0,1:T(8,128)(4,1)S(1)} %fusion.61) | copy-start | bytes 786436
  14.9 115.6 %copy-start.53 = (f32[512]{0:T(512)S(1)}, f32[512]{0:T(512)}, u32[]{:S(2)}) copy-start(f32[512]{0:T(512)} %param.24) | copy-start | bytes 6148
  92.9 42.2 %copy-start.7 = (f32[512,576]{0,1:T(8,128)}, f32[512,576]{0,1:T(8,128)S(1)}, u32[]{:S(2)}) copy-start(f32[512,576]{0,1:T(8,128)S(1)} %fusion.86) | copy-start | bytes 3538948
  94.8 35.7 %copy-start.55 = (f32[512]{0:T(512)}, f32[512]{0:T(512)S(1)}, u32[]{:S(2)}) copy-start(f32[512]{0:T(512)S(1)} %get-tuple-element.47) | copy-start | bytes 6148
  135.1 64.1 %copy-start.20 = (bf16[512,1024]{0,1:T(8,128)(2,1)}, bf16[512,1024]{0,1:T(8,128)(2,1)S(1)}, u32[]{:S(2)}) copy-start(bf16[512,1024]{0,1:T(8,128)(2,1)S(1)} %copy.138) | copy-start | bytes 3145732
  135.1 62.0 %copy-start.22 = (bf16[512,4,128]{0,2,1:T(8,128)(2,1)}, bf16[512,4,128]{0,2,1:T(8,128)(2,1)S(1)}, u32[]{:S(2)}) copy-start(bf16[512,4,128]{0,2,1:T(8,128)(2,1)S(1)} %slice.79) | copy-start | bytes 1572868
  241.6 35.8 %copy-start.2 = (bf16[1,128,2048]{2,1,0:T(8,128)(2,1)S(1)}, bf16[1,128,2048]{2,1,0:T(8,128)(2,1)}, u32[]{:S(2)}) copy-start(bf16[1,128,2048]{2,1,0:T(8,128)(2,1)} %param.18) | copy-start | bytes 1572868
  246.0 33.2 %copy-start.49 = (f32[2048]{0:T(1024)S(1)}, f32[2048]{0:T(1024)}, u32[]{:S(2)}) copy-start(f32[2048]{0:T(1024)} %param.27) | copy-start | bytes 24580
  246.0 238.3 %all-gather.32.cloned.1.call-start = ((), (), s32[]{:S(2)}) async-start(), calls=%async_computation.28 | async-start | bytes 20971520 | tf_op jit(solution)/shard_map/all_gather | solution.py:87
  246.3 133.9 %copy-start.47 = (s32[1,128,6]{1,2,0:T(8,128)}, s32[1,128,6]{1,2,0:T(8,128)S(1)}, u32[]{:S(2)}) copy-start(s32[1,128,6]{1,2,0:T(8,128)S(1)} %copy.159) | copy-start | bytes 9220
  246.7 133.6 %copy-start.57 = (s32[128,6]{0,1:T(8,128)}, s32[128,6]{0,1:T(8,128)S(1)}, u32[]{:S(2)}) copy-start(s32[128,6]{0,1:T(8,128)S(1)} %multiply_add_fusion.1) | copy-start | bytes 9220
  280.4 99.4 %copy-start.9 = (bf16[128,2048]{1,0:T(8,128)(2,1)}, bf16[128,2048]{1,0:T(8,128)(2,1)S(1)}, u32[]{:S(2)}) copy-start(bf16[128,2048]{1,0:T(8,128)(2,1)S(1)} %multiply_convert_fusion.6) | copy-start | bytes 1572868
  379.8 212.0 %all-gather.36.cloned.1.call-start = ((), (), s32[]{:S(2)}) async-start(), calls=%async_computation.32 | async-start | bytes 20971520 | tf_op jit(solution)/shard_map/all_gather | solution.py:87
  481.2 291.9 %reduce-scatter.18.cloned.1.call-start = ((), (), s32[]{:S(2)}) async-start(), calls=%async_computation.29 | async-start | bytes 20971520 | tf_op jit(solution)/shard_map/reduce_scatter | solution.py:91
  615.4 62.9 %copy-start.5 = (bf16[32,8,16,352]{3,2,0,1:T(8,128)(2,1)}, bf16[32,8,16,352]{3,2,0,1:T(8,128)(2,1)S(1)}, u32[]{:S(2)}) copy-start(bf16[32,8,16,352]{3,2,0,1:T(8,128)(2,1)S(1)} %get-tuple-element.29) | copy-start | bytes 8650756
  647.9 247.1 %all-gather.26.cloned.1.call-start = ((), (), s32[]{:S(2)}) async-start(), calls=%async_computation.24 | async-start | bytes 3244032 | tf_op jit(solution)/shard_map/all_gather | solution.py:147
  648.5 271.2 %all-gather.24.cloned.1.call-start = ((), (), s32[]{:S(2)}) async-start(), calls=%async_computation.23 | async-start | bytes 2621440 | tf_op jit(solution)/shard_map/all_gather | solution.py:73
  649.2 330.1 %all-gather.28.cloned.1.call-start = ((), (), s32[]{:S(2)}) async-start(), calls=%async_computation.25 | async-start | bytes 3244032 | tf_op jit(solution)/shard_map/all_gather | solution.py:148
  649.8 354.2 %all-gather.34.cloned.1.call-start = ((), (), s32[]{:S(2)}) async-start(), calls=%async_computation.30 | async-start | bytes 2621440 | tf_op jit(solution)/shard_map/all_gather | solution.py:73
  652.0 411.7 %all-gather.30.cloned.1.call-start = ((), (), s32[]{:S(2)}) async-start(), calls=%async_computation.26 | async-start | bytes 3244032 | tf_op jit(solution)/shard_map/all_gather | solution.py:149
  652.5 539.2 %reduce-scatter.22.cloned.1.call-start = ((), (), s32[]{:S(2)}) async-start(), calls=%async_computation.33 | async-start | bytes 20971520 | tf_op jit(solution)/shard_map/reduce_scatter | solution.py:91
  773.1 418.7 %all-to-all-start.1 = ((bf16[64,16,2048]{2,1,0:T(8,128)(2,1)}), bf16[64,16,2048]{2,1,0:T(8,128)(2,1)}, u32[]{:S(2)}, u32[]{:S(2)}) async-start(bf16[64,16,2048]{2,1,0:T(8,128)(2,1)} %reduce-scatter.18.cloned.1.call-done), calls=%async_computation.4 | async-start | bytes 8388608 | tf_op jit(solution)/shard_map/all_to_all | solution.py:94
  919.6 59.7 %copy-start.82 = (bf16[512,2048]{1,0:T(8,128)(2,1)S(1)}, bf16[512,2048]{1,0:T(8,128)(2,1)}, u32[]{:S(2)}) copy-start(bf16[512,2048]{1,0:T(8,128)(2,1)} %all-gather.24.cloned.1.call-done) | copy-start | bytes 6291460
  983.9 87.2 %copy-start.19 = (bf16[2048,704]{0,1:T(8,128)(2,1)S(1)}, bf16[2048,704]{0,1:T(8,128)(2,1)}, u32[]{:S(2)}) copy-start(bf16[2048,704]{0,1:T(8,128)(2,1)} %all-gather.26.cloned.1.call-done) | copy-start | bytes 8650756
  1075.0 122.9 %copy-start.79 = (bf16[2048,704]{0,1:T(8,128)(2,1)S(1)}, bf16[2048,704]{0,1:T(8,128)(2,1)}, u32[]{:S(2)}) copy-start(bf16[2048,704]{0,1:T(8,128)(2,1)} %all-gather.28.cloned.1.call-done) | copy-start | bytes 8650756
  1191.8 96.6 %all-to-all-start.3 = ((bf16[64,16,2048]{2,1,0:T(8,128)(2,1)}), bf16[64,16,2048]{2,1,0:T(8,128)(2,1)}, u32[]{:S(2)}, u32[]{:S(2)}) async-start(bf16[64,16,2048]{2,1,0:T(8,128)(2,1)} %reduce-scatter.22.cloned.1.call-done), calls=%async_computation.8 | async-start | bytes 8388608 | tf_op jit(solution)/shard_map/all_to_all | solution.py:94
  1197.8 97.6 %reduce-scatter.20.cloned.1.call-start = ((), (), s32[]{:S(2)}) async-start(), calls=%async_computation.31 | async-start | bytes 2621440 | tf_op jit(solution)/shard_map/reduce_scatter | solution.py:77
  1203.5 94.7 %reduce-scatter.16.cloned.1.call-start = ((), (), s32[]{:S(2)}) async-start(), calls=%async_computation.27 | async-start | bytes 2621440 | tf_op jit(solution)/shard_map/reduce_scatter | solution.py:77
  1208.8 115.3 %all-gather.38.cloned.1.call-start = ((), (), s32[]{:S(2)}) async-start(), calls=%async_computation.34 | async-start | bytes 2621440 | tf_op jit(solution)/shard_map/all_gather | solution.py:73
  1216.8 78.6 %copy-start.43 = (bf16[128,64]{0,1:T(8,128)(2,1)}, bf16[128,64]{0,1:T(8,128)(2,1)S(1)}, u32[]{:S(2)}) copy-start(bf16[128,64]{0,1:T(8,128)(2,1)S(1)} %select_reduce_fusion) | copy-start | bytes 49156
  1301.3 26.6 %copy-start.30 = (pred[512,512]{0,1:T(8,128)(4,1)S(1)}, pred[512,512]{0,1:T(8,128)(4,1)}, u32[]{:S(2)}) copy-start(pred[512,512]{0,1:T(8,128)(4,1)} %copy-done.29) | copy-start | bytes 786436
  1301.3 26.6 %copy-start.66 = (f32[4,512]{1,0:T(4,128)S(1)}, f32[4,512]{1,0:T(4,128)}, u32[]{:S(2)}) copy-start(f32[4,512]{1,0:T(4,128)} %copy-done.65) | copy-start | bytes 24580
  1301.3 68.1 %all-reduce.7.cloned.1.call-start = ((), (), s32[]{:S(2)}) async-start(), calls=%async_computation.44 | async-start | bytes 1179648 | tf_op jit(solution)/shard_map/psum | solution.py:347
  1335.4 110.4 %reduce-scatter.34.cloned.1.call-start = ((), (), s32[]{:S(2)}) async-start(), calls=%async_computation.41 | async-start | bytes 3244032 | tf_op jit(solution)/shard_map/reduce_scatter | solution.py:391
  1340.3 181.8 %reduce-scatter.36.cloned.1.call-start = ((), (), s32[]{:S(2)}) async-start(), calls=%async_computation.42 | async-start | bytes 3244032 | tf_op jit(solution)/shard_map/reduce_scatter | solution.py:394
  1345.9 252.5 %reduce-scatter.38.cloned.1.call-start = ((), (), s32[]{:S(2)}) async-start(), calls=%async_computation.43 | async-start | bytes 3244032 | tf_op jit(solution)/shard_map/reduce_scatter | solution.py:397
  1351.1 314.4 %reduce-scatter.30.cloned.1.call-start = ((), (), s32[]{:S(2)}) async-start(), calls=%async_computation.38 | async-start | bytes 1179648 | tf_op jit(solution)/shard_map/reduce_scatter | solution.py:385
  1354.3 344.1 %reduce-scatter.24.cloned.1.call-start = ((), (), s32[]{:S(2)}) async-start(), calls=%async_computation.35 | async-start | bytes 2621440 | tf_op jit(solution)/shard_map/reduce_scatter | solution.py:77
  1360.5 409.7 %reduce-scatter.32.cloned.1.call-start = ((), (), s32[]{:S(2)}) async-start(), calls=%async_computation.39 | async-start | bytes 2359296 | tf_op jit(solution)/shard_map/reduce_scatter | solution.py:388
  1364.2 479.2 %reduce-scatter.28.cloned.1.call-start = ((), (), s32[]{:S(2)}) async-start(), calls=%async_computation.37 | async-start | bytes 2654208 | tf_op jit(solution)/shard_map/reduce_scatter | solution.py:382
  1376.8 223.6 %copy-start.6 = (bf16[32,8,16,352]{3,2,0,1:T(8,128)(2,1)S(1)}, bf16[32,8,16,352]{3,2,0,1:T(8,128)(2,1)}, u32[]{:S(2)}) copy-start(bf16[32,8,16,352]{3,2,0,1:T(8,128)(2,1)} %copy-done.5) | copy-start | bytes 8650756
  1376.8 543.6 %reduce-scatter.26.cloned.1.call-start = ((), (), s32[]{:S(2)}) async-start(), calls=%async_computation.36 | async-start | bytes 3538944 | tf_op jit(solution)/shard_map/reduce_scatter | solution.py:379
  1634.2 16.3 copy-start.10
  1634.2 16.3 copy-start.44
  1634.2 17.3 copy-start.26
  1634.2 17.4 copy-start.12
  1634.2 420.1 %all-reduce.5.cloned.1.call-start = ((), (), s32[]{:S(2)}) async-start(), calls=%async_computation.40 | async-start | bytes 1048576 | tf_op jit(solution)/shard_map/psum | solution.py:401
  1650.4 47.9 %copy-start.4 = (bf16[1,128,2048]{2,1,0:T(8,128)(2,1)S(1)}, bf16[1,128,2048]{2,1,0:T(8,128)(2,1)}, u32[]{:S(2)}) copy-start(bf16[1,128,2048]{2,1,0:T(8,128)(2,1)} %param.18) | copy-start | bytes 1572868
  1650.4 47.9 %copy-start.51 = (f32[2048]{0:T(1024)S(1)}, f32[2048]{0:T(1024)}, u32[]{:S(2)}) copy-start(f32[2048]{0:T(1024)} %param.21) | copy-start | bytes 24580
  1650.5 47.9 %copy-start.73 = (f32[128]{0:T(128)S(1)}, f32[128]{0:T(128)}, u32[]{:S(2)}) copy-start(f32[128]{0:T(128)} %copy-done.72) | copy-start | bytes 1540
  1651.7 49.3 %copy-start.15 = (f32[128,2048]{1,0:T(8,128)S(1)}, f32[128,2048]{1,0:T(8,128)}, u32[]{:S(2)}) copy-start(f32[128,2048]{1,0:T(8,128)} %get-tuple-element.28) | copy-start | bytes 3145732
  1651.7 49.3 %copy-start.76 = (f32[128]{0:T(128)S(1)}, f32[128]{0:T(128)}, u32[]{:S(2)}) copy-start(f32[128]{0:T(128)} %get-tuple-element.48) | copy-start | bytes 1540
  1701.0 71.0 %copy-start.52 = (f32[2048]{0:T(1024)S(1)}, f32[2048]{0:T(1024)}, u32[]{:S(2)}) copy-start(f32[2048]{0:T(1024)} %get-tuple-element.18) | copy-start | bytes 24580
  1701.0 355.2 %copy-start.1 = (bf16[2048,64]{0,1:T(8,128)(2,1)S(1)}, bf16[2048,64]{0,1:T(8,128)(2,1)}, u32[]{:S(2)}) copy-start(bf16[2048,64]{0,1:T(8,128)(2,1)} %param.28) | copy-start | bytes 786436
  (51 other events, 226.1 us)
Sparse Core Ops, SparseCore 0:
  11.7 23.7 all-gather.13
  37.5 51.6 all-gather.15
  91.3 39.1 all-gather.17
  132.6 59.8 all-gather.19
  194.4 47.1 all-gather.21
  246.1 31.1 reduce-scatter.13
  379.9 104.3 all-gather.31
  485.9 105.8 all-gather.35
  648.0 125.0 reduce-scatter.17
  775.0 119.9 all-gather.25
  897.1 22.4 all-gather.23
  921.5 57.7 all-gather.27
  981.4 22.5 all-gather.33
  1005.9 57.7 all-gather.29
  1066.7 125.0 reduce-scatter.21
  1203.6 31.1 reduce-scatter.19
  1237.7 31.1 reduce-scatter.15
  1301.4 22.7 all-gather.37
  1335.5 33.8 all-reduce.6
  1373.4 72.3 reduce-scatter.33
  1450.0 72.1 reduce-scatter.35
  1526.3 72.1 reduce-scatter.37
  1601.8 63.6 reduce-scatter.29
  1667.9 30.3 reduce-scatter.23
  1701.9 68.2 reduce-scatter.31
  1773.6 69.7 reduce-scatter.27
  1846.8 73.6 reduce-scatter.25
  1925.7 128.5 all-reduce.4
where the time goes:
time: 2070 us; the launch traced here: 2060 us
  waiting for transfers between devices  1430 us (69%)
  matrix products  289 us (14%)
  blocking collectives  235 us (11%)
  local copies, waits for them, and re-layouts  38.5 us (2%)
  other arithmetic  36.8 us (2%)
    all_to_all x2, blocking collectives, to_experts(): lax.all_to_all(buffer, 'col', split_axis=0, concat_axis=0, tiled=True)  194 us
    reduce_scatter x2, waiting for transfers between devices, from_experts(): lax.psum_scatter(partial_value.astype(jnp.bfloat16), 'row', scatter_dimen...  174 us
    psum x1, waiting for transfers between devices, on_device(): lax.psum((first_gain_part, latent_gain_part, second_gain_part, router_par...  132 us
    all_gather x1, waiting for transfers between devices, on_device(): lax.all_gather(shared_gate, 'col', axis=0, tiled=True)  116 us
    all_gather x4, waiting for transfers between devices, token_rows(): return lax.all_gather(values, 'row', axis=0, tiled=True)  88.2 us
    all_gather x2, waiting for transfers between devices, to_experts(): return lax.all_gather(arrived, 'row', axis=0, tiled=True)  76.8 us
    reduce_scatter x1, waiting for transfers between devices, on_device(): lax.psum_scatter(query_part.astype(jnp.bfloat16), 'col', scatter_dimensio...  75.3 us
    reduce_scatter x1, waiting for transfers between devices, on_device(): lax.psum_scatter(shared_up_part.astype(jnp.bfloat16), 'col', scatter_dime...  74.4 us
  transfers between devices with their start and end apart: 30, of which 27 were waited for; matrix products, arithmetic and copies ran while one was open for 13% of the time, Pallas kernels for 0%

commit v1 on v0

v1 whole, which is shorter than its diff:
```python
import functools

import jax
import jax.numpy as jnp
from jax import lax
from jax.experimental import pallas as pl
from jax.experimental.pallas import tpu as pltpu
from jax.sharding import PartitionSpec as P

NOPE = 128
ROPE = 64
LATENT = 512
VD = 128
TOPK = 6


EPS = 1e-06
ROWS_CONTRACT = (((0,), (0,)), ((), ()))
COLS_CONTRACT = (((1,), (1,)), ((), ()))


def matmul(left_side, right_side):
    return jnp.dot(left_side, right_side, preferred_element_type=jnp.float32)


def inner_rows(left_side, right_side):
    return lax.dot_general(left_side, right_side, ROWS_CONTRACT, preferred_element_type=jnp.float32)


def outer_cols(left_side, right_side):
    return lax.dot_general(left_side, right_side, COLS_CONTRACT, preferred_element_type=jnp.float32)


def rms_scale(values):
    return lax.rsqrt(jnp.mean(values * values, axis=-1, keepdims=True) + EPS)


def rms_back(values, scaling, gradient):
    return scaling * gradient - values * scaling**3 * jnp.mean(
        gradient * values, axis=-1, keepdims=True
    )


def silu_parts(preact):
    logistic = jax.nn.sigmoid(preact)
    return (preact * logistic, logistic * (1.0 + preact * (1.0 - logistic)))


def angle_tables(length):
    halfway = ROPE // 2
    frequency = 10000.0 ** (-2.0 * jnp.arange(halfway, dtype=jnp.float32) / ROPE)
    angles = jnp.arange(length, dtype=jnp.float32)[:, None] * frequency[None, :]
    return (jnp.cos(angles), jnp.sin(angles))


def rotate(values, cosine_in, sine_in):
    halfway = values.shape[-1] // 2
    leading = values[..., :halfway]
    trailing = values[..., halfway:]
    return jnp.concatenate(
        [leading * cosine_in - trailing * sine_in, leading * sine_in + trailing * cosine_in],
        axis=-1,
    )


def unrotate(values, cosine_in, sine_in):
    halfway = values.shape[-1] // 2
    leading = values[..., :halfway]
    trailing = values[..., halfway:]
    return jnp.concatenate(
        [leading * cosine_in + trailing * sine_in, trailing * cosine_in - leading * sine_in],
        axis=-1,
    )


F32 = jnp.float32
BF16 = jnp.bfloat16
EVERY = ("col", "row")
VMEM_LIMIT = 63 * 1024 * 1024


def token_rows(values):
    return lax.all_gather(values, "row", axis=0, tiled=True)


def every_token(values):
    return lax.all_gather(values, EVERY, axis=0, tiled=True)


def row_total(partial_value):
    return lax.psum_scatter(
        partial_value.astype(BF16), "row", scatter_dimension=0, tiled=True
    ).astype(F32)


def every_total(partial_value):
    return lax.psum_scatter(partial_value, EVERY, scatter_dimension=0, tiled=True).astype(F32)


def col_gather(values):
    return lax.all_gather(values, "col", axis=0, tiled=True)


def col_total(partial_value, dim):
    return lax.psum_scatter(
        partial_value.astype(BF16), "col", scatter_dimension=dim, tiled=True
    ).astype(F32)


MESH_ID = pl.DeviceIdType.MESH


def places():
    row, col = lax.axis_index("row"), lax.axis_index("col")
    return row // 2, lax.rem(row, 2), col // 2, lax.rem(col, 2)


def to_place(wide, core, line, side):
    return {"row": wide * 2 + core, "col": line * 2 + side}


def greet(partners, everyone):
    barrier = pltpu.get_barrier_semaphore()
    if everyone:
        n_row, n_col = lax.axis_size("row"), lax.axis_size("col")
        total = n_row * n_col
        me = lax.axis_index("col") * n_row + lax.axis_index("row")

        @pl.loop(1, total)
        def _(step):
            other = lax.rem(me + step, total)
            pl.semaphore_signal(
                barrier,
                inc=1,
                device_id={"row": lax.rem(other, n_row), "col": other // n_row},
                device_id_type=MESH_ID,
            )

        pl.semaphore_wait(barrier, total - 1)
        return
    for there, partner in partners:

        @pl.when(there)
        def _(partner=partner):
            pl.semaphore_signal(barrier, inc=1, device_id=partner, device_id_type=MESH_ID)

    for there, partner in partners:

        @pl.when(there)
        def _():
            pl.semaphore_wait(barrier, 1)


def remote(src, dst, send_sem, recv_sem, partner):
    return pltpu.make_async_remote_copy(
        src_ref=src,
        dst_ref=dst,
        send_sem=send_sem,
        recv_sem=recv_sem,
        device_id=partner,
        device_id_type=MESH_ID,
    )


def small_exchange(small_ref, small_out, send_sem, recv_sem, personal):
    n_row = lax.axis_size("row")
    total = n_row * lax.axis_size("col")
    me = lax.axis_index("col") * n_row + lax.axis_index("row")

    def copy(other, slot):
        return remote(
            small_ref.at[other] if personal else small_ref,
            small_out.at[slot],
            send_sem.at[other],
            recv_sem.at[slot],
            {"row": lax.rem(other, n_row), "col": other // n_row},
        )

    def start():
        @pl.loop(1, total)
        def _(step):
            copy(lax.rem(me + step, total), me).start()

        small_out[me] = small_ref[me] if personal else small_ref[...]

    def finish():
        @pl.loop(1, total)
        def _(step):
            other = lax.rem(me + step, total)
            copy(other, other).wait_recv()
            copy(other, me).wait_send()

    return start, finish


def line_order(lines):
    order = []
    for step in range((lines + 1) // 2):
        order.append(step)
        if lines - 1 - step != step:
            order.append(lines - 1 - step)
    return order


def scatter_body(lines, count, small, *refs):
    bigs, refs = refs[:count], refs[count:]
    if small:
        small_ref, refs = refs[0], refs[1:]
    outs, refs = refs[:count], refs[count:]
    if small:
        small_out, refs = refs[0], refs[1:]
    own, core_in, wide_in, side_in, up_in, down_in = refs[:6]
    load_sem, core_send, core_recv, wide_send, wide_recv, side_send, side_recv = refs[6:13]
    up_send, up_recv, down_send, down_recv = refs[13:17]
    wide, core, line, side = places()
    tokens = own.shape[1]
    half = tokens // 2
    core_mate = to_place(wide, 1 - core, line, side)
    wide_mate = to_place(1 - wide, core, line, side)
    side_mate = to_place(wide, core, line, 1 - side)
    above = to_place(wide, core, line + 1, side)
    below = to_place(wide, core, line - 1, side)
    has_above = line < lines - 1
    has_below = line > 0
    greet(
        [
            (core >= 0, core_mate),
            (core >= 0, wide_mate),
            (core >= 0, side_mate),
            (has_above, above),
            (has_below, below),
        ],
        small,
    )
    parts = [pl.ds(0, half), pl.ds(half, half)]

    def at(a, l, s, w):
        return ((a * lines + l) * 2 + s) * 2 + w

    def core_copy(a, i):
        n = a * 4 * lines + i
        return remote(
            bigs[a].at[pl.ds((2 * i + 1 - core) * tokens, tokens)],
            core_in.at[n],
            core_send.at[n],
            core_recv.at[n],
            core_mate,
        )

    def load(a, i):
        n = a * 4 * lines + i
        return pltpu.make_async_copy(
            bigs[a].at[pl.ds((2 * i + core) * tokens, tokens)], own.at[n], load_sem.at[n]
        )

    def wide_one(a, l, s):
        n = (a * lines + l) * 3 + s
        return remote(
            own.at[at(a, l, s, 1 - wide), parts[0]],
            wide_in.at[n],
            wide_send.at[n],
            wide_recv.at[n],
            wide_mate,
        )

    def side_one(a, l, w):
        n = (a * lines + l) * 3 + w
        return remote(
            own.at[at(a, l, 1 - side, w), parts[1]],
            side_in.at[n],
            side_send.at[n],
            side_recv.at[n],
            side_mate,
        )

    def side_two(a, l):
        n = (a * lines + l) * 3 + 2
        return remote(
            own.at[at(a, l, 1 - side, wide), parts[0]],
            side_in.at[n],
            side_send.at[n],
            side_recv.at[n],
            side_mate,
        )

    def wide_two(a, l):
        n = (a * lines + l) * 3 + 2
        return remote(
            own.at[at(a, l, side, 1 - wide), parts[1]],
            wide_in.at[n],
            wide_send.at[n],
            wide_recv.at[n],
            wide_mate,
        )

    def up_copy(a, l, h):
        n = (a * lines + l) * 2 + h
        return remote(
            own.at[at(a, l, side, wide), parts[h]],
            up_in.at[n],
            up_send.at[n],
            up_recv.at[n],
            above,
        )

    def down_copy(a, l, h):
        n = (a * lines + l) * 2 + h
        return remote(
            own.at[at(a, l, side, wide), parts[h]],
            down_in.at[n],
            down_send.at[n],
            down_recv.at[n],
            below,
        )

    def add(i, rows, other):
        own[i, rows] = (own[i, rows].astype(F32) + other[...].astype(F32)).astype(BF16)

    items = [(a, l) for a in range(count) for l in line_order(lines)]
    for a, l in items:
        for j in range(4):
            core_copy(a, l * 4 + j).start()
            load(a, l * 4 + j).start()
    if small:
        small_start, small_finish = small_exchange(small_ref, small_out, *refs[17:19], True)
        small_start()

    def stage_one(a, l):
        for j in range(4):
            i = l * 4 + j
            load(a, i).wait()
            core_copy(a, i).wait_recv()
            add(a * 4 * lines + i, pl.ds(0, tokens), core_in.at[a * 4 * lines + i])
        for j in range(2):
            wide_one(a, l, j).start()
            side_one(a, l, j).start()

    def stage_two(a, l):
        n = (a * lines + l) * 3
        for j in range(2):
            s = 1 - side if j == 0 else side
            wide_one(a, l, s).wait_recv()
            add(at(a, l, s, wide), parts[0], wide_in.at[n + s])
            if j == 0:
                side_two(a, l).start()
            w = 1 - wide if j == 0 else wide
            side_one(a, l, w).wait_recv()
            add(at(a, l, side, w), parts[1], side_in.at[n + w])
            if j == 0:
                wide_two(a, l).start()

    def stage_three(a, l):
        n = (a * lines + l) * 3 + 2
        i = at(a, l, side, wide)
        for h in range(2):
            if h == 0:
                side_two(a, l).wait_recv()
                add(i, parts[0], side_in.at[n])
            else:
                wide_two(a, l).wait_recv()
                add(i, parts[1], wide_in.at[n])

            @pl.when(jnp.logical_and(line == 0, l > 0))
            def _(h=h):
                up_copy(a, l, h).start()

            @pl.when(jnp.logical_and(line == lines - 1, l < lines - 1))
            def _(h=h):
                down_copy(a, l, h).start()

    def stage_four(a, l):
        i = at(a, l, side, wide)
        for h in range(2):

            @pl.when(jnp.logical_and(has_below, line <= l))
            def _(h=h):
                up_copy(a, l, h).wait_recv()
                add(i, parts[h], up_in.at[(a * lines + l) * 2 + h])

            @pl.when(jnp.logical_and(has_above, line >= l))
            def _(h=h):
                down_copy(a, l, h).wait_recv()
                add(i, parts[h], down_in.at[(a * lines + l) * 2 + h])

            @pl.when(jnp.logical_and(jnp.logical_and(has_below, has_above), line < l))
            def _(h=h):
                up_copy(a, l, h).start()

            @pl.when(jnp.logical_and(jnp.logical_and(has_below, has_above), line > l))
            def _(h=h):
                down_copy(a, l, h).start()

    for step in range(len(items) + 3):
        if step < len(items):
            stage_one(*items[step])
        if 0 <= step - 1 < len(items):
            stage_two(*items[step - 1])
        if 0 <= step - 2 < len(items):
            stage_three(*items[step - 2])
        if 0 <= step - 3 < len(items):
            stage_four(*items[step - 3])
    for a in range(count):
        outs[a][...] = own[at(a, line, side, wide)].astype(F32)
    if small:
        small_finish()
    for a, l in items:
        for j in range(4):
            core_copy(a, l * 4 + j).wait_send()
        for j in range(2):
            wide_one(a, l, j).wait_send()
            side_one(a, l, j).wait_send()
        side_two(a, l).wait_send()
        wide_two(a, l).wait_send()
        for h in range(2):

            @pl.when(jnp.logical_and(has_above, line < l))
            def _(h=h):
                up_copy(a, l, h).wait_send()

            @pl.when(jnp.logical_and(has_below, line > l))
            def _(h=h):
                down_copy(a, l, h).wait_send()


def kernel_total(partials, small_value, number):
    n_row, n_col = lax.axis_size("row"), lax.axis_size("col")
    lines, count = n_col // 2, len(partials)
    width = partials[0].shape[1]
    tokens = partials[0].shape[0] // (n_row * n_col)
    small = small_value is not None
    out_shape = [jax.ShapeDtypeStruct((tokens, width), F32)] * count
    in_specs = [pl.BlockSpec(memory_space=pl.ANY)] * count
    operands = list(partials)
    if small:
        in_specs.append(pl.BlockSpec(memory_space=pltpu.VMEM))
        out_shape.append(jax.ShapeDtypeStruct(small_value.shape, small_value.dtype))
        operands.append(small_value)
    dma = pltpu.SemaphoreType.DMA
    scratch = [
        pltpu.VMEM((count * 4 * lines, tokens, width), BF16),
        pltpu.VMEM((count * 4 * lines, tokens, width), BF16),
        pltpu.VMEM((count * 3 * lines, tokens // 2, width), BF16),
        pltpu.VMEM((count * 3 * lines, tokens // 2, width), BF16),
        pltpu.VMEM((count * 2 * lines, tokens // 2, width), BF16),
        pltpu.VMEM((count * 2 * lines, tokens // 2, width), BF16),
        *[dma((count * 4 * lines,))] * 3,
        *[dma((count * 3 * lines,))] * 4,
        *[dma((count * 2 * lines,))] * 4,
    ]
    if small:
        scratch += [dma((n_row * n_col,))] * 2
    return pl.pallas_call(
        functools.partial(scatter_body, lines, count, small),
        out_shape=out_shape,
        in_specs=in_specs,
        out_specs=[pl.BlockSpec(memory_space=pltpu.VMEM)] * len(out_shape),
        scratch_shapes=scratch,
        compiler_params=pltpu.CompilerParams(
            collective_id=number, has_side_effects=True, vmem_limit_bytes=VMEM_LIMIT
        ),
        name=f"scatter_{number}",
    )(*operands)


def gather_body(lines, small, *refs):
    own_ref, refs = refs[0], refs[1:]
    if small:
        small_ref, refs = refs[0], refs[1:]
    out_ref, refs = refs[0], refs[1:]
    if small:
        small_out, refs = refs[0], refs[1:]
    local_sem, core_send, core_recv, wide_send, wide_recv, side_send, side_recv = refs[:7]
    up_send, up_recv, down_send, down_recv = refs[7:11]
    wide, core, line, side = places()
    tokens = own_ref.shape[0]
    half = tokens // 2
    core_mate = to_place(wide, 1 - core, line, side)
    wide_mate = to_place(1 - wide, core, line, side)
    side_mate = to_place(wide, core, line, 1 - side)
    above = to_place(wide, core, line + 1, side)
    below = to_place(wide, core, line - 1, side)
    has_above = line < lines - 1
    has_below = line > 0
    greet(
        [
            (core >= 0, core_mate),
            (core >= 0, wide_mate),
            (core >= 0, side_mate),
            (has_above, above),
            (has_below, below),
        ],
        small,
    )

    def spot(l, s, w, k, h):
        return out_ref.at[pl.ds((((l * 2 + s) * 2 + w) * 2 + k) * tokens + h * half, half)]

    def source(l, s, w, h, here):
        return own_ref.at[pl.ds(h * half, half)] if here else spot(l, s, w, core, h)

    def core_copy(l, s, w, h, here=False):
        n = ((l * 2 + s) * 2 + w) * 2 + h
        return remote(
            source(l, s, w, h, here),
            spot(l, s, w, core, h),
            core_send.at[n],
            core_recv.at[n],
            core_mate,
        )

    def wide_copy(l, s, h, here=False):
        n = l * 3 + (2 if h else s)
        return remote(
            source(l, s, wide, h, here),
            spot(l, s, wide, core, h),
            wide_send.at[n],
            wide_recv.at[n],
            wide_mate,
        )

    def side_copy(l, w, h, here=False):
        n = l * 3 + (w if h else 2)
        return remote(
            source(l, side, w, h, here),
            spot(l, side, w, core, h),
            side_send.at[n],
            side_recv.at[n],
            side_mate,
        )

    def up_copy(l, h, here=False):
        n = l * 2 + h
        return remote(
            source(l, side, wide, h, here),
            spot(l, side, wide, core, h),
            up_send.at[n],
            up_recv.at[n],
            above,
        )

    def down_copy(l, h, here=False):
        n = l * 2 + h
        return remote(
            source(l, side, wide, h, here),
            spot(l, side, wide, core, h),
            down_send.at[n],
            down_recv.at[n],
            below,
        )

    def local(h):
        return pltpu.make_async_copy(
            own_ref.at[pl.ds(h * half, half)], spot(line, side, wide, core, h), local_sem.at[h]
        )

    def spread(l, h, here=False):
        if h == 0:
            side_copy(l, wide, 0, here).start()
            wide_copy(l, side, 0, here).start()
        else:
            wide_copy(l, side, 1, here).start()
            side_copy(l, wide, 1, here).start()
        core_copy(l, side, wide, h, here).start()

    def second(l):
        side_copy(l, wide, 0).wait_recv()
        wide_copy(l, 1 - side, 0).start()
        core_copy(l, 1 - side, wide, 0).start()
        wide_copy(l, side, 1).wait_recv()
        side_copy(l, 1 - wide, 1).start()
        core_copy(l, side, 1 - wide, 1).start()

    def third(l):
        for j in range(2):
            s = 1 - side if j else side
            wide_copy(l, s, 0).wait_recv()
            core_copy(l, s, 1 - wide, 0).start()
            w = 1 - wide if j else wide
            side_copy(l, w, 1).wait_recv()
            core_copy(l, 1 - side, w, 1).start()

    for h in range(2):

        @pl.when(has_above)
        def _(h=h):
            up_copy(line, h, True).start()

        @pl.when(has_below)
        def _(h=h):
            down_copy(line, h, True).start()

        spread(line, h, True)
    if small:
        small_start, small_finish = small_exchange(small_ref, small_out, *refs[11:13], False)
        small_start()
    for h in range(2):
        local(h).start()

    def from_line(dist, up):
        l = line - dist if up else line + dist
        there = l >= 0 if up else l < lines
        further = has_above if up else has_below
        copy = up_copy if up else down_copy

        @pl.when(there)
        def _():
            for h in range(2):
                copy(l, h).wait_recv()

                @pl.when(further)
                def _(h=h):
                    copy(l, h).start()

                spread(l, h)

    def stage(action, dist):
        if dist == 0:
            action(line)
            return

        @pl.when(line - dist >= 0)
        def _():
            action(line - dist)

        @pl.when(line + dist < lines)
        def _():
            action(line + dist)

    for dist in range(1, lines + 2):
        if dist < lines:
            from_line(dist, True)
            from_line(dist, False)
        if dist - 1 < lines:
            stage(second, dist - 1)
        if 0 <= dist - 2 < lines:
            stage(third, dist - 2)
    if small:
        small_finish()
    for h in range(2):
        local(h).wait()
    for l in range(lines):
        for s in range(2):
            for w in range(2):
                for h in range(2):
                    core_copy(l, s, w, h).wait_recv()
                    core_copy(l, s, w, h).wait_send()
        for j in range(2):
            wide_copy(l, j, 0).wait_send()
            side_copy(l, j, 1).wait_send()
        wide_copy(l, side, 1).wait_send()
        side_copy(l, wide, 0).wait_send()
        for h in range(2):

            @pl.when(jnp.logical_and(has_above, line >= l))
            def _(h=h):
                up_copy(l, h).wait_send()

            @pl.when(jnp.logical_and(has_below, line <= l))
            def _(h=h):
                down_copy(l, h).wait_send()


def kernel_gather(own, small_value, number):
    n_row, n_col = lax.axis_size("row"), lax.axis_size("col")
    lines, total = n_col // 2, n_row * n_col
    tokens, width = own.shape
    small = small_value is not None
    out_shape = [jax.ShapeDtypeStruct((total * tokens, width), own.dtype)]
    in_specs = [pl.BlockSpec(memory_space=pltpu.VMEM)]
    out_specs = [pl.BlockSpec(memory_space=pl.ANY)]
    operands = [own]
    if small:
        in_specs.append(pl.BlockSpec(memory_space=pltpu.VMEM))
        out_specs.append(pl.BlockSpec(memory_space=pltpu.VMEM))
        out_shape.append(jax.ShapeDtypeStruct((total, *small_value.shape), small_value.dtype))
        operands.append(small_value)
    dma = pltpu.SemaphoreType.DMA
    scratch = [
        dma((2,)),
        *[dma((8 * lines,))] * 2,
        *[dma((3 * lines,))] * 4,
        *[dma((2 * lines,))] * 4,
    ]
    if small:
        scratch += [dma((total,))] * 2
    return pl.pallas_call(
        functools.partial(gather_body, lines, small),
        out_shape=out_shape,
        in_specs=in_specs,
        out_specs=out_specs,
        scratch_shapes=scratch,
        compiler_params=pltpu.CompilerParams(collective_id=number, has_side_effects=True),
        name=f"gather_{number}",
    )(*operands)


def kernel_fits(rows, width, count):
    n_row, n_col = lax.axis_size("row"), lax.axis_size("col")
    tokens = rows // (n_row * n_col)
    held = count * n_col * 2 * width * tokens * 13 // 4
    return n_row == 4 and n_col % 2 == 0 and tokens % 32 == 0 and held < 58 * 1024 * 1024


def small_body(personal, value_ref, out_ref, send_sem, recv_sem):
    greet([], True)
    start, finish = small_exchange(value_ref, out_ref, send_sem, recv_sem, personal)
    start()
    finish()


def kernel_small(value, personal, number):
    total = lax.axis_size("row") * lax.axis_size("col")
    shape = value.shape if personal else (total, *value.shape)
    dma = pltpu.SemaphoreType.DMA
    return pl.pallas_call(
        functools.partial(small_body, personal),
        out_shape=jax.ShapeDtypeStruct(shape, value.dtype),
        in_specs=[pl.BlockSpec(memory_space=pltpu.VMEM)],
        out_specs=pl.BlockSpec(memory_space=pltpu.VMEM),
        scratch_shapes=[dma((total,)), dma((total,))],
        compiler_params=pltpu.CompilerParams(collective_id=number, has_side_effects=True),
        name=f"small_{number}",
    )(value)


def gather_every(own, small_value, number):
    total = lax.axis_size("row") * lax.axis_size("col")
    if kernel_fits(total * own.shape[0], own.shape[1], 1):
        return kernel_gather(own, small_value, number)
    return every_token(own), every_token(small_value[None])


def total_every(partials, small_value, number):
    if kernel_fits(partials[0].shape[0], partials[0].shape[1], len(partials)):
        return kernel_total(partials, small_value, number)
    exchanged = lax.all_to_all(small_value, EVERY, split_axis=0, concat_axis=0, tiled=True)
    return *[every_total(p) for p in partials], exchanged


def padded_rows(values):
    return jnp.pad(values, ((0, -values.shape[0] % 8), (0, 0)))


def masked_scores(queries, attn_keys, allowed, softmax_scale):
    scores = (
        jnp.einsum("qhd,khd->hqk", queries, attn_keys, preferred_element_type=jnp.float32)
        * softmax_scale
    )
    return jnp.where(allowed[None], scores, -1e30)


def select_body(group, capacity, place_ref, rows_ref, slots_ref):
    tokens = place_ref.shape[2]
    for block in range(group):
        picked = matmul(place_ref[block], rows_ref[block * tokens : (block + 1) * tokens, :])
        slots_ref[:, block] = picked.astype(BF16).reshape(-1, capacity, picked.shape[-1])


def select_rows(place, rows, capacity):
    blocks, slots, tokens = place.shape
    width = rows.shape[1]
    local_experts = slots // capacity
    group = 4 if blocks % 4 == 0 else 1
    out = pl.pallas_call(
        functools.partial(select_body, group, capacity),
        grid=(blocks // group,),
        in_specs=[
            pl.BlockSpec((group, slots, tokens), lambda i: (i, 0, 0)),
            pl.BlockSpec((group * tokens, width), lambda i: (i, 0)),
        ],
        out_specs=pl.BlockSpec((local_experts, group, capacity, width), lambda i: (0, i, 0, 0)),
        out_shape=jax.ShapeDtypeStruct((local_experts, blocks, capacity, width), BF16),
        compiler_params=pltpu.CompilerParams(vmem_limit_bytes=VMEM_LIMIT),
        cost_estimate=pl.CostEstimate(
            flops=2 * blocks * slots * tokens * width,
            bytes_accessed=4 * blocks * tokens * width,
            transcendentals=0,
        ),
        name="select_rows",
    )(place, rows)
    return out.reshape(local_experts, blocks * capacity, width)


def experts_body(
    x_ref, g_ref, gate_ref, wg_ref, wu_ref, wd_ref, y_ref, r_ref, dg_ref, du_ref, dd_ref, gg_ref
):
    first = pl.program_id(1) == 0
    x = x_ref[0]
    g = g_ref[0]
    gate = gate_ref[0]
    pre = outer_cols(x, wg_ref[0])
    lin = outer_cols(x, wu_ref[0])
    back = outer_cols(g, wd_ref[0])
    act, slope = silu_parts(pre)
    hidden = act * lin
    gg_ref[0] = jnp.sum(hidden * back, axis=-1, keepdims=True)
    hidden = (hidden * gate).astype(BF16)
    back = back * gate
    pre_grad = (back * lin * slope).astype(BF16)
    lin_grad = (back * act).astype(BF16)
    width = x_ref.shape[2]
    chunk = 512 if width % 512 == 0 else width
    for start in range(0, width, chunk):
        cols = slice(start, start + chunk)
        y_ref[0, :, cols] = matmul(hidden, wd_ref[0, :, cols]).astype(BF16)
        r_ref[0, :, cols] = (
            matmul(pre_grad, wg_ref[0, :, cols]) + matmul(lin_grad, wu_ref[0, :, cols])
        ).astype(BF16)
        d_gate = inner_rows(pre_grad, x_ref[0, :, cols])
        d_up = inner_rows(lin_grad, x_ref[0, :, cols])
        d_down = inner_rows(hidden, g_ref[0, :, cols])

        @pl.when(first)
        def _():
            dg_ref[0, :, cols] = d_gate
            du_ref[0, :, cols] = d_up
            dd_ref[0, :, cols] = d_down

        @pl.when(jnp.logical_not(first))
        def _():
            dg_ref[0, :, cols] += d_gate
            du_ref[0, :, cols] += d_up
            dd_ref[0, :, cols] += d_down


def run_experts(x_slots, g_slots, gates, w_gate, w_up, w_down):
    count, rows, width = x_slots.shape
    hidden = w_down.shape[1]
    chunk = 512 if rows % 512 == 0 else rows
    row_block = pl.BlockSpec((1, chunk, width), lambda e, r: (e, r, 0))
    col_block = pl.BlockSpec((1, chunk, 1), lambda e, r: (e, r, 0))
    out_block = pl.BlockSpec((1, hidden, width), lambda e, r: (e, 0, 0))
    y, r, d_gate, d_up, d_down, dots = pl.pallas_call(
        experts_body,
        grid=(count, rows // chunk),
        in_specs=[row_block, row_block, col_block, out_block, out_block, out_block],
        out_specs=[row_block, row_block, out_block, out_block, out_block, col_block],
        out_shape=[
            jax.ShapeDtypeStruct((count, rows, width), BF16),
            jax.ShapeDtypeStruct((count, rows, width), BF16),
            jax.ShapeDtypeStruct((count, hidden, width), F32),
            jax.ShapeDtypeStruct((count, hidden, width), F32),
            jax.ShapeDtypeStruct((count, hidden, width), F32),
            jax.ShapeDtypeStruct((count, rows, 1), F32),
        ],
        compiler_params=pltpu.CompilerParams(vmem_limit_bytes=VMEM_LIMIT),
        cost_estimate=pl.CostEstimate(
            flops=18 * count * rows * width * hidden,
            bytes_accessed=count * (8 * rows * width + 18 * width * hidden),
            transcendentals=count * rows * hidden,
        ),
        name="run_experts",
    )(x_slots, g_slots, gates, w_gate.transpose(0, 2, 1), w_up.transpose(0, 2, 1), w_down)
    return y, r, d_gate.transpose(0, 2, 1), d_up.transpose(0, 2, 1), d_down, dots


def combine_body(group, place_ref, slots_ref, extra_ref, weight_ref, out_ref):
    tokens = place_ref.shape[2]
    width = out_ref.shape[1]
    for block in range(group):
        rows = slice(block * tokens, (block + 1) * tokens)
        total = inner_rows(place_ref[block], slots_ref[:, block].reshape(-1, width))
        total += matmul(extra_ref[rows, :], weight_ref[...])
        out_ref[rows, :] = total.astype(BF16)


def combine_rows(place, slots, extra, weight, capacity):
    blocks, slot_count, tokens = place.shape
    local_experts, _, width = slots.shape
    group = 4 if blocks % 4 == 0 else 1
    inner = extra.shape[1]
    return pl.pallas_call(
        functools.partial(combine_body, group),
        grid=(blocks // group,),
        in_specs=[
            pl.BlockSpec((group, slot_count, tokens), lambda i: (i, 0, 0)),
            pl.BlockSpec((local_experts, group, capacity, width), lambda i: (0, i, 0, 0)),
            pl.BlockSpec((group * tokens, inner), lambda i: (i, 0)),
            pl.BlockSpec((inner, width), lambda i: (0, 0)),
        ],
        out_specs=pl.BlockSpec((group * tokens, width), lambda i: (i, 0)),
        out_shape=jax.ShapeDtypeStruct((blocks * tokens, width), BF16),
        compiler_params=pltpu.CompilerParams(vmem_limit_bytes=VMEM_LIMIT),
        cost_estimate=pl.CostEstimate(
            flops=2 * blocks * tokens * (slot_count + inner) * width,
            bytes_accessed=4 * blocks * tokens * width,
            transcendentals=0,
        ),
        name="combine_rows",
    )(place, slots.reshape(local_experts, blocks, capacity, width), extra, weight)


def on_device(
    inputs,
    segment_ids,
    routes,
    first_gain,
    query_weight,
    latent_down,
    latent_gain,
    latent_up,
    output_weight,
    second_gain,
    router_weight,
    shared_gate,
    shared_up,
    shared_down,
    expert_gate,
    expert_up,
    expert_down,
    cotangent,
):
    n_row = lax.axis_size("row")
    n_col = lax.axis_size("col")
    blocks = n_row * n_col
    own_row = lax.axis_index("row")
    own_col = lax.axis_index("col")
    own_rows = inputs.shape[1]
    width = inputs.shape[2]
    experts = router_weight.shape[1]
    local_experts = expert_gate.shape[0]
    capacity = max(2, own_rows // 8)
    stream = inputs.reshape(own_rows, width).astype(F32)
    grad_out = cotangent.reshape(own_rows, width)
    own_routes = routes.reshape(own_rows, TOPK)
    segments = segment_ids.reshape(-1)
    length = segments.shape[0]
    own_start = own_row * own_rows
    qk_dim = NOPE + ROPE
    softmax_scale = qk_dim ** (-0.5)
    cosine_table, sine_table = angle_tables(length)

    scale_one = rms_scale(stream)
    normed_one = (stream * scale_one * first_gain).astype(BF16)
    seq_normed = token_rows(normed_one)
    down_cols = latent_down.shape[1] // n_row
    own_down = lax.dynamic_slice_in_dim(latent_down, own_row * down_cols, down_cols, 1)
    query_cols = query_weight.shape[1]
    query_down = col_gather(jnp.concatenate([query_weight, own_down], axis=1))
    query_all = query_down[:, :query_cols]
    down_all = query_down[:, query_cols:]
    expand_all = col_gather(latent_up)
    output_all = lax.all_gather(output_weight, "col", axis=1, tiled=True)

    all_routes = kernel_small(padded_rows(own_routes.astype(F32).T), False, 1)
    all_routes = all_routes[:, :TOPK].astype(jnp.int32)
    grad_all = every_token(grad_out.astype(BF16))
    local_ids = own_col * local_experts + jnp.arange(local_experts)
    named = all_routes[:, :, None, :] == local_ids[None, None, :, None]
    chosen_here = jnp.max(named.astype(BF16), axis=1)
    before = (jnp.arange(own_rows)[:, None] < jnp.arange(own_rows)[None, :]).astype(BF16)
    rank = matmul(chosen_here.reshape(-1, own_rows), before).reshape(chosen_here.shape)
    slot_of = jnp.where(chosen_here > 0, rank.astype(jnp.int32), -1)
    placed = slot_of[:, :, None, :] == jnp.arange(capacity)[None, None, :, None]
    place = placed.astype(BF16).reshape(blocks, local_experts * capacity, own_rows)
    grad_slots = select_rows(place, grad_all, capacity)

    shared_cols = shared_gate.shape[1] // n_col
    shared_send = jnp.stack([shared_gate.T, shared_up.T, shared_down], axis=0)
    depth = shared_send.shape[2]
    shared_send = (
        shared_send.reshape(3, n_col, shared_cols, depth)
        .transpose(1, 0, 2, 3)
        .reshape(n_col, 3 * shared_cols, depth)
    )
    shared_own = (
        lax.all_to_all(shared_send, "col", split_axis=0, concat_axis=0, tiled=True)
        .transpose(1, 0, 2)
        .reshape(3, shared_cols, width)
    )
    gate_up_own = shared_own[:2].reshape(2 * shared_cols, width)
    down_own = shared_own[2]

    heads_local = query_cols // qk_dim
    query_raw = matmul(seq_normed, query_all).reshape(length, heads_local, qk_dim)
    queries = jnp.concatenate(
        [
            query_raw[..., :NOPE],
            rotate(query_raw[..., NOPE:], cosine_table[:, None, :], sine_table[:, None, :]),
        ],
        axis=-1,
    ).astype(BF16)
    latent_all = lax.all_gather(matmul(seq_normed, down_all), "row", axis=1, tiled=True)
    latent = latent_all[:, :LATENT]
    scale_latent = rms_scale(latent)
    latent_normed = (latent * scale_latent * latent_gain).astype(BF16)
    keyval = matmul(latent_normed, expand_all).reshape(length, heads_local, NOPE + VD)
    key_rope = rotate(latent_all[:, LATENT:], cosine_table, sine_table)
    attn_keys = jnp.concatenate(
        [keyval[..., :NOPE], jnp.broadcast_to(key_rope[:, None, :], (length, heads_local, ROPE))],
        axis=-1,
    ).astype(BF16)
    values = keyval[..., NOPE:].astype(BF16)
    positions = jnp.arange(length)
    allowed = (positions[:, None] >= positions[None, :]) & (segments[:, None] == segments[None, :])
    scores = masked_scores(queries, attn_keys, allowed, softmax_scale)
    highest = jnp.max(scores, axis=-1, keepdims=True)
    log_total = highest + jnp.log(jnp.sum(jnp.exp(scores - highest), axis=-1, keepdims=True))
    attn_probs = jnp.exp(scores - log_total).astype(BF16)
    heads_out = (
        jnp.einsum("hqk,khd->qhd", attn_probs, values, preferred_element_type=jnp.float32)
        .astype(BF16)
        .reshape(length, heads_local * VD)
    )
    residual = stream + row_total(matmul(heads_out, output_all))

    scale_two = rms_scale(residual)
    normed_two = (residual * scale_two * second_gain).astype(BF16)
    logits = matmul(normed_two, router_weight)
    expert_ids = jnp.arange(experts)
    chosen = own_routes[:, :, None] == expert_ids[None, None, :]
    picked = jnp.sum(jnp.where(chosen, logits[:, None, :], 0.0), axis=-1)
    gate_probs = jax.nn.softmax(picked, axis=-1)

    all_normed, all_gates = gather_every(normed_two, padded_rows(gate_probs.T), 2)
    all_gates = all_gates[:, :TOPK]
    gate_here = jnp.sum(jnp.where(named, all_gates[:, :, None, :], 0.0), axis=1)
    slot_gate = jnp.sum(jnp.where(placed, gate_here[:, :, None, :], 0.0), axis=-1)
    slot_gate = slot_gate.transpose(1, 0, 2).reshape(local_experts, blocks * capacity, 1)
    normed_slots = select_rows(place, all_normed, capacity)
    out_slots, rows_slots, expert_gate_grad, expert_up_grad, expert_down_grad, slot_dot = (
        run_experts(normed_slots, grad_slots, slot_gate, expert_gate, expert_up, expert_down)
    )

    shared_both = outer_cols(all_normed, gate_up_own)
    shared_act, shared_slope = silu_parts(shared_both[:, :shared_cols])
    shared_lin = shared_both[:, shared_cols:]
    shared_hidden = (shared_act * shared_lin).astype(BF16)
    shared_hidden_grad = outer_cols(grad_all, down_own)
    shared_both_grad = jnp.concatenate(
        [
            (shared_hidden_grad * shared_lin * shared_slope).astype(BF16),
            (shared_hidden_grad * shared_act).astype(BF16),
        ],
        axis=1,
    )
    slot_dot = slot_dot.reshape(local_experts, blocks, capacity).transpose(1, 0, 2)
    token_dot = jnp.sum(jnp.where(placed, slot_dot[:, :, :, None], 0.0), axis=2)
    out_total, rows_total, token_dot = total_every(
        [
            combine_rows(place, out_slots, shared_hidden, down_own, capacity),
            combine_rows(place, rows_slots, shared_both_grad, gate_up_own, capacity),
        ],
        token_dot,
        3,
    )
    layer_out = (residual + out_total).astype(BF16).reshape(1, own_rows, width)
    gate_up_part = inner_rows(shared_both_grad, all_normed)
    down_part = inner_rows(shared_hidden, grad_all)
    shared_back = jnp.concatenate([gate_up_part, down_part], axis=0).astype(BF16)
    shared_back = (
        shared_back.reshape(3 * shared_cols, n_col, depth).transpose(1, 0, 2)
    )
    shared_back = lax.all_to_all(shared_back, "col", split_axis=0, concat_axis=0, tiled=True)
    shared_back = (
        shared_back.reshape(n_col, 3, shared_cols, depth)
        .transpose(1, 0, 2, 3)
        .reshape(3, n_col * shared_cols, depth)
        .astype(F32)
    )
    shared_gate_grad = shared_back[0].T
    shared_up_grad = shared_back[1].T
    shared_down_grad = shared_back[2]

    token_dot = jnp.sum(token_dot.reshape(n_col, n_row, local_experts, own_rows), axis=1)
    token_dot = token_dot.reshape(experts, own_rows).T
    gate_grad = jnp.sum(jnp.where(chosen, token_dot[:, None, :], 0.0), axis=-1)
    picked_grad = gate_probs * (gate_grad - jnp.sum(gate_probs * gate_grad, axis=-1, keepdims=True))
    logit_grad = jnp.sum(jnp.where(chosen, picked_grad[:, :, None], 0.0), axis=1).astype(BF16)
    all_logit_grad = kernel_small(logit_grad, False, 4).reshape(-1, experts)
    router_grad = inner_rows(all_normed, all_logit_grad)

    normed_two_grad = rows_total + outer_cols(logit_grad, router_weight)
    second_gain_part = jnp.sum(normed_two_grad * residual * scale_two, axis=0)
    residual_grad = grad_out + rms_back(residual, scale_two, normed_two_grad * second_gain)

    seq_resid = token_rows(residual_grad.astype(BF16))
    output_part = inner_rows(heads_out, seq_resid)
    heads_grad = outer_cols(seq_resid, output_all).astype(BF16).reshape(length, heads_local, VD)
    recomputed = jnp.exp(masked_scores(queries, attn_keys, allowed, softmax_scale) - log_total)
    delta_rows = jnp.sum(
        heads_grad.astype(F32) * heads_out.reshape(length, heads_local, VD).astype(F32),
        axis=-1,
    )
    prob_grad = jnp.einsum("qhd,khd->hqk", heads_grad, values, preferred_element_type=jnp.float32)
    score_grad = (recomputed * (prob_grad - delta_rows.T[:, :, None]) * softmax_scale).astype(BF16)
    queries_grad = jnp.einsum(
        "hqk,khd->qhd", score_grad, attn_keys, preferred_element_type=jnp.float32
    )
    key_grad = jnp.einsum("hqk,qhd->khd", score_grad, queries, preferred_element_type=jnp.float32)
    value_grad = jnp.einsum(
        "hqk,qhd->khd",
        recomputed.astype(BF16),
        heads_grad,
        preferred_element_type=jnp.float32,
    )
    query_full = (
        jnp.concatenate(
            [
                queries_grad[..., :NOPE],
                unrotate(
                    queries_grad[..., NOPE:], cosine_table[:, None, :], sine_table[:, None, :]
                ),
            ],
            axis=-1,
        )
        .astype(BF16)
        .reshape(length, heads_local * qk_dim)
    )
    keyval_grad = (
        jnp.concatenate([key_grad[..., :NOPE], value_grad], axis=-1)
        .astype(BF16)
        .reshape(length, heads_local * (NOPE + VD))
    )
    expand_part = inner_rows(latent_normed, keyval_grad)
    latent_normed_part = outer_cols(keyval_grad, expand_all)
    rope_part = jnp.sum(key_grad[..., NOPE:], axis=1)
    latent_normed_grad, rope_raw = (
        lax.psum(latent_normed_part.astype(BF16), "row").astype(F32),
        lax.psum(rope_part.astype(BF16), "row").astype(F32),
    )
    rope_grad = unrotate(rope_raw, cosine_table, sine_table)
    latent_gain_part = jnp.sum(
        lax.dynamic_slice_in_dim(
            latent_normed_grad * latent * scale_latent, own_start, own_rows, 0
        ),
        axis=0,
    )
    latent_grad = rms_back(latent, scale_latent, latent_normed_grad * latent_gain)
    down_grad_in = jnp.concatenate([latent_grad, rope_grad], axis=-1).astype(BF16)
    own_down_grad = lax.dynamic_slice_in_dim(down_grad_in, own_row * down_cols, down_cols, 1)
    both_grad = jnp.concatenate([query_full, own_down_grad], axis=1)
    normed_one_grad = row_total(outer_cols(both_grad, query_down))
    first_gain_part = jnp.sum(normed_one_grad * stream * scale_one, axis=0)
    input_grad = (
        residual_grad + rms_back(stream, scale_one, normed_one_grad * first_gain)
    ).reshape(1, own_rows, width)

    output_grad = col_total(output_part, 1)
    latent_up_grad = col_total(expand_part, 0)
    both_total = col_total(inner_rows(seq_normed, both_grad), 0)
    query_grad = both_total[:, :query_cols]
    latent_down_grad = lax.all_gather(
        both_total[:, query_cols:].astype(BF16), "row", axis=1, tiled=True
    ).astype(F32)
    gains = jnp.concatenate([first_gain_part, latent_gain_part, second_gain_part])
    gains = padded_rows(gains.reshape(-1, LATENT // 4))
    gains = jnp.sum(kernel_small(gains, False, 5), axis=0).reshape(-1)
    first_gain_grad = gains[:width]
    latent_gain_grad = gains[width : width + LATENT]
    second_gain_grad = gains[width + LATENT : 2 * width + LATENT]
    return (
        layer_out,
        input_grad,
        first_gain_grad,
        query_grad,
        latent_down_grad,
        latent_gain_grad,
        latent_up_grad,
        output_grad,
        second_gain_grad,
        router_grad,
        shared_gate_grad,
        shared_up_grad,
        shared_down_grad,
        expert_gate_grad,
        expert_up_grad,
        expert_down_grad,
    )


def solution(mesh):
    return jax.shard_map(
        on_device,
        mesh=mesh,
        in_specs=(
            P("col", "row", None),
            P("col", None),
            P("col", "row", None),
            P(),
            P("col", "row"),
            P("col", None),
            P(),
            P("col", "row"),
            P("row", "col"),
            P(),
            P(),
            P("col", "row"),
            P("col", "row"),
            P("row", "col"),
            P("col", None, "row"),
            P("col", None, "row"),
            P("col", "row", None),
            P("col", "row", None),
        ),
        out_specs=(
            P("col", "row", None),
            P("col", "row", None),
            P(),
            P("col", "row"),
            P("col", None),
            P(),
            P("col", "row"),
            P("row", "col"),
            P(),
            P(),
            P("col", "row"),
            P("col", "row"),
            P("row", "col"),
            P("col", None, "row"),
            P("col", None, "row"),
            P("col", "row", None),
        ),
        check_vma=False,
    )
```

time: 2070 us -> 1150 us (0.56)
  waiting for transfers between devices: 1430 us -> 374 us
  Pallas kernels: 0 us -> 563 us
  blocking collectives: 235 us -> 5.88 us
  matrix products: 289 us -> 101 us
    pallas_call x0 -> x10, Pallas kernels: none -> 563 us  [the longest x1 180 us: kernel_total(): pl.pallas_call(functools.partial(scatter_body, lines, count, small), out_...]
    reduce_scatter x13 -> x5, waiting for transfers between devices: 640 us -> 141 us  [the longest x3 109 us: col_total(): lax.psum_scatter(partial_value.astype(BF16), 'col', scatter_dimension=dim...]
    all_gather x9 -> x5, waiting for transfers between devices: 492 us -> 162 us  [the longest x2 113 us: col_gather(): return lax.all_gather(values, 'col', axis=0, tiled=True)]
    all_to_all x2 -> x0, blocking collectives: 194 us -> none  [to_experts(): lax.all_to_all(buffer, 'col', split_axis=0, concat_axis=0, tiled=True)]
    dot_general x10 -> x1, matrix products: 172 us -> 1.37 us  [on_device(): jnp.einsum('hqk,qhd->khd', recomputed.astype(BF16), heads_grad, preferred...]
    psum x2 -> x1, waiting for transfers between devices: 137 us -> 24.2 us  [on_device(): lax.psum(latent_normed_part.astype(BF16), 'row').astype(F32)]
    all_to_all x2, waiting for transfers between devices: 71.6 us -> 0.01 us  [the longest x1 0.01 us: on_device(): lax.all_to_all(shared_send, 'col', split_axis=0, concat_axis=0, tiled=True)]
    all_gather x4 -> x2, waiting for transfers between devices: 88.2 us -> 46.1 us  [token_rows(): return lax.all_gather(values, 'row', axis=0, tiled=True)]
  transfers between devices with their start and end apart: 30 -> 15, of which waited for: 27 -> 10; matrix products, arithmetic and copies ran while one was open for 13% -> 10% of each run, Pallas kernels for 0% -> 22%
where the time goes in v1:
time: 1150 us; the launch traced here: 1140 us
  Pallas kernels  563 us (49%)
  waiting for transfers between devices  374 us (33%)
  matrix products  101 us (9%)
  other arithmetic  44 us (4%)
  local copies, waits for them, and re-layouts  19.6 us (2%)
  between operations  17.2 us (1%)
  starting transfers between devices  13 us (1%)
    pallas_call x1, Pallas kernels, kernel_total(): pl.pallas_call(functools.partial(scatter_body, lines, count, small), out_...  180 us
    pallas_call x3, Pallas kernels, kernel_small(): pl.pallas_call(functools.partial(small_body, personal), out_shape=jax.Sha...  120 us
    all_gather x2, waiting for transfers between devices, col_gather(): return lax.all_gather(values, 'col', axis=0, tiled=True)  113 us
    pallas_call x1, Pallas kernels, kernel_gather(): pl.pallas_call(functools.partial(gather_body, lines, small), out_shape=ou...  113 us
    reduce_scatter x3, waiting for transfers between devices, col_total(): lax.psum_scatter(partial_value.astype(BF16), 'col', scatter_dimension=dim...  109 us
    pallas_call x1, Pallas kernels, run_experts(): pl.pallas_call(experts_body, grid=(count, rows // chunk), in_specs=[row_b...  81 us
    all_gather x2, waiting for transfers between devices, token_rows(): return lax.all_gather(values, 'row', axis=0, tiled=True)  46.1 us
    all_gather x1, waiting for transfers between devices, on_device(): output_all = lax.all_gather(output_weight, 'col', axis=1, tiled=True)  39.8 us
  transfers between devices with their start and end apart: 15, of which 10 were waited for; matrix products, arithmetic and copies ran while one was open for 10% of the time, Pallas kernels for 22%

profile of v1, /device:TPU:8, one launch (start us, length us, event | category | flops | bytes accessed | tf_op | source)
XLA Modules:
  0.0 1138.8 jit_solution(7662184012414852258)
XLA Ops:
  8.1 1.3 fusion.12
  9.9 2.0 fusion.14
  13.1 22.7 %all-gather.8.cloned.1.call-done = bf16[512,2048]{1,0:T(8,128)(2,1)} async-done(((bf16[128,2048]{1,0:T(8,128)(2,1)}), bf16[512,2048]{1,0:T(8,128)(2,1)}) %all-gather.8.cloned.1.call-update) | async-done | bytes 2097168 | tf_op jit(solution)/shard_map/all_gather | solution.py:83
  35.9 75.2 %all-gather.10.cloned.1.call-done = bf16[2048,912]{1,0:T(8,128)(2,1)} async-done(((bf16[256,912]{1,0:T(8,128)(2,1)}), bf16[2048,912]{1,0:T(8,128)(2,1)}) %all-gather.10.cloned.1.call-update) | async-done | bytes 3735568 | tf_op jit(solution)/shard_map/all_gather | solution.py:101
  111.1 3.4 fusion.19
  116.3 3.8 fusion.1
  121.8 9.2 all-gather.12.cloned.1.call-done
  130.9 2.4 fusion.50
  134.0 38.1 %all-gather.14.cloned.1.call-done = bf16[512,1024]{1,0:T(8,128)(2,1)} async-done(((bf16[64,1024]{1,0:T(8,128)(2,1)}), bf16[512,1024]{1,0:T(8,128)(2,1)}) %all-gather.14.cloned.1.call-update) | async-done | bytes 1048592 | tf_op jit(solution)/shard_map/all_gather | solution.py:101
  172.1 3.0 convolution_convert_fusion.7
  175.1 1.5 copy.150
  177.1 2.3 fusion.3
  181.4 1.4 convolution_convert_fusion.10
  182.8 39.8 %all-gather.16.cloned.1.call-done = bf16[512,2048]{1,0:T(8,128)(2,1)} async-done(((bf16[512,256]{1,0:T(8,128)(2,1)}), bf16[512,2048]{1,0:T(8,128)(2,1)}) %all-gather.16.cloned.1.call-update) | async-done | bytes 2097168 | tf_op jit(solution)/shard_map/all_gather | solution.py:943
  222.6 4.2 convolution_convert_fusion.3
  230.1 5.9 all-to-all-start
  236.8 40.5 %small_1.1 = f32[32,8,128]{2,1,0:T(8,128)} custom-call(f32[8,128]{1,0:T(8,128)} %pad.11.value_ref), custom_call_target="tpu_custom_call" | custom-call | tf_op jit(solution)/shard_map/small_1/pallas_call | solution.py:715
  278.6 1.3 fusion.5.place_ref
  281.8 1.3 multiply_reduce_fusion.4
  283.1 1.3 multiply_convert_fusion.4.refs_0_
  285.4 113.2 %gather_2.1 = (bf16[4096,2048]{1,0:T(8,128)(2,1)}, f32[32,8,128]{2,1,0:T(8,128)}) custom-call(bf16[128,2048]{1,0:T(8,128)(2,1)} %copy-done.9, f32[8,128]{1,0:T(8,128)} %pad.12.refs_1_), custom_call_target="tpu_custom_call" | custom-call | tf_op jit(solution)/shard_map/gather_2/pallas_call | solution.py:686
  400.4 2.4 reshape.378.gate_ref
  402.8 16.1 %select_rows.2 = bf16[8,32,16,2048]{3,2,1,0:T(8,128)(2,1)} custom-call(bf16[32,128,128]{2,1,0:T(8,128)(2,1)} %fusion.5.place_ref, bf16[4096,2048]{1,0:T(8,128)(2,1)} %get-tuple-element.27.rows_ref), custom_call_target="tpu_custom_call" | custom-call | flops 2147483648 | bytes 33554432 | tf_op jit(solution)/shard_map/select_rows/pallas_call | solution.py:764
  418.9 12.4 %fusion.52 = f32[4096,176]{1,0:T(8,128)} fusion(bf16[4096,2048]{1,0:T(8,128)(2,1)} %get-tuple-element.27.rows_ref, bf16[176,2048]{1,0:T(8,128)(2,1)} %bitcast.170), kind=kOutput, calls=%fused_computation.162 | convolution fusion | flops 2952790016 | bytes 20381696 | tf_op jit(solution)/shard_map/dot_general | solution.py:31
  431.3 16.1 %select_rows.3 = bf16[8,32,16,2048]{3,2,1,0:T(8,128)(2,1)} custom-call(bf16[32,128,128]{2,1,0:T(8,128)(2,1)} %fusion.5.place_ref, bf16[4096,2048]{1,0:T(8,128)(2,1)} %all-gather.18.cloned.1.call-done.rows_ref), custom_call_target="tpu_custom_call" | custom-call | flops 2147483648 | bytes 33554432 | tf_op jit(solution)/shard_map/select_rows/pallas_call | solution.py:764
  447.3 81.0 %run_experts.1 = (bf16[8,512,2048]{2,1,0:T(8,128)(2,1)}, bf16[8,512,2048]{2,1,0:T(8,128)(2,1)}, f32[8,352,2048]{2,1,0:T(8,128)}, f32[8,352,2048]{2,1,0:T(8,128)}...) custom-call(bf16[8,512,2048]{2,1,0:T(8,128)(2,1)} %bitcast.160, bf16[8,512,2048]{2,1,0:T(8,128)(2,1)} %bitcast.161, ...), custom_call_target="tpu_custom_call" | custom-call | flops 53150220288 | bytes 170917888 | tf_op jit(solution)/shard_map/run_experts/pallas_call | solution.py:833
  528.4 2.2 reduce
  530.8 1.6 select_reduce_fusion.refs_2_
  532.4 13.8 %multiply_convert_fusion.2 = (bf16[4096,88]{1,0:T(8,128)(2,1)S(1)}, bf16[4096,88]{1,0:T(8,128)(2,1)S(1)}, bf16[4096,88]{1,0:T(8,128)(2,1)}) fusion(f32[4096,176]{1,0:T(8,128)} %fusion.52, bf16[88,2048]{1,0:T(8,128)(2,1)S(1)} %bitcast.176, bf16[4096,2048]{1,0:T(8,128)(2,1)} %all-gather.18.cloned.1.call-done.rows_ref), kind=kOutput, calls=%fused_computation.27 | convolution fusion | flops 1481801728 | bytes 22183936 | tf_op jit(solution)/shard_map/dot_general | solution.py:31
  546.2 2.3 pad_maximum_fusion.extra_ref
  548.4 18.0 %combine_rows.2.refs_0_ = bf16[4096,2048]{1,0:T(8,128)(2,1)} custom-call(bf16[32,128,128]{2,1,0:T(8,128)(2,1)} %fusion.5.place_ref, bf16[8,32,16,2048]{3,2,1,0:T(8,128)(2,1)} %bitcast.158, bf16[4096,88]{1,0:T(8,128)(2,1)} %get-tuple-element.112.extra_ref, bf16[88,2048]{1,0:T(8,128)(2,1)} %bitcast.175), custom_call_target="tpu_custom_call" | custom-call | flops 3623878656 | bytes 33554432 | tf_op jit(solution)/shard_map/combine_rows/pallas_call | solution.py:872
  566.5 18.6 %combine_rows.3.refs_1_ = bf16[4096,2048]{1,0:T(8,128)(2,1)} custom-call(bf16[32,128,128]{2,1,0:T(8,128)(2,1)} %fusion.5.place_ref, bf16[8,32,16,2048]{3,2,1,0:T(8,128)(2,1)} %bitcast.159, bf16[4096,176]{1,0:T(8,128)(2,1)} %pad_maximum_fusion.extra_ref, bf16[176,2048]{1,0:T(8,128)(2,1)} %bitcast.171), custom_call_target="tpu_custom_call" | custom-call | flops 5100273664 | bytes 33554432 | tf_op jit(solution)/shard_map/combine_rows/pallas_call | solution.py:872
  585.1 180.3 %scatter_3.1 = (f32[128,2048]{1,0:T(8,128)}, f32[128,2048]{1,0:T(8,128)}, f32[32,8,128]{2,1,0:T(8,128)}) custom-call(bf16[4096,2048]{1,0:T(8,128)(2,1)} %combine_rows.2.refs_0_, bf16[4096,2048]{1,0:T(8,128)(2,1)} %combine_rows.3.refs_1_, f32[32,8,128]{2,1,0:T(8,128)} %select_reduce_fusion.refs_2_), custom_call_target="tpu_custom_call" | custom-call | tf_op jit(solution)/shard_map/scatter_3/pallas_call | solution.py:452
  766.8 1.9 multiply_reduce_fusion
  768.8 1.8 fusion.48
  770.8 23.4 %all-gather.20.cloned.1.call-done = bf16[512,2048]{1,0:T(8,128)(2,1)} async-done(((bf16[128,2048]{1,0:T(8,128)(2,1)}), bf16[512,2048]{1,0:T(8,128)(2,1)}) %all-gather.20.cloned.1.call-update) | async-done | bytes 2097168 | tf_op jit(solution)/shard_map/all_gather | solution.py:83
  794.2 3.7 multiply_reduce_fusion.2
  798.0 1.4 fusion.7
  799.4 1.8 multiply_convert_fusion
  803.8 1.5 convolution_convert_fusion.11
  805.4 1.7 convolution_convert_fusion.6
  807.2 4.3 convolution_convert_fusion.2
  812.6 2.2 convolution_bitcast_fusion.2
  815.1 24.2 %all-reduce.6.cloned.1.call-done = (bf16[512,512]{0,1:T(8,128)(2,1)}, bf16[512,64]{0,1:T(8,128)(2,1)}) async-done(((bf16[512,512]{0,1:T(8,128)(2,1)}, bf16[512,64]{0,1:T(8,128)(2,1)}), (bf16[512,512]{0,1:T(8,128)(2,1)}, bf16[512,64]{0,1:T(8,128)(2,1)})) %all-reduce.6.cloned.1.call-update) | async-done | bytes 589840 | tf_op jit(solution)/shard_map/psum | solution.py:1119
  840.2 1.4 multiply_reduce_fusion.1
  842.6 3.8 convolution_convert_fusion.1
  846.7 5.6 convolution_convert_fusion
  852.4 1.2 copy-done.7
  853.6 8.8 convolution_convert_fusion.5
  862.5 9.1 convolution_convert_fusion.4
  872.7 6.0 all-to-all-start.1
  878.8 50.1 %small_4.1 = bf16[32,128,64]{2,1,0:T(8,128)(2,1)} custom-call(bf16[128,64]{1,0:T(8,128)(2,1)} %copy-done.45), custom_call_target="tpu_custom_call" | custom-call | tf_op jit(solution)/shard_map/small_4/pallas_call | solution.py:715
  929.0 10.1 fusion.53
  939.2 1.4 fusion.49
  940.7 1.2 fusion.29
  942.0 1.6 convert_element_type.187
  943.6 49.0 %reduce-scatter.14.cloned.1.call-done = bf16[512,256]{1,0:T(8,128)(2,1)} async-done(((bf16[512,2048]{1,0:T(8,128)(2,1)}), bf16[512,256]{1,0:T(8,128)(2,1)}) %reduce-scatter.14.cloned.1.call-update) | async-done | bytes 262160 | tf_op jit(solution)/shard_map/reduce_scatter | solution.py:105
  992.6 1.8 convert_element_type.189
  994.4 31.5 %reduce-scatter.8.cloned.1.call-done = bf16[128,2048]{1,0:T(8,128)(2,1)} async-done(((bf16[512,2048]{1,0:T(8,128)(2,1)}), bf16[128,2048]{1,0:T(8,128)(2,1)}) %reduce-scatter.8.cloned.1.call-update) | async-done | bytes 524304 | tf_op jit(solution)/shard_map/reduce_scatter | solution.py:91
  1025.9 1.4 fusion.18
  1027.9 29.3 %small_5.1 = f32[32,40,128]{2,1,0:T(8,128)} custom-call(f32[40,128]{1,0:T(8,128)} %pad.13.value_ref), custom_call_target="tpu_custom_call" | custom-call | tf_op jit(solution)/shard_map/small_5/pallas_call | solution.py:715
  1059.6 1.4 fusion.11
  1061.0 60.0 %reduce-scatter.10.cloned.1.call-done = bf16[256,912]{0,1:T(8,128)(2,1)} async-done(((bf16[2048,912]{0,1:T(8,128)(2,1)}), bf16[256,912]{0,1:T(8,128)(2,1)}) %reduce-scatter.10.cloned.1.call-update) | async-done | bytes 466960 | tf_op jit(solution)/shard_map/reduce_scatter | solution.py:105
  1121.9 5.9 all_gather.31
  (233 shorter events, 34.3 us)
Async XLA Ops:
  8.0 4.0 copy-start
  8.0 4.2 copy-start.41
  8.0 27.8 %all-gather.8.cloned.1.call-start = ((), (), s32[]{:S(2)}) async-start(), calls=%async_computation.7 | async-start | bytes 2621440 | tf_op jit(solution)/shard_map/all_gather | solution.py:83
  9.9 2.1 copy-start.55
  12.0 99.1 %all-gather.10.cloned.1.call-start = ((), (), s32[]{:S(2)}) async-start(), calls=%async_computation.8 | async-start | bytes 4718592 | tf_op jit(solution)/shard_map/all_gather | solution.py:101
  13.1 103.0 %copy-start.53 = (s32[1,512]{1,0:T(1,128)S(1)}, s32[1,512]{1,0:T(1,128)}, u32[]{:S(2)}) copy-start(s32[1,512]{1,0:T(1,128)} %param.19) | copy-start | bytes 6148
  13.1 117.8 %all-gather.12.cloned.1.call-start = ((), (), s32[]{:S(2)}) async-start(), calls=%async_computation.9 | async-start | bytes 1474560 | tf_op jit(solution)/shard_map/all_gather | solution.py:983
  35.9 80.5 %copy-start.25 = (bf16[512,2048]{1,0:T(8,128)(2,1)S(1)}, bf16[512,2048]{1,0:T(8,128)(2,1)}, u32[]{:S(2)}) copy-start(bf16[512,2048]{1,0:T(8,128)(2,1)} %all-gather.8.cloned.1.call-done) | copy-start | bytes 6291460
  114.5 57.6 %all-gather.14.cloned.1.call-start = ((), (), s32[]{:S(2)}) async-start(), calls=%async_computation.10 | async-start | bytes 1179648 | tf_op jit(solution)/shard_map/all_gather | solution.py:101
  115.1 107.5 %all-gather.16.cloned.1.call-start = ((), (), s32[]{:S(2)}) async-start(), calls=%async_computation.11 | async-start | bytes 2359296 | tf_op jit(solution)/shard_map/all_gather | solution.py:943
  115.7 166.1 %reduce-scatter.6.cloned.1.call-start = ((), (), s32[]{:S(2)}) async-start(), calls=%async_computation.12 | async-start | bytes 2621440 | tf_op jit(solution)/shard_map/reduce_scatter | solution.py:91
  115.7 60.9 %copy-start.57 = (f32[32]{0:T(128)}, f32[32]{0:T(128)S(1)}, u32[]{:S(2)}) copy-start(f32[32]{0:T(128)S(1)} %multiply_power_fusion) | copy-start | bytes 388
  116.1 5.0 copy-start.34
  116.1 5.0 copy-start.36
  116.3 64.0 %copy-start.31 = (pred[512,512]{0,1:T(8,128)(4,1)}, pred[512,512]{0,1:T(8,128)(4,1)S(1)}, u32[]{:S(2)}) copy-start(pred[512,512]{0,1:T(8,128)(4,1)S(1)} %fusion.21) | copy-start | bytes 786436
  120.2 51.9 %copy-start.49 = (f32[512]{0:T(512)S(1)}, f32[512]{0:T(512)}, u32[]{:S(2)}) copy-start(f32[512]{0:T(512)} %param.24) | copy-start | bytes 6148
  121.8 55.3 %copy-start.38 = (bf16[512,4,32]{0,2,1:T(8,128)(2,1)}, bf16[512,4,32]{0,2,1:T(8,128)(2,1)S(1)}, u32[]{:S(2)}) copy-start(bf16[512,4,32]{0,2,1:T(8,128)(2,1)S(1)} %get-tuple-element.118) | copy-start | bytes 393220
  130.9 41.1 %copy-start.3 = (f32[512,576]{0,1:T(8,128)S(1)}, f32[512,576]{0,1:T(8,128)}, u32[]{:S(2)}) copy-start(f32[512,576]{0,1:T(8,128)} %all-gather.12.cloned.1.call-done) | copy-start | bytes 3538948
  134.0 42.6 %copy-start.51 = (f32[512]{0:T(512)}, f32[512]{0:T(512)S(1)}, u32[]{:S(2)}) copy-start(f32[512]{0:T(512)S(1)} %get-tuple-element.132) | copy-start | bytes 6148
  176.6 3.7 copy-start.19
  176.7 2.7 copy-start.22
  177.1 2.3 copy-start.29
  179.4 2.1 copy-start.10
  182.8 44.0 %copy-start.62 = (bf16[4,128,512]{2,1,0:T(8,128)(2,1)}, bf16[4,128,512]{2,1,0:T(8,128)(2,1)S(1)}, u32[]{:S(2)}) copy-start(bf16[4,128,512]{2,1,0:T(8,128)(2,1)S(1)} %convolution_convert_fusion.10) | copy-start | bytes 1572868
  226.8 2.1 copy-start.42
  226.8 2.1 copy-start.43
  226.8 2.1 copy-start.44
  226.9 204.4 %all-gather.18.cloned.1.call-start = ((), (), s32[]{:S(2)}) async-start(), calls=%async_computation.13 | async-start | bytes 17301504 | tf_op jit(solution)/shard_map/all_gather | solution.py:87
  229.0 7.3 copy-start.59
  230.1 49.9 %all-to-all-start = ((bf16[8,264,256]{2,1,0:T(8,128)(2,1)}), bf16[8,264,256]{2,1,0:T(8,128)(2,1)S(1)}, u32[]{:S(2)}, u32[]{:S(2)}) async-start(bf16[8,264,256]{2,1,0:T(8,128)(2,1)} %bitcast.26), calls=%async_computation.1 | async-start | bytes 2162688 | tf_op jit(solution)/shard_map/all_to_all | solution.py:967
  235.9 558.3 %all-gather.20.cloned.1.call-start = ((), (), s32[]{:S(2)}) async-start(), calls=%async_computation.14 | async-start | bytes 2621440 | tf_op jit(solution)/shard_map/all_gather | solution.py:83
  280.0 3.1 copy-start.47
  281.0 3.4 copy-start.27
  528.3 4.0 copy-start.26
  546.2 2.3 copy-start.12
  546.2 2.3 copy-start.14
  585.1 181.7 %copy-start.28 = (bf16[2048,64]{0,1:T(8,128)(2,1)S(1)}, bf16[2048,64]{0,1:T(8,128)(2,1)}, u32[]{:S(2)}) copy-start(bf16[2048,64]{0,1:T(8,128)(2,1)} %param.28) | copy-start | bytes 786436
  765.4 3.3 copy-start.6
  765.4 3.3 copy-start.17
  765.4 3.3 copy-start.33
  766.7 3.8 copy-start.45
  770.5 27.4 %copy-start.32 = (pred[512,512]{0,1:T(8,128)(4,1)S(1)}, pred[512,512]{0,1:T(8,128)(4,1)}, u32[]{:S(2)}) copy-start(pred[512,512]{0,1:T(8,128)(4,1)} %copy-done.31) | copy-start | bytes 786436
  770.6 68.7 %all-reduce.6.cloned.1.call-start = ((), (), s32[]{:S(2)}) async-start(), calls=%async_computation.19 | async-start | bytes 1179648 | tf_op jit(solution)/shard_map/psum | solution.py:1119
  794.2 3.8 copy-start.11
  803.4 2.0 copy-start.4
  805.3 136.7 %reduce-scatter.12.cloned.1.call-start = ((), (), s32[]{:S(2)}) async-start(), calls=%async_computation.17 | async-start | bytes 1179648 | tf_op jit(solution)/shard_map/reduce_scatter | solution.py:105
  807.2 185.4 %reduce-scatter.14.cloned.1.call-start = ((), (), s32[]{:S(2)}) async-start(), calls=%async_computation.18 | async-start | bytes 2359296 | tf_op jit(solution)/shard_map/reduce_scatter | solution.py:105
  811.6 3.3 copy-start.35
  811.6 3.3 copy-start.37
  811.6 214.3 %reduce-scatter.8.cloned.1.call-start = ((), (), s32[]{:S(2)}) async-start(), calls=%async_computation.15 | async-start | bytes 2621440 | tf_op jit(solution)/shard_map/reduce_scatter | solution.py:91
  814.9 26.7 %copy-start.58 = (f32[32]{0:T(128)S(1)}, f32[32]{0:T(128)}, u32[]{:S(2)}) copy-start(f32[32]{0:T(128)} %copy-done.57) | copy-start | bytes 388
  814.9 27.1 %copy-start.54 = (f32[512]{0:T(512)S(1)}, f32[512]{0:T(512)}, u32[]{:S(2)}) copy-start(f32[512]{0:T(512)} %get-tuple-element.131) | copy-start | bytes 6148
  839.3 2.7 copy-start.8
  840.2 2.4 copy-start.46
  846.4 274.6 %reduce-scatter.10.cloned.1.call-start = ((), (), s32[]{:S(2)}) async-start(), calls=%async_computation.16 | async-start | bytes 4202496 | tf_op jit(solution)/shard_map/reduce_scatter | solution.py:105
  853.6 8.9 copy-start.13
  853.6 8.9 copy-start.15
  872.7 66.3 %all-to-all-start.1 = ((bf16[8,264,256]{2,1,0:T(8,128)(2,1)}), bf16[8,264,256]{2,1,0:T(8,128)(2,1)S(1)}, u32[]{:S(2)}, u32[]{:S(2)}) async-start(bf16[8,264,256]{2,1,0:T(8,128)(2,1)} %maximum_bitcast_fusion), calls=%async_computation.6 | async-start | bytes 2162688 | tf_op jit(solution)/shard_map/all_to_all | solution.py:1054
  940.6 85.3 %copy-start.48 = (f32[2048]{0:T(1024)S(1)}, f32[2048]{0:T(1024)}, u32[]{:S(2)}) copy-start(f32[2048]{0:T(1024)} %param.21) | copy-start | bytes 24580
  940.6 85.3 %copy-start.56 = (f32[128]{0:T(128)S(1)}, f32[128]{0:T(128)}, u32[]{:S(2)}) copy-start(f32[128]{0:T(128)} %copy-done.55) | copy-start | bytes 1540
  940.7 118.8 %copy-start.18 = (f32[128,2048]{1,0:T(8,128)S(1)}, f32[128,2048]{1,0:T(8,128)}, u32[]{:S(2)}) copy-start(f32[128,2048]{1,0:T(8,128)} %get-tuple-element.109) | copy-start | bytes 3145732
  940.7 118.8 %copy-start.60 = (f32[128]{0:T(128)S(1)}, f32[128]{0:T(128)}, u32[]{:S(2)}) copy-start(f32[128]{0:T(128)} %get-tuple-element.133) | copy-start | bytes 1540
  1025.9 33.7 %copy-start.21 = (bf16[128,2048]{1,0:T(8,128)(2,1)S(1)}, bf16[128,2048]{1,0:T(8,128)(2,1)}, u32[]{:S(2)}) copy-start(bf16[128,2048]{1,0:T(8,128)(2,1)} %reduce-scatter.8.cloned.1.call-done) | copy-start | bytes 1572868
  1059.6 71.3 %copy-start.1 = (bf16[256,576]{0,1:T(8,128)(2,1)S(1)}, bf16[256,576]{0,1:T(8,128)(2,1)}, u32[]{:S(2)}) copy-start(bf16[256,576]{0,1:T(8,128)(2,1)} %param.23) | copy-start | bytes 884740
  (14 other events, 20.8 us)
Sparse Core Ops, SparseCore 0:
  12.1 23.7 all-gather.7
  38.5 72.4 all-gather.9
  114.6 16.2 all-gather.11
  132.9 39.1 all-gather.13
  174.0 48.6 all-gather.15
  227.0 31.5 reduce-scatter.5
  770.7 23.5 all-gather.19
  805.5 33.8 all-reduce.5
  842.7 79.0 reduce-scatter.11
  925.2 67.3 reduce-scatter.13
  995.1 30.6 reduce-scatter.7
  1029.4 91.6 reduce-scatter.9
Sparse Core Ops, SparseCore 1:
  230.8 168.3 all-gather.17

commit v2 on v1

--- a/solution.py
+++ b/solution.py
@@ -144,11 +144,7 @@
         def _(partner=partner):
             pl.semaphore_signal(barrier, inc=1, device_id=partner, device_id_type=MESH_ID)
 
-    for there, partner in partners:
-
-        @pl.when(there)
-        def _():
-            pl.semaphore_wait(barrier, 1)
+    pl.semaphore_wait(barrier, sum(jnp.int32(there) for there, _ in partners))
 
 
 def remote(src, dst, send_sem, recv_sem, partner):
@@ -368,39 +364,62 @@
             def _(h=h):
                 down_copy(a, l, h).start()
 
-    def stage_four(a, l):
-        i = at(a, l, side, wide)
+    def onward(a, l, up):
+        @pl.when(jnp.logical_and(has_below, has_above))
+        def _():
+            copy, arrived = (up_copy, up_in) if up else (down_copy, down_in)
+            for h in range(2):
+                copy(a, l, h).wait_recv()
+                add(at(a, l, side, wide), parts[h], arrived.at[(a * lines + l) * 2 + h])
+                copy(a, l, h).start()
+
+    def passing(a, j):
+        high, low = lines - 1 - j, j
+        lower_half = line * 2 < lines
+
+        def go(up, when):
+            l = high if up else low
+            beyond = line < l if up else line > l
+
+            @pl.when(jnp.logical_and(when, beyond))
+            def _():
+                onward(a, l, up)
+
+        go(True, lower_half)
+        go(False, lower_half)
+        go(False, jnp.logical_not(lower_half))
+        go(True, jnp.logical_not(lower_half))
+
+    def final(a):
         for h in range(2):
 
-            @pl.when(jnp.logical_and(has_below, line <= l))
+            @pl.when(has_below)
             def _(h=h):
-                up_copy(a, l, h).wait_recv()
-                add(i, parts[h], up_in.at[(a * lines + l) * 2 + h])
-
-            @pl.when(jnp.logical_and(has_above, line >= l))
+                up_copy(a, line, h).wait_recv()
+                add(at(a, line, side, wide), parts[h], up_in.at[(a * lines + line) * 2 + h])
+
+            @pl.when(has_above)
             def _(h=h):
-                down_copy(a, l, h).wait_recv()
-                add(i, parts[h], down_in.at[(a * lines + l) * 2 + h])
-
-            @pl.when(jnp.logical_and(jnp.logical_and(has_below, has_above), line < l))
-            def _(h=h):
-                up_copy(a, l, h).start()
-
-            @pl.when(jnp.logical_and(jnp.logical_and(has_below, has_above), line > l))
-            def _(h=h):
-                down_copy(a, l, h).start()
-
-    for step in range(len(items) + 3):
+                down_copy(a, line, h).wait_recv()
+                add(at(a, line, side, wide), parts[h], down_in.at[(a * lines + line) * 2 + h])
+
+        outs[a][...] = own[at(a, line, side, wide)].astype(F32)
+
+    passes = {}
+    for a in range(count):
+        for j in range(lines - 1):
+            after = a * lines + min(2 * j + 2, lines - 1) + 3
+            passes.setdefault(after, []).append(functools.partial(passing, a, j))
+        passes.setdefault(a * lines + lines + 3, []).append(functools.partial(final, a))
+    for step in range(len(items) + 4):
         if step < len(items):
             stage_one(*items[step])
         if 0 <= step - 1 < len(items):
             stage_two(*items[step - 1])
         if 0 <= step - 2 < len(items):
             stage_three(*items[step - 2])
-        if 0 <= step - 3 < len(items):
-            stage_four(*items[step - 3])
-    for a in range(count):
-        outs[a][...] = own[at(a, line, side, wide)].astype(F32)
+        for action in passes.get(step, []):
+            action()
     if small:
         small_finish()
     for a, l in items:
@@ -701,6 +720,430 @@
     return n_row == 4 and n_col % 2 == 0 and tokens % 32 == 0 and held < 58 * 1024 * 1024
 
 
+def row_mates(wide, core, line, side):
+    return to_place(wide, 1 - core, line, side), to_place(1 - wide, core, line, side)
+
+
+def strip(ref, dim, index, size):
+    start = pl.multiple_of(index * size, size)
+    return ref.at[pl.ds(start, size)] if dim == 0 else ref.at[:, pl.ds(start, size)]
+
+
+def mixed_gather_body(lines, dims, flips, small, *refs):
+    count = len(dims)
+    cols, row_ref, refs = refs[:count], refs[count], refs[count + 1 :]
+    if small:
+        small_ref, refs = refs[0], refs[1:]
+    col_outs, row_out, refs = refs[:count], refs[count], refs[count + 1 :]
+    if small:
+        small_out, refs = refs[0], refs[1:]
+    local_sem, core_send, core_recv, wide_send, wide_recv = refs[:5]
+    refs = refs[5:]
+    if count:
+        side_send, side_recv, up_send, up_recv, down_send, down_recv = refs[:6]
+        refs = refs[6:]
+    wide, core, line, side = places()
+    core_mate, wide_mate = row_mates(wide, core, line, side)
+    side_mate = to_place(wide, core, line, 1 - side)
+    above = to_place(wide, core, line + 1, side)
+    below = to_place(wide, core, line - 1, side)
+    has_above = line < lines - 1
+    has_below = line > 0
+    partners = [(core >= 0, core_mate), (core >= 0, wide_mate)]
+    if count:
+        partners += [(core >= 0, side_mate), (has_above, above), (has_below, below)]
+    greet(partners, small)
+
+    def spot(m, l, s):
+        size = cols[m].shape[dims[m]]
+        return strip(col_outs[m], dims[m], l * 2 + s, size)
+
+    def line_copy(m, l, s, up, here=False):
+        n = (m * lines + l) * 2 + s
+        return remote(
+            cols[m] if here else spot(m, l, s),
+            spot(m, l, s),
+            (up_send if up else down_send).at[n],
+            (up_recv if up else down_recv).at[n],
+            above if up else below,
+        )
+
+    def side_copy(m, l, here=False):
+        n = m * lines + l
+        return remote(
+            cols[m] if here else spot(m, l, side),
+            spot(m, l, side),
+            side_send.at[n],
+            side_recv.at[n],
+            side_mate,
+        )
+
+    tokens = row_ref.shape[0]
+
+    def row_spot(w, k):
+        return strip(row_out, 0, w * 2 + k, tokens)
+
+    def core_copy(n):
+        src = row_ref if n == 0 else row_spot(1 - wide, core)
+        dst = row_spot(wide if n == 0 else 1 - wide, core)
+        return remote(src, dst, core_send.at[n], core_recv.at[n], core_mate)
+
+    def to_line(m, s, here):
+        @pl.when(has_above)
+        def _():
+            line_copy(m, line, s, True, here).start()
+
+        @pl.when(has_below)
+        def _():
+            line_copy(m, line, s, False, here).start()
+
+    wide_copy = remote(row_ref, row_spot(wide, core), wide_send.at[0], wide_recv.at[0], wide_mate)
+    wide_copy.start()
+    core_copy(0).start()
+    for m in range(count):
+
+        to_line(m, side, True)
+        side_copy(m, line, True).start()
+    if small:
+        small_start, small_finish = small_exchange(small_ref, small_out, *refs[:2], False)
+        small_start()
+    local = [pltpu.make_async_copy(row_ref, row_spot(wide, core), local_sem.at[count])]
+    for m in range(count):
+        local.append(pltpu.make_async_copy(cols[m], spot(m, line, side), local_sem.at[m]))
+    for copy in local:
+        copy.start()
+
+    def from_line(m, dist, up):
+        l = line - dist if up else line + dist
+
+        @pl.when(l >= 0 if up else l < lines)
+        def _():
+            for s in (side, 1 - side) if flips[m] else (side,):
+                line_copy(m, l, s, up).wait_recv()
+
+                @pl.when(has_above if up else has_below)
+                def _(s=s):
+                    line_copy(m, l, s, up).start()
+
+            if not flips[m]:
+                side_copy(m, l).start()
+
+    for m in range(count):
+        if flips[m]:
+            side_copy(m, line).wait_recv()
+            to_line(m, 1 - side, False)
+
+    def pass_on():
+        wide_copy.wait_recv()
+        core_copy(1).start()
+
+    if lines == 1 or not count:
+        pass_on()
+    for dist in range(1, lines if count else 1):
+        for m in range(count):
+            from_line(m, dist, True)
+            from_line(m, dist, False)
+        if dist == 1:
+            pass_on()
+    if small:
+        small_finish()
+    for copy in local:
+        copy.wait()
+    wide_copy.wait_send()
+    for n in range(2):
+        core_copy(n).wait()
+    for m in range(count):
+        if flips[m]:
+            side_copy(m, line).wait_send()
+        for l in range(lines):
+            if not flips[m]:
+                side_copy(m, l).wait()
+            for s in range(2) if flips[m] else (side,):
+
+                @pl.when(jnp.logical_and(has_above, line >= l))
+                def _(m=m, l=l, s=s):
+                    line_copy(m, l, s, True).wait_send()
+
+                @pl.when(jnp.logical_and(has_below, line <= l))
+                def _(m=m, l=l, s=s):
+                    line_copy(m, l, s, False).wait_send()
+
+
+def mixed_gather(col_values, dims, flips, row_value, small_value, number):
+    n_row, n_col = lax.axis_size("row"), lax.axis_size("col")
+    lines, count, small = n_col // 2, len(dims), small_value is not None
+    tokens, width = row_value.shape
+    hbm, vmem = pl.BlockSpec(memory_space=pl.ANY), pl.BlockSpec(memory_space=pltpu.VMEM)
+    out_shape = []
+    for value, dim in zip(col_values, dims):
+        shape = list(value.shape)
+        shape[dim] *= n_col
+        out_shape.append(jax.ShapeDtypeStruct(tuple(shape), value.dtype))
+    out_shape.append(jax.ShapeDtypeStruct((n_row * tokens, width), row_value.dtype))
+    operands = [*col_values, row_value]
+    in_specs, out_specs = [hbm] * count + [vmem], [hbm] * (count + 1)
+    dma = pltpu.SemaphoreType.DMA
+    scratch = [dma((count + 1,)), dma((2,)), dma((2,)), dma((1,)), dma((1,))]
+    if count:
+        scratch += [dma((count * lines,))] * 2 + [dma((2 * count * lines,))] * 4
+    if small:
+        operands.append(small_value)
+        in_specs.append(vmem)
+        out_specs.append(vmem)
+        out_shape.append(
+            jax.ShapeDtypeStruct((n_row * n_col, *small_value.shape), small_value.dtype)
+        )
+        scratch += [dma((n_row * n_col,))] * 2
+    return pl.pallas_call(
+        functools.partial(mixed_gather_body, lines, tuple(dims), tuple(flips), small),
+        out_shape=out_shape,
+        in_specs=in_specs,
+        out_specs=out_specs,
+        scratch_shapes=scratch,
+        compiler_params=pltpu.CompilerParams(collective_id=number, has_side_effects=True),
+        name=f"mixed_gather_{number}",
+    )(*operands)
+
+
+def mixed_total_body(lines, dims, flips, *refs):
+    count = len(dims)
+    cols, row_ref, refs = refs[:count], refs[count], refs[count + 1 :]
+    col_outs, row_out, refs = refs[:count], refs[count], refs[count + 1 :]
+    row_own, row_core, row_wide, refs = refs[0], refs[1], refs[2], refs[3:]
+    owns, refs = refs[:count], refs[count:]
+    side_ins, refs = refs[:count], refs[count:]
+    up_ins, refs = refs[:count], refs[count:]
+    down_ins, refs = refs[:count], refs[count:]
+    row_load, core_send, core_recv, wide_send, wide_recv = refs[:5]
+    if count:
+        load_sem, side_send, side_recv, up_send, up_recv, down_send, down_recv = refs[5:12]
+    wide, core, line, side = places()
+    core_mate, wide_mate = row_mates(wide, core, line, side)
+    side_mate = to_place(wide, core, line, 1 - side)
+    above = to_place(wide, core, line + 1, side)
+    below = to_place(wide, core, line - 1, side)
+    has_above = line < lines - 1
+    has_below = line > 0
+    partners = [(core >= 0, core_mate), (core >= 0, wide_mate)]
+    if count:
+        partners += [(core >= 0, side_mate), (has_above, above), (has_below, below)]
+    greet(partners, False)
+    tokens = row_out.shape[0]
+
+    def core_copy(w):
+        return remote(
+            strip(row_ref, 0, w * 2 + 1 - core, tokens),
+            row_core.at[w],
+            core_send.at[w],
+            core_recv.at[w],
+            core_mate,
+        )
+
+    def row_loaded(w):
+        return pltpu.make_async_copy(
+            strip(row_ref, 0, w * 2 + core, tokens), row_own.at[w], row_load.at[w]
+        )
+
+    wide_copy = remote(row_own.at[1 - wide], row_wide, wide_send.at[0], wide_recv.at[0], wide_mate)
+
+    def source(m, l, s):
+        return strip(cols[m], dims[m], l * 2 + s, col_outs[m].shape[dims[m]])
+
+    def side_copy(m, l):
+        n = m * lines + l
+        return remote(
+            owns[m].at[l, 1 - side] if flips[m] else source(m, l, 1 - side),
+            side_ins[m].at[0 if flips[m] else l],
+            side_send.at[n],
+            side_recv.at[n],
+            side_mate,
+        )
+
+    def own_at(m, l, s):
+        return owns[m].at[l, s] if flips[m] else owns[m].at[l]
+
+    def loaded(m, l, s):
+        return pltpu.make_async_copy(
+            source(m, l, s), own_at(m, l, s), load_sem.at[(m * lines + l) * 2 + s]
+        )
+
+    def line_copy(m, l, s, up):
+        n = (m * lines + l) * 2 + s
+        into = (up_ins if up else down_ins)[m]
+        return remote(
+            own_at(m, l, s),
+            into.at[l, s] if flips[m] else into.at[l],
+            (up_send if up else down_send).at[n],
+            (up_recv if up else down_recv).at[n],
+            above if up else below,
+        )
+
+    def sides(m):
+        return (1 - side, side) if flips[m] else (side,)
+
+    for w in range(2):
+        core_copy(w).start()
+        row_loaded(w).start()
+    items = [(m, l) for l in (line_order(lines) if count else []) for m in range(count)]
+    for m, l in items:
+        for s in sides(m):
+            loaded(m, l, s).start()
+        if not flips[m]:
+            side_copy(m, l).start()
+    for j in range(2):
+        w = wide if j else 1 - wide
+        row_loaded(w).wait()
+        core_copy(w).wait_recv()
+        row_own[w] = (row_own[w].astype(F32) + row_core[w].astype(F32)).astype(BF16)
+        if j == 0:
+            wide_copy.start()
+
+    def add(m, l, s, other):
+        mine = own_at(m, l, s)
+        mine[...] = (mine[...].astype(F32) + other.astype(F32)).astype(BF16)
+
+    def near(m, l):
+        for s in sides(m):
+            loaded(m, l, s).wait()
+            if not flips[m]:
+                side_copy(m, l).wait_recv()
+                add(m, l, s, side_ins[m][l])
+
+            @pl.when(jnp.logical_and(line == 0, l > 0))
+            def _(s=s):
+                line_copy(m, l, s, True).start()
+
+            @pl.when(jnp.logical_and(line == lines - 1, l < lines - 1))
+            def _(s=s):
+                line_copy(m, l, s, False).start()
+
+    def onward(m, l, up):
+        @pl.when(jnp.logical_and(has_below, has_above))
+        def _():
+            for s in sides(m):
+                where = (l, s) if flips[m] else (l,)
+                line_copy(m, l, s, up).wait_recv()
+                add(m, l, s, (up_ins if up else down_ins)[m][where])
+                line_copy(m, l, s, up).start()
+
+    def passing(m, j):
+        high, low = lines - 1 - j, j
+        lower_half = line * 2 < lines
+
+        def go(up, when):
+            l = high if up else low
+            beyond = line < l if up else line > l
+
+            @pl.when(jnp.logical_and(when, beyond))
+            def _():
+                onward(m, l, up)
+
+        go(True, lower_half)
+        go(False, lower_half)
+        go(False, jnp.logical_not(lower_half))
+        go(True, jnp.logical_not(lower_half))
+
+    def final(m):
+        for s in sides(m):
+            where = (line, s) if flips[m] else (line,)
+
+            @pl.when(has_below)
+            def _(s=s, where=where):
+                line_copy(m, line, s, True).wait_recv()
+                add(m, line, s, up_ins[m][where])
+
+            @pl.when(has_above)
+            def _(s=s, where=where):
+                line_copy(m, line, s, False).wait_recv()
+                add(m, line, s, down_ins[m][where])
+
+        if flips[m]:
+            side_copy(m, line).start()
+
+    flipped = [m for m in range(count) if flips[m]]
+    straight = [m for m in range(count) if not flips[m]]
+    order = line_order(lines)
+    for l in order:
+        for m in flipped:
+            near(m, l)
+    if count:
+        for step in range(lines + 2):
+            if step < lines:
+                for m in straight:
+                    near(m, order[step])
+            if step < lines - 1:
+                for m in flipped:
+                    passing(m, step)
+            if step == lines - 1:
+                for m in flipped:
+                    final(m)
+            if 2 <= step < lines + 1:
+                for m in straight:
+                    passing(m, step - 2)
+            if step == lines + 1:
+                for m in straight:
+                    final(m)
+    wide_copy.wait()
+    row_out[...] = row_own[wide].astype(F32) + row_wide[...].astype(F32)
+    for w in range(2):
+        core_copy(w).wait_send()
+    for m in range(count):
+        if flips[m]:
+            side_copy(m, line).wait()
+            add(m, line, side, side_ins[m][0])
+        col_outs[m][...] = own_at(m, line, side)[...].astype(F32)
+        for l in range(lines):
+            if not flips[m]:
+                side_copy(m, l).wait_send()
+            for s in sides(m):
+
+                @pl.when(jnp.logical_and(has_above, line < l))
+                def _(m=m, l=l, s=s):
+                    line_copy(m, l, s, True).wait_send()
+
+                @pl.when(jnp.logical_and(has_below, line > l))
+                def _(m=m, l=l, s=s):
+                    line_copy(m, l, s, False).wait_send()
+
+
+def mixed_total(col_values, dims, flips, row_value, number):
+    n_row, n_col = lax.axis_size("row"), lax.axis_size("col")
+    lines, count = n_col // 2, len(dims)
+    tokens, width = row_value.shape[0] // n_row, row_value.shape[1]
+    hbm, vmem = pl.BlockSpec(memory_space=pl.ANY), pl.BlockSpec(memory_space=pltpu.VMEM)
+    blocks = []
+    for value, dim in zip(col_values, dims):
+        shape = list(value.shape)
+        shape[dim] //= n_col
+        blocks.append(tuple(shape))
+    dma = pltpu.SemaphoreType.DMA
+    scratch = [
+        pltpu.VMEM((2, tokens, width), BF16),
+        pltpu.VMEM((2, tokens, width), BF16),
+        pltpu.VMEM((tokens, width), BF16),
+    ]
+    doubled = [(lines, 2) if flip else (lines,) for flip in flips]
+    side_held = [(1,) if flip else (lines,) for flip in flips]
+    for lead in (doubled, side_held, doubled, doubled):
+        scratch += [pltpu.VMEM((*d, *shape), BF16) for d, shape in zip(lead, blocks)]
+    scratch += [dma((2,)), dma((2,)), dma((2,)), dma((1,)), dma((1,))]
+    if count:
+        scratch += [dma((2 * count * lines,))] + [dma((count * lines,))] * 2
+        scratch += [dma((2 * count * lines,))] * 4
+    return pl.pallas_call(
+        functools.partial(mixed_total_body, lines, tuple(dims), tuple(flips)),
+        out_shape=[jax.ShapeDtypeStruct(shape, F32) for shape in blocks]
+        + [jax.ShapeDtypeStruct((tokens, width), F32)],
+        in_specs=[hbm] * (count + 1),
+        out_specs=[vmem] * (count + 1),
+        scratch_shapes=scratch,
+        compiler_params=pltpu.CompilerParams(
+            collective_id=number, has_side_effects=True, vmem_limit_bytes=VMEM_LIMIT
+        ),
+        name=f"mixed_total_{number}",
+    )(*col_values, row_value)
+
+
 def small_body(personal, value_ref, out_ref, send_sem, recv_sem):
     greet([], True)
     start, finish = small_exchange(value_ref, out_ref, send_sem, recv_sem, personal)
@@ -735,6 +1178,24 @@
         return kernel_total(partials, small_value, number)
     exchanged = lax.all_to_all(small_value, EVERY, split_axis=0, concat_axis=0, tiled=True)
     return *[every_total(p) for p in partials], exchanged
+
+
+def mixed_fits(col_values):
+    n_row, lines = lax.axis_size("row"), lax.axis_size("col") // 2
+    return n_row == 4 and (not col_values or (lax.axis_size("col") % 2 == 0 and lines <= 8))
+
+
+def gather_mixed(col_values, dims, flips, row_value, small_value, number):
+    if mixed_fits(col_values):
+        return mixed_gather(col_values, dims, flips, row_value, small_value, number)
+    cols = [lax.all_gather(v, "col", axis=d, tiled=True) for v, d in zip(col_values, dims)]
+    return *cols, token_rows(row_value), every_token(small_value[None])
+
+
+def total_mixed(col_values, dims, flips, row_value, number):
+    if mixed_fits(col_values):
+        return mixed_total(col_values, dims, flips, row_value, number)
+    return *[col_total(v, d) for v, d in zip(col_values, dims)], row_total(row_value)
 
 
 def padded_rows(values):
@@ -932,17 +1393,21 @@
 
     scale_one = rms_scale(stream)
     normed_one = (stream * scale_one * first_gain).astype(BF16)
-    seq_normed = token_rows(normed_one)
     down_cols = latent_down.shape[1] // n_row
     own_down = lax.dynamic_slice_in_dim(latent_down, own_row * down_cols, down_cols, 1)
+    output_rows = output_weight.shape[0]
     query_cols = query_weight.shape[1]
-    query_down = col_gather(jnp.concatenate([query_weight, own_down], axis=1))
-    query_all = query_down[:, :query_cols]
-    down_all = query_down[:, query_cols:]
-    expand_all = col_gather(latent_up)
-    output_all = lax.all_gather(output_weight, "col", axis=1, tiled=True)
-
-    all_routes = kernel_small(padded_rows(own_routes.astype(F32).T), False, 1)
+    query_all, output_down, expand_all, seq_normed, all_routes = gather_mixed(
+        [query_weight, jnp.concatenate([output_weight, own_down.T], axis=0), latent_up],
+        [0, 1, 0],
+        [False, False, True],
+        normed_one,
+        padded_rows(own_routes.astype(F32).T),
+        1,
+    )
+    output_all = output_down[:output_rows]
+    down_all = output_down[output_rows:]
+
     all_routes = all_routes[:, :TOPK].astype(jnp.int32)
     grad_all = every_token(grad_out.astype(BF16))
     local_ids = own_col * local_experts + jnp.arange(local_experts)
@@ -980,7 +1445,7 @@
         ],
         axis=-1,
     ).astype(BF16)
-    latent_all = lax.all_gather(matmul(seq_normed, down_all), "row", axis=1, tiled=True)
+    latent_all = lax.all_gather(outer_cols(seq_normed, down_all), "row", axis=1, tiled=True)
     latent = latent_all[:, :LATENT]
     scale_latent = rms_scale(latent)
     latent_normed = (latent * scale_latent * latent_gain).astype(BF16)
@@ -1002,7 +1467,9 @@
         .astype(BF16)
         .reshape(length, heads_local * VD)
     )
-    residual = stream + row_total(matmul(heads_out, output_all))
+    heads_out, grad_all = lax.optimization_barrier((heads_out, grad_all))
+    (attn_total,) = total_mixed([], [], [], matmul(heads_out, output_all).astype(BF16), 6)
+    residual = stream + attn_total
 
     scale_two = rms_scale(residual)
     normed_two = (residual * scale_two * second_gain).astype(BF16)
@@ -1067,14 +1534,15 @@
     gate_grad = jnp.sum(jnp.where(chosen, token_dot[:, None, :], 0.0), axis=-1)
     picked_grad = gate_probs * (gate_grad - jnp.sum(gate_probs * gate_grad, axis=-1, keepdims=True))
     logit_grad = jnp.sum(jnp.where(chosen, picked_grad[:, :, None], 0.0), axis=1).astype(BF16)
-    all_logit_grad = kernel_small(logit_grad, False, 4).reshape(-1, experts)
-    router_grad = inner_rows(all_normed, all_logit_grad)
 
     normed_two_grad = rows_total + outer_cols(logit_grad, router_weight)
     second_gain_part = jnp.sum(normed_two_grad * residual * scale_two, axis=0)
     residual_grad = grad_out + rms_back(residual, scale_two, normed_two_grad * second_gain)
 
-    seq_resid = token_rows(residual_grad.astype(BF16))
+    seq_resid, all_logit_grad = gather_mixed(
+        [], [], [], residual_grad.astype(BF16), logit_grad, 4
+    )
+    router_grad = inner_rows(all_normed, all_logit_grad.reshape(-1, experts))
     output_part = inner_rows(heads_out, seq_resid)
     heads_grad = outer_cols(seq_resid, output_all).astype(BF16).reshape(length, heads_local, VD)
     recomputed = jnp.exp(masked_scores(queries, attn_keys, allowed, softmax_scale) - log_total)
@@ -1129,23 +1597,30 @@
     latent_grad = rms_back(latent, scale_latent, latent_normed_grad * latent_gain)
     down_grad_in = jnp.concatenate([latent_grad, rope_grad], axis=-1).astype(BF16)
     own_down_grad = lax.dynamic_slice_in_dim(down_grad_in, own_row * down_cols, down_cols, 1)
-    both_grad = jnp.concatenate([query_full, own_down_grad], axis=1)
-    normed_one_grad = row_total(outer_cols(both_grad, query_down))
+    output_down_part = jnp.concatenate(
+        [output_part.astype(BF16), inner_rows(own_down_grad, seq_normed).astype(BF16)], axis=0
+    )
+    input_part = outer_cols(query_full, query_all) + matmul(own_down_grad, down_all)
+    query_grad, output_down_grad, latent_up_grad, normed_one_grad = total_mixed(
+        [inner_rows(seq_normed, query_full).astype(BF16), output_down_part, expand_part.astype(BF16)],
+        [0, 1, 0],
+        [False, False, True],
+        input_part.astype(BF16),
+        7,
+    )
+    output_grad = output_down_grad[:output_rows]
     first_gain_part = jnp.sum(normed_one_grad * stream * scale_one, axis=0)
     input_grad = (
         residual_grad + rms_back(stream, scale_one, normed_one_grad * first_gain)
     ).reshape(1, own_rows, width)
 
-    output_grad = col_total(output_part, 1)
-    latent_up_grad = col_total(expand_part, 0)
-    both_total = col_total(inner_rows(seq_normed, both_grad), 0)
-    query_grad = both_total[:, :query_cols]
-    latent_down_grad = lax.all_gather(
-        both_total[:, query_cols:].astype(BF16), "row", axis=1, tiled=True
-    ).astype(F32)
     gains = jnp.concatenate([first_gain_part, latent_gain_part, second_gain_part])
     gains = padded_rows(gains.reshape(-1, LATENT // 4))
-    gains = jnp.sum(kernel_small(gains, False, 5), axis=0).reshape(-1)
+    down_total, all_gains = gather_mixed(
+        [], [], [], output_down_grad[output_rows:].astype(BF16), gains, 5
+    )
+    latent_down_grad = down_total.astype(F32).T
+    gains = jnp.sum(all_gains, axis=0).reshape(-1)
     first_gain_grad = gains[:width]
     latent_gain_grad = gains[width : width + LATENT]
     second_gain_grad = gains[width + LATENT : 2 * width + LATENT]

time: 1150 us -> 976 us (0.85)
  waiting for transfers between devices: 374 us -> 133 us
  Pallas kernels: 563 us -> 647 us
    all_gather x6 -> x1, waiting for transfers between devices: 208 us -> 0.01 us  [on_device(): lax.all_gather(outer_cols(seq_normed, down_all), 'row', axis=1, tiled=True)]
    reduce_scatter x5 -> x0, waiting for transfers between devices: 141 us -> none  [the longest x3 109 us: col_total(): lax.psum_scatter(partial_value.astype(BF16), 'col', scatter_dimension=dim...]
    pallas_call x3 -> x5, Pallas kernels: 120 us -> 241 us  [the longest x3 127 us: mixed_gather(): pl.pallas_call(functools.partial(mixed_gather_body, lines, tuple(dims), t...]
    all_gather x1, waiting for transfers between devices: 0.01 us -> 98.6 us  [every_token(): return lax.all_gather(values, EVERY, axis=0, tiled=True)]
    pallas_call x1, Pallas kernels: 113 us -> 79.3 us  [kernel_gather(): pl.pallas_call(functools.partial(gather_body, lines, small), out_shape=ou...]
    dot_general x6 -> x7, matrix products: 39.7 us -> 31.1 us  [inner_rows(): lax.dot_general(left_side, right_side, ROWS_CONTRACT, preferred_element_t...]
    dot_general x6 -> x7, matrix products: 37.2 us -> 37.7 us  [outer_cols(): lax.dot_general(left_side, right_side, COLS_CONTRACT, preferred_element_t...]
  transfers between devices with their start and end apart: 15 -> 5, of which waited for: 10 -> 2; matrix products, arithmetic and copies ran while one was open for 10% -> 6% of each run, Pallas kernels for 22% -> 11%
where the time goes in v2:
time: 976 us; the launch traced here: 970 us
  Pallas kernels  647 us (66%)
  waiting for transfers between devices  133 us (14%)
  matrix products  93 us (10%)
  other arithmetic  43.5 us (4%)
  local copies, waits for them, and re-layouts  26.2 us (3%)
  between operations  15.1 us (2%)
  starting transfers between devices  13.2 us (1%)
    pallas_call x1, Pallas kernels, kernel_total(): pl.pallas_call(functools.partial(scatter_body, lines, count, small), out_...  176 us
    pallas_call x3, Pallas kernels, mixed_gather(): pl.pallas_call(functools.partial(mixed_gather_body, lines, tuple(dims), t...  127 us
    pallas_call x2, Pallas kernels, mixed_total(): pl.pallas_call(functools.partial(mixed_total_body, lines, tuple(dims), tu...  114 us
    all_gather x1, waiting for transfers between devices, every_token(): return lax.all_gather(values, EVERY, axis=0, tiled=True)  98.6 us
    pallas_call x1, Pallas kernels, run_experts(): pl.pallas_call(experts_body, grid=(count, rows // chunk), in_specs=[row_b...  80.8 us
    pallas_call x1, Pallas kernels, kernel_gather(): pl.pallas_call(functools.partial(gather_body, lines, small), out_shape=ou...  79.3 us
    dot_general x7, matrix products, outer_cols(): lax.dot_general(left_side, right_side, COLS_CONTRACT, preferred_element_t...  37.7 us
    pallas_call x2, Pallas kernels, combine_rows(): pl.pallas_call(functools.partial(combine_body, group), grid=(blocks // gr...  36.8 us
  transfers between devices with their start and end apart: 5, of which 2 were waited for; matrix products, arithmetic and copies ran while one was open for 6% of the time, Pallas kernels for 11%

profile of v2, /device:TPU:8, one launch (start us, length us, event | category | flops | bytes accessed | tf_op | source)
XLA Modules:
  0.0 970.3 jit_solution(4722941730360564047)
XLA Ops:
  7.2 1.3 fusion.12
  9.8 1.7 pad_maximum_fusion.9.refs_1_
  11.5 2.0 fusion.14.refs_3_
  14.1 77.7 %mixed_gather_1.1 = (bf16[2048,768]{1,0:T(8,128)(2,1)}, bf16[656,2048]{1,0:T(8,128)(2,1)}, bf16[512,1024]{1,0:T(8,128)(2,1)}, bf16[512,2048]{1,0:T(8,128)(2,1)}, f32[32,8,128]{2,1,0:T(8,128)}) custom-call(bf16[256,768]{1,0:T(8,128)(2,1)} %refs_0_.1, bf16[656,256]{1,0:T(8,128)(2,1)} %pad_maximum_fusion.9.refs_1_, bf16[64,1024]{1,0:T(8,128)(2,1)} %refs_2_.1, ...), custom_call_target="tpu_custom_call" | custom-call | tf_op jit(solution)/shard_map/mixed_gather_1/pallas_call | solution.py:897
  91.8 3.3 fusion.28
  97.6 7.5 all-to-all-start
  105.2 4.4 fusion.56
  109.6 1.1 copy-done.39
  111.2 1.3 fusion.3.place_ref
  113.5 1.8 subtract_convert_fusion.2
  115.3 2.4 fusion.55
  118.3 3.0 convolution_convert_fusion.7
  121.3 2.3 copy.146
  125.8 2.0 fusion.1
  129.9 1.4 convolution_convert_fusion.9
  133.1 98.6 %all-gather.5.cloned.1.call-done.rows_ref = bf16[4096,2048]{1,0:T(8,128)(2,1)} async-done(((bf16[128,2048]{1,0:T(8,128)(2,1)}), bf16[4096,2048]{1,0:T(8,128)(2,1)}) %all-gather.5.cloned.1.call-update) | async-done | bytes 16777232 | tf_op jit(solution)/shard_map/all_gather | solution.py:87
  231.7 4.2 convolution_convert_fusion.2.refs_0_
  235.9 28.6 %mixed_total_6.1 = f32[128,2048]{1,0:T(8,128)} custom-call(bf16[512,2048]{1,0:T(8,128)(2,1)} %convolution_convert_fusion.2.refs_0_), custom_call_target="tpu_custom_call" | custom-call | tf_op jit(solution)/shard_map/mixed_total_6/pallas_call | solution.py:1133
  264.5 1.5 multiply_reduce_fusion.3
  268.1 79.3 %gather_2.1 = (bf16[4096,2048]{1,0:T(8,128)(2,1)}, f32[32,8,128]{2,1,0:T(8,128)}) custom-call(bf16[128,2048]{1,0:T(8,128)(2,1)} %copy-done.10, f32[8,128]{1,0:T(8,128)} %pad.12.refs_1_), custom_call_target="tpu_custom_call" | custom-call | tf_op jit(solution)/shard_map/gather_2/pallas_call | solution.py:705
  347.5 10.2 %fusion.58 = f32[4096,176]{1,0:T(8,128)} fusion(bf16[4096,2048]{1,0:T(8,128)(2,1)} %get-tuple-element.48.rows_ref, bf16[176,2048]{1,0:T(8,128)(2,1)S(1)} %bitcast.172), kind=kOutput, calls=%fused_computation.163 | convolution fusion | flops 2952790016 | bytes 20381696 | tf_op jit(solution)/shard_map/dot_general | solution.py:31
  357.7 12.9 %multiply_convert_fusion.2 = (bf16[4096,88]{1,0:T(8,128)(2,1)S(1)}, bf16[4096,88]{1,0:T(8,128)(2,1)S(1)}, bf16[4096,88]{1,0:T(8,128)(2,1)S(1)}) fusion(f32[4096,176]{1,0:T(8,128)} %fusion.58, bf16[4096,2048]{1,0:T(8,128)(2,1)} %all-gather.5.cloned.1.call-done.rows_ref, bf16[88,2048]{1,0:T(8,128)(2,1)S(1)} %bitcast.177), kind=kOutput, calls=%fused_computation.26 | convolution fusion | flops 1481801728 | bytes 22183936 | tf_op jit(solution)/shard_map/dot_general | solution.py:31
  370.7 4.1 convolution_convert_fusion.3
  374.8 2.3 pad_maximum_fusion.1.extra_ref
  377.1 8.7 convolution_convert_fusion.5
  387.1 2.5 reshape.382.gate_ref
  389.6 16.0 %select_rows.2 = bf16[8,32,16,2048]{3,2,1,0:T(8,128)(2,1)} custom-call(bf16[32,128,128]{2,1,0:T(8,128)(2,1)} %fusion.3.place_ref, bf16[4096,2048]{1,0:T(8,128)(2,1)} %get-tuple-element.48.rows_ref), custom_call_target="tpu_custom_call" | custom-call | flops 2147483648 | bytes 33554432 | tf_op jit(solution)/shard_map/select_rows/pallas_call | solution.py:1225
  405.6 16.0 %select_rows.3 = bf16[8,32,16,2048]{3,2,1,0:T(8,128)(2,1)} custom-call(bf16[32,128,128]{2,1,0:T(8,128)(2,1)} %fusion.3.place_ref, bf16[4096,2048]{1,0:T(8,128)(2,1)} %all-gather.5.cloned.1.call-done.rows_ref), custom_call_target="tpu_custom_call" | custom-call | flops 2147483648 | bytes 33554432 | tf_op jit(solution)/shard_map/select_rows/pallas_call | solution.py:1225
  421.6 80.8 %run_experts.1 = (bf16[8,512,2048]{2,1,0:T(8,128)(2,1)}, bf16[8,512,2048]{2,1,0:T(8,128)(2,1)}, f32[8,352,2048]{2,1,0:T(8,128)}, f32[8,352,2048]{2,1,0:T(8,128)}...) custom-call(bf16[8,512,2048]{2,1,0:T(8,128)(2,1)} %bitcast.163, bf16[8,512,2048]{2,1,0:T(8,128)(2,1)} %bitcast.164, ...), custom_call_target="tpu_custom_call" | custom-call | flops 53150220288 | bytes 170917888 | tf_op jit(solution)/shard_map/run_experts/pallas_call | solution.py:1294
  502.4 18.0 %combine_rows.2.refs_0_ = bf16[4096,2048]{1,0:T(8,128)(2,1)} custom-call(bf16[32,128,128]{2,1,0:T(8,128)(2,1)} %fusion.3.place_ref, bf16[8,32,16,2048]{3,2,1,0:T(8,128)(2,1)} %bitcast.161, bf16[4096,88]{1,0:T(8,128)(2,1)} %copy-done.8, bf16[88,2048]{1,0:T(8,128)(2,1)} %bitcast.176), custom_call_target="tpu_custom_call" | custom-call | flops 3623878656 | bytes 33554432 | tf_op jit(solution)/shard_map/combine_rows/pallas_call | solution.py:1333
  520.5 2.2 reduce
  522.9 1.6 select_reduce_fusion.refs_2_
  524.4 18.8 %combine_rows.3.refs_1_ = bf16[4096,2048]{1,0:T(8,128)(2,1)} custom-call(bf16[32,128,128]{2,1,0:T(8,128)(2,1)} %fusion.3.place_ref, bf16[8,32,16,2048]{3,2,1,0:T(8,128)(2,1)} %bitcast.162, bf16[4096,176]{1,0:T(8,128)(2,1)} %pad_maximum_fusion.1.extra_ref, bf16[176,2048]{1,0:T(8,128)(2,1)} %bitcast.171), custom_call_target="tpu_custom_call" | custom-call | flops 5100273664 | bytes 33554432 | tf_op jit(solution)/shard_map/combine_rows/pallas_call | solution.py:1333
  543.2 176.4 %scatter_3.1 = (f32[128,2048]{1,0:T(8,128)}, f32[128,2048]{1,0:T(8,128)}, f32[32,8,128]{2,1,0:T(8,128)}) custom-call(bf16[4096,2048]{1,0:T(8,128)(2,1)} %combine_rows.2.refs_0_, bf16[4096,2048]{1,0:T(8,128)(2,1)} %combine_rows.3.refs_1_, f32[32,8,128]{2,1,0:T(8,128)} %select_reduce_fusion.refs_2_), custom_call_target="tpu_custom_call" | custom-call | tf_op jit(solution)/shard_map/scatter_3/pallas_call | solution.py:471
  721.0 2.1 multiply_reduce_fusion
  723.1 1.8 fusion.53
  724.9 29.4 %mixed_gather_4.1 = (bf16[512,2048]{1,0:T(8,128)(2,1)}, bf16[32,128,64]{2,1,0:T(8,128)(2,1)}) custom-call(bf16[128,2048]{1,0:T(8,128)(2,1)} %get-tuple-element.74.refs_0_, bf16[128,64]{1,0:T(8,128)(2,1)} %copy-done.51), custom_call_target="tpu_custom_call" | custom-call | tf_op jit(solution)/shard_map/mixed_gather_4/pallas_call | solution.py:897
  754.3 3.8 fusion.22
  758.1 2.2 fusion.10
  760.3 1.8 multiply_convert_fusion
  765.5 2.6 convolution_convert_fusion.1
  768.2 3.8 fusion.59
  772.0 3.5 convolution_convert_fusion.refs_0_
  776.7 5.4 all-to-all-start.1
  782.3 9.7 %fusion.60 = f32[2048,64]{0,1:T(8,128)} fusion(bf16[4096,2048]{1,0:T(8,128)(2,1)} %get-tuple-element.48.rows_ref, bf16[4096,64]{1,0:T(8,128)(2,1)S(1)} %bitcast.180), kind=kOutput, calls=%fused_computation.165 | convolution fusion | flops 1073741824 | bytes 17825792 | tf_op jit(solution)/shard_map/dot_general | solution.py:27
  792.1 1.1 copy-done.74
  793.2 1.5 convolution_convert_fusion.10
  794.8 1.8 convolution_convert_fusion.6.refs_2_
  796.6 34.0 %all-reduce.6.cloned.1.call-done = (bf16[512,512]{0,1:T(8,128)(2,1)}, bf16[512,64]{0,1:T(8,128)(2,1)}) async-done(((bf16[512,512]{0,1:T(8,128)(2,1)}, bf16[512,64]{0,1:T(8,128)(2,1)}), (bf16[512,512]{0,1:T(8,128)(2,1)}, bf16[512,64]{0,1:T(8,128)(2,1)})) %all-reduce.6.cloned.1.call-update) | async-done | bytes 589840 | tf_op jit(solution)/shard_map/psum | solution.py:1587
  830.6 2.3 convert_element_type.172
  832.8 1.4 multiply_reduce_fusion.1
  835.5 1.3 copy-done.14
  836.8 3.5 add_convert_fusion.refs_3_
  840.3 1.7 pad_maximum_fusion.refs_1_
  842.0 85.9 %mixed_total_7.1 = (f32[256,768]{1,0:T(8,128)}, f32[656,256]{1,0:T(8,128)}, f32[64,1024]{1,0:T(8,128)}, f32[128,2048]{1,0:T(8,128)}) custom-call(bf16[2048,768]{1,0:T(8,128)(2,1)} %convolution_convert_fusion.refs_0_, bf16[656,2048]{1,0:T(8,128)(2,1)} %pad_maximum_fusion.refs_1_, bf16[512,1024]{1,0:T(8,128)(2,1)} %convolution_convert_fusion.6.refs_2_, ...), custom_call_target="tpu_custom_call" | custom-call | tf_op jit(solution)/shard_map/mixed_total_7/pallas_call | solution.py:1133
  927.9 1.6 slice.245.refs_0_
  929.5 1.9 slice.150
  931.4 1.3 fusion.34
  933.6 19.8 %mixed_gather_5.1 = (bf16[576,256]{1,0:T(8,128)(2,1)}, f32[32,40,128]{2,1,0:T(8,128)}) custom-call(bf16[144,256]{1,0:T(8,128)(2,1)} %slice.245.refs_0_, f32[40,128]{1,0:T(8,128)} %pad.13.refs_1_), custom_call_target="tpu_custom_call" | custom-call | tf_op jit(solution)/shard_map/mixed_gather_5/pallas_call | solution.py:897
  953.5 1.1 reduce_sum.219
  955.8 1.8 convert_bitcast_fusion.1
  957.6 1.4 fusion.18
  959.0 1.4 convert_bitcast_fusion
  960.5 1.4 fusion.54
  (241 shorter events, 27.2 us)
Async XLA Ops:
  7.2 2.6 copy-start
  7.2 108.1 %all-gather.3.cloned.1.call-start = ((), (), s32[]{:S(2)}) async-start(), calls=%async_computation.2 | async-start | bytes 1474560 | tf_op jit(solution)/shard_map/all_gather | solution.py:1448
  9.1 82.7 %copy-start.66 = (f32[128]{0:T(128)}, f32[128]{0:T(128)S(1)}, u32[]{:S(2)}) copy-start(f32[128]{0:T(128)S(1)} %get-tuple-element.102) | copy-start | bytes 1540
  91.8 3.4 copy-start.16
  95.2 136.5 %all-gather.5.cloned.1.call-start = ((), (), s32[]{:S(2)}) async-start(), calls=%async_computation.3 | async-start | bytes 17301504 | tf_op jit(solution)/shard_map/all_gather | solution.py:87
  97.6 33.6 %all-to-all-start = ((bf16[8,264,256]{2,1,0:T(8,128)(2,1)}), bf16[8,264,256]{2,1,0:T(8,128)(2,1)S(1)}, u32[]{:S(2)}, u32[]{:S(2)}) async-start(bf16[8,264,256]{2,1,0:T(8,128)(2,1)} %bitcast.27), calls=%async_computation | async-start | bytes 2162688 | tf_op jit(solution)/shard_map/all_to_all | solution.py:1432
  105.2 5.7 copy-start.53
  109.6 3.3 copy-start.62
  110.8 15.0 %copy-start.22 = (bf16[512,4,128]{0,2,1:T(8,128)(2,1)}, bf16[512,4,128]{0,2,1:T(8,128)(2,1)S(1)}, u32[]{:S(2)}) copy-start(bf16[512,4,128]{0,2,1:T(8,128)(2,1)S(1)} %slice.244) | copy-start | bytes 1572868
  111.2 7.1 copy-start.58
  112.5 12.9 %copy-start.68 = (f32[32]{0:T(128)}, f32[32]{0:T(128)S(1)}, u32[]{:S(2)}) copy-start(f32[32]{0:T(128)S(1)} %multiply_power_fusion) | copy-start | bytes 388
  113.1 15.7 %copy-start.35 = (pred[512,512]{0,1:T(8,128)(4,1)}, pred[512,512]{0,1:T(8,128)(4,1)S(1)}, u32[]{:S(2)}) copy-start(pred[512,512]{0,1:T(8,128)(4,1)S(1)} %fusion.23) | copy-start | bytes 786436
  115.3 10.6 %copy-start.44 = (bf16[512,4,32]{0,2,1:T(8,128)(2,1)}, bf16[512,4,32]{0,2,1:T(8,128)(2,1)S(1)}, u32[]{:S(2)}) copy-start(bf16[512,4,32]{0,2,1:T(8,128)(2,1)S(1)} %get-tuple-element.86) | copy-start | bytes 393220
  115.3 3.0 copy-start.4
  118.3 6.4 copy-start.60
  124.7 3.1 copy-start.24
  125.8 2.1 copy-start.33
  131.3 100.4 %copy-start.75 = (bf16[4,128,512]{2,1,0:T(8,128)(2,1)}, bf16[4,128,512]{2,1,0:T(8,128)(2,1)S(1)}, u32[]{:S(2)}) copy-start(bf16[4,128,512]{2,1,0:T(8,128)(2,1)S(1)} %convolution_convert_fusion.9) | copy-start | bytes 1572868
  235.9 28.6 %copy-start.6 = (bf16[1,128,2048]{2,1,0:T(8,128)(2,1)S(1)}, bf16[1,128,2048]{2,1,0:T(8,128)(2,1)}, u32[]{:S(2)}) copy-start(bf16[1,128,2048]{2,1,0:T(8,128)(2,1)} %param.18) | copy-start | bytes 1572868
  264.5 2.5 copy-start.55
  264.5 2.6 copy-start.31
  266.0 81.5 %copy-start.19 = (bf16[8,22,8,256]{3,2,0,1:T(8,128)(2,1)S(1)}, bf16[8,22,8,256]{3,2,0,1:T(8,128)(2,1)}, u32[]{:S(2)}) copy-start(bf16[8,22,8,256]{3,2,0,1:T(8,128)(2,1)} %copy.150) | copy-start | bytes 2162692
  347.5 10.2 %copy-start.29 = (bf16[8,11,8,256]{3,2,0,1:T(8,128)(2,1)S(1)}, bf16[8,11,8,256]{3,2,0,1:T(8,128)(2,1)}, u32[]{:S(2)}) copy-start(bf16[8,11,8,256]{3,2,0,1:T(8,128)(2,1)} %copy.151) | copy-start | bytes 1081348
  357.7 13.0 %slice-start = ((s8[16777216]{0:T(1024)(128)(4,1)}), s8[4194304]{0:T(1024)(128)(4,1)S(1)}, s32[]{:S(2)}) async-start(s8[16777216]{0:T(1024)(128)(4,1)} %bitcast.159), calls=%async_computation.5 | async-start | bytes 8388608
  357.7 13.0 %slice-start.1 = ((s8[16777216]{0:T(1024)(128)(4,1)}), s8[4194304]{0:T(1024)(128)(4,1)S(1)}, s32[]{:S(2)}) async-start(s8[16777216]{0:T(1024)(128)(4,1)} %bitcast.159), calls=%async_computation.6 | async-start | bytes 8388608
  357.7 13.0 %slice-start.2 = ((s8[16777216]{0:T(1024)(128)(4,1)}), s8[4194304]{0:T(1024)(128)(4,1)S(1)}, s32[]{:S(2)}) async-start(s8[16777216]{0:T(1024)(128)(4,1)} %bitcast.159), calls=%async_computation.7 | async-start | bytes 8388608
  357.7 13.0 %slice-start.3 = ((s8[16777216]{0:T(1024)(128)(4,1)}), s8[4194304]{0:T(1024)(128)(4,1)S(1)}, s32[]{:S(2)}) async-start(s8[16777216]{0:T(1024)(128)(4,1)} %bitcast.159), calls=%async_computation.8 | async-start | bytes 8388608
  370.6 6.5 copy-start.8
  377.1 8.7 copy-start.54
  543.2 177.8 %copy-start.32 = (bf16[2048,64]{0,1:T(8,128)(2,1)S(1)}, bf16[2048,64]{0,1:T(8,128)(2,1)}, u32[]{:S(2)}) copy-start(bf16[2048,64]{0,1:T(8,128)(2,1)} %param.28) | copy-start | bytes 786436
  719.6 3.5 copy-start.3
  719.6 3.5 copy-start.17
  720.9 3.9 copy-start.51
  721.0 2.2 copy-start.37
  754.3 3.8 copy-start.13
  754.3 3.8 copy-start.36
  754.3 3.8 copy-start.64
  758.1 2.2 copy-start.21
  765.4 2.7 copy-start.72
  768.2 3.8 copy-start.26
  772.0 3.5 copy-start.18
  775.6 6.7 copy-start.30
  776.7 182.4 %all-to-all-start.1 = ((bf16[8,264,256]{2,1,0:T(8,128)(2,1)}), bf16[8,264,256]{2,1,0:T(8,128)(2,1)}, u32[]{:S(2)}, u32[]{:S(2)}) async-start(bf16[8,264,256]{2,1,0:T(8,128)(2,1)} %maximum_bitcast_fusion), calls=%async_computation.1 | async-start | bytes 2162688 | tf_op jit(solution)/shard_map/all_to_all | solution.py:1521
  782.1 48.5 %all-reduce.6.cloned.1.call-start = ((), (), s32[]{:S(2)}) async-start(), calls=%async_computation.4 | async-start | bytes 1179648 | tf_op jit(solution)/shard_map/psum | solution.py:1587
  782.3 9.7 %copy-start.47 = (bf16[512,4,128]{0,2,1:T(8,128)(2,1)S(1)}, bf16[512,4,128]{0,2,1:T(8,128)(2,1)}, u32[]{:S(2)}) copy-start(bf16[512,4,128]{0,2,1:T(8,128)(2,1)} %fusion.10) | copy-start | bytes 1572868
  792.1 2.7 copy-start.5
  792.1 2.7 copy-start.59
  792.1 2.7 copy-start.61
  796.5 37.7 %copy-start.69 = (f32[32]{0:T(128)S(1)}, f32[32]{0:T(128)}, u32[]{:S(2)}) copy-start(f32[32]{0:T(128)} %copy-done.68) | copy-start | bytes 388
  796.5 38.1 %copy-start.65 = (f32[512]{0:T(512)S(1)}, f32[512]{0:T(512)}, u32[]{:S(2)}) copy-start(f32[512]{0:T(512)} %get-tuple-element.99) | copy-start | bytes 6148
  830.6 3.7 copy-start.57
  830.6 4.1 copy-start.9
  832.8 2.1 copy-start.27
  834.6 2.2 copy-start.14
  836.8 3.5 copy-start.28
  842.0 89.4 %copy-start.71 = (f32[128]{0:T(128)S(1)}, f32[128]{0:T(128)}, u32[]{:S(2)}) copy-start(f32[128]{0:T(128)} %dynamic-slice) | copy-start | bytes 1540
  842.0 90.7 %copy-start.7 = (bf16[1,128,2048]{2,1,0:T(8,128)(2,1)S(1)}, bf16[1,128,2048]{2,1,0:T(8,128)(2,1)}, u32[]{:S(2)}) copy-start(bf16[1,128,2048]{2,1,0:T(8,128)(2,1)} %param.18) | copy-start | bytes 1572868
  842.0 90.7 %copy-start.56 = (f32[2048]{0:T(1024)S(1)}, f32[2048]{0:T(1024)}, u32[]{:S(2)}) copy-start(f32[2048]{0:T(1024)} %param.21) | copy-start | bytes 24580
  842.0 90.7 %copy-start.67 = (f32[128]{0:T(128)S(1)}, f32[128]{0:T(128)}, u32[]{:S(2)}) copy-start(f32[128]{0:T(128)} %copy-done.66) | copy-start | bytes 1540
  927.9 4.8 copy-start.11
  931.4 26.2 %copy-start.15 = (f32[128,2048]{1,0:T(8,128)S(1)}, f32[128,2048]{1,0:T(8,128)}, u32[]{:S(2)}) copy-start(f32[128,2048]{1,0:T(8,128)} %get-tuple-element.75) | copy-start | bytes 3145732
  931.4 26.2 %copy-start.70 = (f32[128]{0:T(128)S(1)}, f32[128]{0:T(128)}, u32[]{:S(2)}) copy-start(f32[128]{0:T(128)} %get-tuple-element.101) | copy-start | bytes 1540
  960.5 2.4 copy-start.52
  960.5 3.1 copy-start.1
  (22 other events, 29.7 us)
Sparse Core Ops, SparseCore 0:
  95.3 19.0 all-gather.2
  117.9 113.7 all-gather.4
  794.9 35.6 all-reduce.5

commit v3 on v2

--- a/solution.py
+++ b/solution.py
@@ -199,17 +199,22 @@
 
 
 def scatter_body(lines, count, small, *refs):
-    bigs, refs = refs[:count], refs[count:]
+    place_ref, refs = refs[0], refs[1:]
+    slots, extras, weights = refs[:count], refs[count : 2 * count], refs[2 * count : 3 * count]
+    refs = refs[3 * count :]
     if small:
         small_ref, refs = refs[0], refs[1:]
     outs, refs = refs[:count], refs[count:]
     if small:
         small_out, refs = refs[0], refs[1:]
     own, core_in, wide_in, side_in, up_in, down_in = refs[:6]
-    load_sem, core_send, core_recv, wide_send, wide_recv, side_send, side_recv = refs[6:13]
-    up_send, up_recv, down_send, down_recv = refs[13:17]
+    slot_in, staged, slot_sem, credit = refs[6:10]
+    core_send, core_recv, wide_send, wide_recv, side_send, side_recv = refs[10:16]
+    up_send, up_recv, down_send, down_recv = refs[16:20]
+    refs = refs[3:]
     wide, core, line, side = places()
-    tokens = own.shape[1]
+    tokens, width = own.shape[1:]
+    ring, core_ring = slot_in.shape[0], core_in.shape[0]
     half = tokens // 2
     core_mate = to_place(wide, 1 - core, line, side)
     wide_mate = to_place(1 - wide, core, line, side)
@@ -233,20 +238,34 @@
     def at(a, l, s, w):
         return ((a * lines + l) * 2 + s) * 2 + w
 
-    def core_copy(a, i):
-        n = a * 4 * lines + i
+    items = [(a, l) for a in range(count) for l in line_order(lines)]
+    blocks = []
+    for a, l in items:
+        blocks += [(a, 2 * (l * 4 + j) + 1 - core) for j in range(4)]
+        blocks += [(a, 2 * (l * 4 + j) + core) for j in range(4)]
+
+    def slot_copy(q):
+        a, b = blocks[q]
+        return pltpu.make_async_copy(
+            slots[a].at[:, b], slot_in.at[q % ring], slot_sem.at[q % ring]
+        )
+
+    def summed(q):
+        if q + ring - 1 < len(blocks):
+            slot_copy(q + ring - 1).start()
+        slot_copy(q).wait()
+        a, b = blocks[q]
+        rows = pl.ds(pl.multiple_of(b * tokens, tokens), tokens)
+        total = inner_rows(place_ref[b], slot_in[q % ring].reshape(-1, width))
+        return (total + matmul(extras[a][rows, :], weights[a][...])).astype(BF16)
+
+    def core_copy(n):
         return remote(
-            bigs[a].at[pl.ds((2 * i + 1 - core) * tokens, tokens)],
-            core_in.at[n],
+            staged.at[n % ring],
+            core_in.at[n % core_ring],
             core_send.at[n],
             core_recv.at[n],
             core_mate,
-        )
-
-    def load(a, i):
-        n = a * 4 * lines + i
-        return pltpu.make_async_copy(
-            bigs[a].at[pl.ds((2 * i + core) * tokens, tokens)], own.at[n], load_sem.at[n]
         )
 
     def wide_one(a, l, s):
@@ -312,21 +331,32 @@
     def add(i, rows, other):
         own[i, rows] = (own[i, rows].astype(F32) + other[...].astype(F32)).astype(BF16)
 
-    items = [(a, l) for a in range(count) for l in line_order(lines)]
-    for a, l in items:
-        for j in range(4):
-            core_copy(a, l * 4 + j).start()
-            load(a, l * 4 + j).start()
+    for q in range(ring - 1):
+        slot_copy(q).start()
     if small:
         small_start, small_finish = small_exchange(small_ref, small_out, *refs[17:19], True)
         small_start()
 
-    def stage_one(a, l):
+    def stage_one(t):
+        a, l = items[t]
         for j in range(4):
-            i = l * 4 + j
-            load(a, i).wait()
-            core_copy(a, i).wait_recv()
-            add(a * 4 * lines + i, pl.ds(0, tokens), core_in.at[a * 4 * lines + i])
+            n = t * 4 + j
+            if n >= ring:
+                core_copy(n - ring).wait_send()
+            staged[n % ring] = summed(t * 8 + j)
+            if n >= core_ring:
+                pl.semaphore_wait(credit, 1)
+            core_copy(n).start()
+        for j in range(4):
+            own[a * 4 * lines + l * 4 + j] = summed(t * 8 + 4 + j)
+        for j in range(4):
+            n = t * 4 + j
+            core_copy(n).wait_recv()
+            add(a * 4 * lines + l * 4 + j, pl.ds(0, tokens), core_in.at[n % core_ring])
+            if n + core_ring < 4 * len(items):
+                pl.semaphore_signal(
+                    credit, inc=1, device_id=core_mate, device_id_type=MESH_ID
+                )
         for j in range(2):
             wide_one(a, l, j).start()
             side_one(a, l, j).start()
@@ -413,7 +443,7 @@
         passes.setdefault(a * lines + lines + 3, []).append(functools.partial(final, a))
     for step in range(len(items) + 4):
         if step < len(items):
-            stage_one(*items[step])
+            stage_one(step)
         if 0 <= step - 1 < len(items):
             stage_two(*items[step - 1])
         if 0 <= step - 2 < len(items):
@@ -422,9 +452,9 @@
             action()
     if small:
         small_finish()
+    for n in range(4 * len(items) - ring, 4 * len(items)):
+        core_copy(n).wait_send()
     for a, l in items:
-        for j in range(4):
-            core_copy(a, l * 4 + j).wait_send()
         for j in range(2):
             wide_one(a, l, j).wait_send()
             side_one(a, l, j).wait_send()
@@ -441,28 +471,36 @@
                 down_copy(a, l, h).wait_send()
 
 
-def kernel_total(partials, small_value, number):
+def kernel_total(place, partials, small_value, number):
     n_row, n_col = lax.axis_size("row"), lax.axis_size("col")
     lines, count = n_col // 2, len(partials)
-    width = partials[0].shape[1]
-    tokens = partials[0].shape[0] // (n_row * n_col)
+    blocks, _, tokens = place.shape
+    local_experts, rows, width = partials[0][0].shape
+    capacity = rows // blocks
     small = small_value is not None
     out_shape = [jax.ShapeDtypeStruct((tokens, width), F32)] * count
-    in_specs = [pl.BlockSpec(memory_space=pl.ANY)] * count
-    operands = list(partials)
+    hbm, vmem = pl.BlockSpec(memory_space=pl.ANY), pl.BlockSpec(memory_space=pltpu.VMEM)
+    in_specs = [vmem] + [hbm] * count + [vmem] * (2 * count)
+    operands = [place]
+    operands += [p[0].reshape(local_experts, blocks, capacity, width) for p in partials]
+    operands += [p[1] for p in partials] + [p[2] for p in partials]
     if small:
-        in_specs.append(pl.BlockSpec(memory_space=pltpu.VMEM))
+        in_specs.append(vmem)
         out_shape.append(jax.ShapeDtypeStruct(small_value.shape, small_value.dtype))
         operands.append(small_value)
     dma = pltpu.SemaphoreType.DMA
     scratch = [
         pltpu.VMEM((count * 4 * lines, tokens, width), BF16),
-        pltpu.VMEM((count * 4 * lines, tokens, width), BF16),
+        pltpu.VMEM((8, tokens, width), BF16),
         pltpu.VMEM((count * 3 * lines, tokens // 2, width), BF16),
         pltpu.VMEM((count * 3 * lines, tokens // 2, width), BF16),
         pltpu.VMEM((count * 2 * lines, tokens // 2, width), BF16),
         pltpu.VMEM((count * 2 * lines, tokens // 2, width), BF16),
-        *[dma((count * 4 * lines,))] * 3,
+        pltpu.VMEM((4, local_experts, capacity, width), BF16),
+        pltpu.VMEM((4, tokens, width), BF16),
+        dma((4,)),
+        pltpu.SemaphoreType.REGULAR,
+        *[dma((count * 4 * lines,))] * 2,
         *[dma((count * 3 * lines,))] * 4,
         *[dma((count * 2 * lines,))] * 4,
     ]
@@ -481,35 +519,167 @@
     )(*operands)
 
 
-def gather_body(lines, small, *refs):
-    own_ref, refs = refs[0], refs[1:]
-    if small:
-        small_ref, refs = refs[0], refs[1:]
-    out_ref, refs = refs[0], refs[1:]
-    if small:
-        small_out, refs = refs[0], refs[1:]
-    local_sem, core_send, core_recv, wide_send, wide_recv, side_send, side_recv = refs[:7]
-    up_send, up_recv, down_send, down_recv = refs[7:11]
-    wide, core, line, side = places()
-    tokens = own_ref.shape[0]
-    half = tokens // 2
-    core_mate = to_place(wide, 1 - core, line, side)
-    wide_mate = to_place(1 - wide, core, line, side)
+def kernel_fits(rows, width, count):
+    n_row, n_col = lax.axis_size("row"), lax.axis_size("col")
+    tokens = rows // (n_row * n_col)
+    held = count * n_col * 2 * width * tokens * 13 // 4
+    return n_row == 4 and n_col % 2 == 0 and tokens % 32 == 0 and held < 58 * 1024 * 1024
+
+
+def row_mates(wide, core, line, side):
+    return to_place(wide, 1 - core, line, side), to_place(1 - wide, core, line, side)
+
+
+def strip(ref, dim, index, size):
+    start = pl.multiple_of(index * size, size)
+    return ref.at[pl.ds(start, size)] if dim == 0 else ref.at[:, pl.ds(start, size)]
+
+
+def cols_plan(lines, dims, flips, spots, cols, outs, sems):
+    wide, core, line, side = spots
     side_mate = to_place(wide, core, line, 1 - side)
     above = to_place(wide, core, line + 1, side)
     below = to_place(wide, core, line - 1, side)
-    has_above = line < lines - 1
-    has_below = line > 0
-    greet(
-        [
-            (core >= 0, core_mate),
-            (core >= 0, wide_mate),
-            (core >= 0, side_mate),
-            (has_above, above),
-            (has_below, below),
-        ],
-        small,
-    )
+    has_above, has_below = line < lines - 1, line > 0
+    local_sem, side_send, side_recv, up_send, up_recv, down_send, down_recv = sems
+    count = len(dims)
+
+    def spot(m, l, s):
+        return strip(outs[m], dims[m], l * 2 + s, cols[m].shape[dims[m]])
+
+    def line_copy(m, l, s, up, here=False):
+        n = (m * lines + l) * 2 + s
+        return remote(
+            cols[m] if here else spot(m, l, s),
+            spot(m, l, s),
+            (up_send if up else down_send).at[n],
+            (up_recv if up else down_recv).at[n],
+            above if up else below,
+        )
+
+    def side_copy(m, l, here=False):
+        n = m * lines + l
+        return remote(
+            cols[m] if here else spot(m, l, side),
+            spot(m, l, side),
+            side_send.at[n],
+            side_recv.at[n],
+            side_mate,
+        )
+
+    def to_line(m, s, here):
+        @pl.when(has_above)
+        def _():
+            line_copy(m, line, s, True, here).start()
+
+        @pl.when(has_below)
+        def _():
+            line_copy(m, line, s, False, here).start()
+
+    def local(m):
+        return pltpu.make_async_copy(cols[m], spot(m, line, side), local_sem.at[m])
+
+    def start():
+        for m in range(count):
+            to_line(m, side, True)
+            side_copy(m, line, True).start()
+        for m in range(count):
+            local(m).start()
+
+    def from_line(m, dist, up):
+        l = line - dist if up else line + dist
+
+        @pl.when(l >= 0 if up else l < lines)
+        def _():
+            for s in (side, 1 - side) if flips[m] else (side,):
+                line_copy(m, l, s, up).wait_recv()
+
+                @pl.when(has_above if up else has_below)
+                def _(s=s):
+                    line_copy(m, l, s, up).start()
+
+            if not flips[m]:
+                side_copy(m, l).start()
+
+    def step(dist):
+        if dist == 1:
+            for m in range(count):
+                if flips[m]:
+                    side_copy(m, line).wait_recv()
+                    to_line(m, 1 - side, False)
+        if dist < lines:
+            for m in range(count):
+                from_line(m, dist, True)
+                from_line(m, dist, False)
+
+    def finish():
+        for m in range(count):
+            local(m).wait()
+            if flips[m]:
+                side_copy(m, line).wait_send()
+            for l in range(lines):
+                if not flips[m]:
+                    side_copy(m, l).wait()
+                for s in range(2) if flips[m] else (side,):
+
+                    @pl.when(jnp.logical_and(has_above, line >= l))
+                    def _(m=m, l=l, s=s):
+                        line_copy(m, l, s, True).wait_send()
+
+                    @pl.when(jnp.logical_and(has_below, line <= l))
+                    def _(m=m, l=l, s=s):
+                        line_copy(m, l, s, False).wait_send()
+
+    return start, step, finish
+
+
+def row_plan(spots, row_ref, out_ref, sems):
+    wide, core, line, side = spots
+    core_mate, wide_mate = row_mates(wide, core, line, side)
+    local_sem, core_send, core_recv, wide_send, wide_recv = sems
+    tokens = row_ref.shape[0]
+
+    def spot(w, k):
+        return strip(out_ref, 0, w * 2 + k, tokens)
+
+    def core_copy(n):
+        src = row_ref if n == 0 else spot(1 - wide, core)
+        dst = spot(wide if n == 0 else 1 - wide, core)
+        return remote(src, dst, core_send.at[n], core_recv.at[n], core_mate)
+
+    wide_copy = remote(row_ref, spot(wide, core), wide_send.at[0], wide_recv.at[0], wide_mate)
+    local = pltpu.make_async_copy(row_ref, spot(wide, core), local_sem.at[0])
+
+    def start():
+        wide_copy.start()
+        core_copy(0).start()
+        local.start()
+
+    def step(dist):
+        if dist == 1:
+            wide_copy.wait_recv()
+            core_copy(1).start()
+
+    def finish():
+        local.wait()
+        wide_copy.wait_send()
+        for n in range(2):
+            core_copy(n).wait()
+
+    return start, step, finish
+
+
+def every_plan(lines, ways, spots, own_ref, out_ref, sems):
+    wide, core, line, side = spots
+    core_mate, wide_mate = row_mates(wide, core, line, side)
+    side_mate = to_place(wide, core, line, 1 - side)
+    above = to_place(wide, core, line + 1, side)
+    below = to_place(wide, core, line - 1, side)
+    has_above, has_below = line < lines - 1, line > 0
+    local_sem, core_send, core_recv, wide_send, wide_recv, side_send, side_recv = sems[:7]
+    up_send, up_recv, down_send, down_recv = sems[7:]
+    tokens = own_ref.shape[0]
+    half = tokens // 2
 
     def spot(l, s, w, k, h):
         return out_ref.at[pl.ds((((l * 2 + s) * 2 + w) * 2 + k) * tokens + h * half, half)]
@@ -528,7 +698,7 @@
         )
 
     def wide_copy(l, s, h, here=False):
-        n = l * 3 + (2 if h else s)
+        n = (l * 2 + h) * 2 + (0 if ways[h] else s)
         return remote(
             source(l, s, wide, h, here),
             spot(l, s, wide, core, h),
@@ -538,7 +708,7 @@
         )
 
     def side_copy(l, w, h, here=False):
-        n = l * 3 + (w if h else 2)
+        n = (l * 2 + h) * 2 + (w if ways[h] else 0)
         return remote(
             source(l, side, w, h, here),
             spot(l, side, w, core, h),
@@ -547,24 +717,14 @@
             side_mate,
         )
 
-    def up_copy(l, h, here=False):
+    def line_copy(l, h, up, here=False):
         n = l * 2 + h
         return remote(
             source(l, side, wide, h, here),
             spot(l, side, wide, core, h),
-            up_send.at[n],
-            up_recv.at[n],
-            above,
-        )
-
-    def down_copy(l, h, here=False):
-        n = l * 2 + h
-        return remote(
-            source(l, side, wide, h, here),
-            spot(l, side, wide, core, h),
-            down_send.at[n],
-            down_recv.at[n],
-            below,
+            (up_send if up else down_send).at[n],
+            (up_recv if up else down_recv).at[n],
+            above if up else below,
         )
 
     def local(h):
@@ -573,62 +733,63 @@
         )
 
     def spread(l, h, here=False):
-        if h == 0:
-            side_copy(l, wide, 0, here).start()
-            wide_copy(l, side, 0, here).start()
+        if ways[h]:
+            wide_copy(l, side, h, here).start()
+            side_copy(l, wide, h, here).start()
         else:
-            wide_copy(l, side, 1, here).start()
-            side_copy(l, wide, 1, here).start()
+            side_copy(l, wide, h, here).start()
+            wide_copy(l, side, h, here).start()
         core_copy(l, side, wide, h, here).start()
 
     def second(l):
-        side_copy(l, wide, 0).wait_recv()
-        wide_copy(l, 1 - side, 0).start()
-        core_copy(l, 1 - side, wide, 0).start()
-        wide_copy(l, side, 1).wait_recv()
-        side_copy(l, 1 - wide, 1).start()
-        core_copy(l, side, 1 - wide, 1).start()
+        for h in range(2):
+            if ways[h]:
+                wide_copy(l, side, h).wait_recv()
+                side_copy(l, 1 - wide, h).start()
+                core_copy(l, side, 1 - wide, h).start()
+            else:
+                side_copy(l, wide, h).wait_recv()
+                wide_copy(l, 1 - side, h).start()
+                core_copy(l, 1 - side, wide, h).start()
 
     def third(l):
         for j in range(2):
-            s = 1 - side if j else side
-            wide_copy(l, s, 0).wait_recv()
-            core_copy(l, s, 1 - wide, 0).start()
-            w = 1 - wide if j else wide
-            side_copy(l, w, 1).wait_recv()
-            core_copy(l, 1 - side, w, 1).start()
-
-    for h in range(2):
-
-        @pl.when(has_above)
-        def _(h=h):
-            up_copy(line, h, True).start()
-
-        @pl.when(has_below)
-        def _(h=h):
-            down_copy(line, h, True).start()
-
-        spread(line, h, True)
-    if small:
-        small_start, small_finish = small_exchange(small_ref, small_out, *refs[11:13], False)
-        small_start()
-    for h in range(2):
-        local(h).start()
+            for h in range(2):
+                if ways[h]:
+                    w = 1 - wide if j else wide
+                    side_copy(l, w, h).wait_recv()
+                    core_copy(l, 1 - side, w, h).start()
+                else:
+                    s = 1 - side if j else side
+                    wide_copy(l, s, h).wait_recv()
+                    core_copy(l, s, 1 - wide, h).start()
+
+    def start():
+        for h in range(2):
+
+            @pl.when(has_above)
+            def _(h=h):
+                line_copy(line, h, True, True).start()
+
+            @pl.when(has_below)
+            def _(h=h):
+                line_copy(line, h, False, True).start()
+
+            spread(line, h, True)
+        for h in range(2):
+            local(h).start()
 
     def from_line(dist, up):
         l = line - dist if up else line + dist
-        there = l >= 0 if up else l < lines
-        further = has_above if up else has_below
-        copy = up_copy if up else down_copy
-
-        @pl.when(there)
+
+        @pl.when(l >= 0 if up else l < lines)
         def _():
             for h in range(2):
-                copy(l, h).wait_recv()
-
-                @pl.when(further)
+                line_copy(l, h, up).wait_recv()
+
+                @pl.when(has_above if up else has_below)
                 def _(h=h):
-                    copy(l, h).start()
+                    line_copy(l, h, up).start()
 
                 spread(l, h)
 
@@ -645,7 +806,7 @@
         def _():
             action(line + dist)
 
-    for dist in range(1, lines + 2):
+    def step(dist):
         if dist < lines:
             from_line(dist, True)
             from_line(dist, False)
@@ -653,255 +814,117 @@
             stage(second, dist - 1)
         if 0 <= dist - 2 < lines:
             stage(third, dist - 2)
-    if small:
+
+    def finish():
+        for h in range(2):
+            local(h).wait()
+        for l in range(lines):
+            for s in range(2):
+                for w in range(2):
+                    for h in range(2):
+                        core_copy(l, s, w, h).wait()
+            for h in range(2):
+                for j in range(1 if ways[h] else 2):
+                    wide_copy(l, side if ways[h] else j, h).wait_send()
+                for j in range(2 if ways[h] else 1):
+                    side_copy(l, j if ways[h] else wide, h).wait_send()
+
+                @pl.when(jnp.logical_and(has_above, line >= l))
+                def _(h=h, l=l):
+                    line_copy(l, h, True).wait_send()
+
+                @pl.when(jnp.logical_and(has_below, line <= l))
+                def _(h=h, l=l):
+                    line_copy(l, h, False).wait_send()
+
+    return start, step, finish
+
+
+def gather_body(lines, dims, flips, ways, kinds, *refs):
+    has_row, has_every, has_small = kinds
+    count = len(dims)
+    outputs = count + has_row + has_every + has_small
+    ins, outs, sems = refs[:outputs], refs[outputs : 2 * outputs], list(refs[2 * outputs :])
+    spots = places()
+    wide, core, line, side = spots
+    core_mate, wide_mate = row_mates(*spots)
+    partners = [(core >= 0, core_mate), (core >= 0, wide_mate)]
+    if count or has_every:
+        partners += [
+            (core >= 0, to_place(wide, core, line, 1 - side)),
+            (line < lines - 1, to_place(wide, core, line + 1, side)),
+            (line > 0, to_place(wide, core, line - 1, side)),
+        ]
+    greet(partners, has_small)
+
+    def take(n):
+        taken, sems[:] = sems[:n], sems[n:]
+        return taken
+
+    plans, at = [], count
+    if count:
+        plans.append(cols_plan(lines, dims, flips, spots, ins[:count], outs[:count], take(7)))
+    if has_row:
+        plans.append(row_plan(spots, ins[at], outs[at], take(5)))
+        at += 1
+    if has_every:
+        plans.append(every_plan(lines, ways, spots, ins[at], outs[at], take(11)))
+        at += 1
+    if has_small:
+        small_start, small_finish = small_exchange(ins[at], outs[at], *take(2), False)
+        small_start()
+    for start, _, _ in plans:
+        start()
+    for dist in range(1, lines + 2):
+        for _, step, _ in plans:
+            step(dist)
+    if has_small:
         small_finish()
-    for h in range(2):
-        local(h).wait()
-    for l in range(lines):
-        for s in range(2):
-            for w in range(2):
-                for h in range(2):
-                    core_copy(l, s, w, h).wait_recv()
-                    core_copy(l, s, w, h).wait_send()
-        for j in range(2):
-            wide_copy(l, j, 0).wait_send()
-            side_copy(l, j, 1).wait_send()
-        wide_copy(l, side, 1).wait_send()
-        side_copy(l, wide, 0).wait_send()
-        for h in range(2):
-
-            @pl.when(jnp.logical_and(has_above, line >= l))
-            def _(h=h):
-                up_copy(l, h).wait_send()
-
-            @pl.when(jnp.logical_and(has_below, line <= l))
-            def _(h=h):
-                down_copy(l, h).wait_send()
-
-
-def kernel_gather(own, small_value, number):
+    for _, _, finish in plans:
+        finish()
+
+
+def kernel_gather(col_values, dims, flips, row_value, every_value, ways, small_value, number):
     n_row, n_col = lax.axis_size("row"), lax.axis_size("col")
-    lines, total = n_col // 2, n_row * n_col
-    tokens, width = own.shape
-    small = small_value is not None
-    out_shape = [jax.ShapeDtypeStruct((total * tokens, width), own.dtype)]
-    in_specs = [pl.BlockSpec(memory_space=pltpu.VMEM)]
-    out_specs = [pl.BlockSpec(memory_space=pl.ANY)]
-    operands = [own]
-    if small:
-        in_specs.append(pl.BlockSpec(memory_space=pltpu.VMEM))
-        out_specs.append(pl.BlockSpec(memory_space=pltpu.VMEM))
+    lines, count, total = n_col // 2, len(dims), n_row * n_col
+    hbm, vmem = pl.BlockSpec(memory_space=pl.ANY), pl.BlockSpec(memory_space=pltpu.VMEM)
+    dma = pltpu.SemaphoreType.DMA
+    operands, in_specs, out_specs, out_shape = list(col_values), [hbm] * count, [hbm] * count, []
+    scratch = []
+    for value, dim in zip(col_values, dims):
+        shape = list(value.shape)
+        shape[dim] *= n_col
+        out_shape.append(jax.ShapeDtypeStruct(tuple(shape), value.dtype))
+    if count:
+        scratch += [dma((count,))] + [dma((count * lines,))] * 2
+        scratch += [dma((2 * count * lines,))] * 4
+    if row_value is not None:
+        scratch += [dma((1,)), dma((2,)), dma((2,)), dma((1,)), dma((1,))]
+    if every_value is not None:
+        scratch += [dma((2,)), *[dma((8 * lines,))] * 2, *[dma((4 * lines,))] * 4]
+        scratch += [dma((2 * lines,))] * 4
+    for value, times in ((row_value, n_row), (every_value, total)):
+        if value is not None:
+            operands.append(value)
+            in_specs.append(vmem)
+            out_specs.append(hbm)
+            shape = (times * value.shape[0], *value.shape[1:])
+            out_shape.append(jax.ShapeDtypeStruct(shape, value.dtype))
+    if small_value is not None:
+        operands.append(small_value)
+        in_specs.append(vmem)
+        out_specs.append(vmem)
         out_shape.append(jax.ShapeDtypeStruct((total, *small_value.shape), small_value.dtype))
-        operands.append(small_value)
-    dma = pltpu.SemaphoreType.DMA
-    scratch = [
-        dma((2,)),
-        *[dma((8 * lines,))] * 2,
-        *[dma((3 * lines,))] * 4,
-        *[dma((2 * lines,))] * 4,
-    ]
-    if small:
         scratch += [dma((total,))] * 2
+    kinds = tuple(value is not None for value in (row_value, every_value, small_value))
     return pl.pallas_call(
-        functools.partial(gather_body, lines, small),
+        functools.partial(gather_body, lines, tuple(dims), tuple(flips), ways, kinds),
         out_shape=out_shape,
         in_specs=in_specs,
         out_specs=out_specs,
         scratch_shapes=scratch,
         compiler_params=pltpu.CompilerParams(collective_id=number, has_side_effects=True),
         name=f"gather_{number}",
-    )(*operands)
-
-
-def kernel_fits(rows, width, count):
-    n_row, n_col = lax.axis_size("row"), lax.axis_size("col")
-    tokens = rows // (n_row * n_col)
-    held = count * n_col * 2 * width * tokens * 13 // 4
-    return n_row == 4 and n_col % 2 == 0 and tokens % 32 == 0 and held < 58 * 1024 * 1024
-
-
-def row_mates(wide, core, line, side):
-    return to_place(wide, 1 - core, line, side), to_place(1 - wide, core, line, side)
-
-
-def strip(ref, dim, index, size):
-    start = pl.multiple_of(index * size, size)
-    return ref.at[pl.ds(start, size)] if dim == 0 else ref.at[:, pl.ds(start, size)]
-
-
-def mixed_gather_body(lines, dims, flips, small, *refs):
-    count = len(dims)
-    cols, row_ref, refs = refs[:count], refs[count], refs[count + 1 :]
-    if small:
-        small_ref, refs = refs[0], refs[1:]
-    col_outs, row_out, refs = refs[:count], refs[count], refs[count + 1 :]
-    if small:
-        small_out, refs = refs[0], refs[1:]
-    local_sem, core_send, core_recv, wide_send, wide_recv = refs[:5]
-    refs = refs[5:]
-    if count:
-        side_send, side_recv, up_send, up_recv, down_send, down_recv = refs[:6]
-        refs = refs[6:]
-    wide, core, line, side = places()
-    core_mate, wide_mate = row_mates(wide, core, line, side)
-    side_mate = to_place(wide, core, line, 1 - side)
-    above = to_place(wide, core, line + 1, side)
-    below = to_place(wide, core, line - 1, side)
-    has_above = line < lines - 1
-    has_below = line > 0
-    partners = [(core >= 0, core_mate), (core >= 0, wide_mate)]
-    if count:
-        partners += [(core >= 0, side_mate), (has_above, above), (has_below, below)]
-    greet(partners, small)
-
-    def spot(m, l, s):
-        size = cols[m].shape[dims[m]]
-        return strip(col_outs[m], dims[m], l * 2 + s, size)
-
-    def line_copy(m, l, s, up, here=False):
-        n = (m * lines + l) * 2 + s
-        return remote(
-            cols[m] if here else spot(m, l, s),
-            spot(m, l, s),
-            (up_send if up else down_send).at[n],
-            (up_recv if up else down_recv).at[n],
-            above if up else below,
-        )
-
-    def side_copy(m, l, here=False):
-        n = m * lines + l
-        return remote(
-            cols[m] if here else spot(m, l, side),
-            spot(m, l, side),
-            side_send.at[n],
-            side_recv.at[n],
-            side_mate,
-        )
-
-    tokens = row_ref.shape[0]
-
-    def row_spot(w, k):
-        return strip(row_out, 0, w * 2 + k, tokens)
-
-    def core_copy(n):
-        src = row_ref if n == 0 else row_spot(1 - wide, core)
-        dst = row_spot(wide if n == 0 else 1 - wide, core)
-        return remote(src, dst, core_send.at[n], core_recv.at[n], core_mate)
-
-    def to_line(m, s, here):
-        @pl.when(has_above)
-        def _():
-            line_copy(m, line, s, True, here).start()
-
-        @pl.when(has_below)
-        def _():
-            line_copy(m, line, s, False, here).start()
-
-    wide_copy = remote(row_ref, row_spot(wide, core), wide_send.at[0], wide_recv.at[0], wide_mate)
-    wide_copy.start()
-    core_copy(0).start()
-    for m in range(count):
-
-        to_line(m, side, True)
-        side_copy(m, line, True).start()
-    if small:
-        small_start, small_finish = small_exchange(small_ref, small_out, *refs[:2], False)
-        small_start()
-    local = [pltpu.make_async_copy(row_ref, row_spot(wide, core), local_sem.at[count])]
-    for m in range(count):
-        local.append(pltpu.make_async_copy(cols[m], spot(m, line, side), local_sem.at[m]))
-    for copy in local:
-        copy.start()
-
-    def from_line(m, dist, up):
-        l = line - dist if up else line + dist
-
-        @pl.when(l >= 0 if up else l < lines)
-        def _():
-            for s in (side, 1 - side) if flips[m] else (side,):
-                line_copy(m, l, s, up).wait_recv()
-
-                @pl.when(has_above if up else has_below)
-                def _(s=s):
-                    line_copy(m, l, s, up).start()
-
-            if not flips[m]:
-                side_copy(m, l).start()
-
-    for m in range(count):
-        if flips[m]:
-            side_copy(m, line).wait_recv()
-            to_line(m, 1 - side, False)
-
-    def pass_on():
-        wide_copy.wait_recv()
-        core_copy(1).start()
-
-    if lines == 1 or not count:
-        pass_on()
-    for dist in range(1, lines if count else 1):
-        for m in range(count):
-            from_line(m, dist, True)
-            from_line(m, dist, False)
-        if dist == 1:
-            pass_on()
-    if small:
-        small_finish()
-    for copy in local:
-        copy.wait()
-    wide_copy.wait_send()
-    for n in range(2):
-        core_copy(n).wait()
-    for m in range(count):
-        if flips[m]:
-            side_copy(m, line).wait_send()
-        for l in range(lines):
-            if not flips[m]:
-                side_copy(m, l).wait()
-            for s in range(2) if flips[m] else (side,):
-
-                @pl.when(jnp.logical_and(has_above, line >= l))
-                def _(m=m, l=l, s=s):
-                    line_copy(m, l, s, True).wait_send()
-
-                @pl.when(jnp.logical_and(has_below, line <= l))
-                def _(m=m, l=l, s=s):
-                    line_copy(m, l, s, False).wait_send()
-
-
-def mixed_gather(col_values, dims, flips, row_value, small_value, number):
-    n_row, n_col = lax.axis_size("row"), lax.axis_size("col")
-    lines, count, small = n_col // 2, len(dims), small_value is not None
-    tokens, width = row_value.shape
-    hbm, vmem = pl.BlockSpec(memory_space=pl.ANY), pl.BlockSpec(memory_space=pltpu.VMEM)
-    out_shape = []
-    for value, dim in zip(col_values, dims):
-        shape = list(value.shape)
-        shape[dim] *= n_col
-        out_shape.append(jax.ShapeDtypeStruct(tuple(shape), value.dtype))
-    out_shape.append(jax.ShapeDtypeStruct((n_row * tokens, width), row_value.dtype))
-    operands = [*col_values, row_value]
-    in_specs, out_specs = [hbm] * count + [vmem], [hbm] * (count + 1)
-    dma = pltpu.SemaphoreType.DMA
-    scratch = [dma((count + 1,)), dma((2,)), dma((2,)), dma((1,)), dma((1,))]
-    if count:
-        scratch += [dma((count * lines,))] * 2 + [dma((2 * count * lines,))] * 4
-    if small:
-        operands.append(small_value)
-        in_specs.append(vmem)
-        out_specs.append(vmem)
-        out_shape.append(
-            jax.ShapeDtypeStruct((n_row * n_col, *small_value.shape), small_value.dtype)
-        )
-        scratch += [dma((n_row * n_col,))] * 2
-    return pl.pallas_call(
-        functools.partial(mixed_gather_body, lines, tuple(dims), tuple(flips), small),
-        out_shape=out_shape,
-        in_specs=in_specs,
-        out_specs=out_specs,
-        scratch_shapes=scratch,
-        compiler_params=pltpu.CompilerParams(collective_id=number, has_side_effects=True),
-        name=f"mixed_gather_{number}",
     )(*operands)
 
 
@@ -1144,40 +1167,164 @@
     )(*col_values, row_value)
 
 
-def small_body(personal, value_ref, out_ref, send_sem, recv_sem):
-    greet([], True)
-    start, finish = small_exchange(value_ref, out_ref, send_sem, recv_sem, personal)
-    start()
-    finish()
-
-
-def kernel_small(value, personal, number):
-    total = lax.axis_size("row") * lax.axis_size("col")
-    shape = value.shape if personal else (total, *value.shape)
+def row_sum_body(value_ref, out_ref, held, core_in, wide_in, *sems):
+    one_send, one_recv, two_send, two_recv, core_send, core_recv, wide_send, wide_recv = sems
+    wide, core, line, side = places()
+    core_mate, wide_mate = row_mates(wide, core, line, side)
+    greet([(core >= 0, core_mate), (core >= 0, wide_mate)], False)
+    tokens = wide_in.shape[0]
+
+    def block(ref, w, k):
+        return strip(ref, 0, w * 2 + k, tokens)
+
+    ones = [
+        remote(block(value_ref, w, 1 - core), core_in.at[w], one_send.at[w], one_recv.at[w], core_mate)
+        for w in range(2)
+    ]
+    two = remote(held.at[1 - wide], wide_in, two_send.at[0], two_recv.at[0], wide_mate)
+    for copy in ones:
+        copy.start()
+    for w in range(2):
+        ones[w].wait_recv()
+        held[w] = (block(value_ref, w, core)[...].astype(F32) + core_in[w].astype(F32)).astype(BF16)
+    two.start()
+    two.wait_recv()
+    held[wide] = (held[wide].astype(F32) + wide_in[...].astype(F32)).astype(BF16)
+
+    def to_core(n):
+        w = wide if n == 0 else 1 - wide
+        src = held.at[wide] if n == 0 else block(out_ref, w, core)
+        return remote(src, block(out_ref, w, core), core_send.at[n], core_recv.at[n], core_mate)
+
+    to_wide = remote(
+        held.at[wide], block(out_ref, wide, core), wide_send.at[0], wide_recv.at[0], wide_mate
+    )
+    to_wide.start()
+    to_core(0).start()
+    block(out_ref, wide, core)[...] = held[wide]
+    to_wide.wait_recv()
+    to_core(1).start()
+    for n in range(2):
+        to_core(n).wait()
+    to_wide.wait_send()
+    two.wait_send()
+    for copy in ones:
+        copy.wait_send()
+
+
+def row_sum(value, number):
+    n_row = lax.axis_size("row")
+    if n_row != 4:
+        return lax.psum(value, "row")
+    tokens, width = value.shape[0] // n_row, value.shape[1]
     dma = pltpu.SemaphoreType.DMA
     return pl.pallas_call(
-        functools.partial(small_body, personal),
-        out_shape=jax.ShapeDtypeStruct(shape, value.dtype),
+        row_sum_body,
+        out_shape=jax.ShapeDtypeStruct(value.shape, value.dtype),
         in_specs=[pl.BlockSpec(memory_space=pltpu.VMEM)],
         out_specs=pl.BlockSpec(memory_space=pltpu.VMEM),
-        scratch_shapes=[dma((total,)), dma((total,))],
+        scratch_shapes=[
+            pltpu.VMEM((2, tokens, width), value.dtype),
+            pltpu.VMEM((2, tokens, width), value.dtype),
+            pltpu.VMEM((tokens, width), value.dtype),
+            dma((2,)),
+            dma((2,)),
+            dma((1,)),
+            dma((1,)),
+            dma((2,)),
+            dma((2,)),
+            dma((1,)),
+            dma((1,)),
+        ],
         compiler_params=pltpu.CompilerParams(collective_id=number, has_side_effects=True),
-        name=f"small_{number}",
+        name=f"row_sum_{number}",
     )(value)
 
 
-def gather_every(own, small_value, number):
-    total = lax.axis_size("row") * lax.axis_size("col")
-    if kernel_fits(total * own.shape[0], own.shape[1], 1):
-        return kernel_gather(own, small_value, number)
-    return every_token(own), every_token(small_value[None])
-
-
-def total_every(partials, small_value, number):
-    if kernel_fits(partials[0].shape[0], partials[0].shape[1], len(partials)):
-        return kernel_total(partials, small_value, number)
+def finish_body(value_ref, gains_ref, out_ref, sums_ref, row_in, held, *sems):
+    local_sem, value_send, value_recv, row_send, row_recv, col_send, col_recv = sems
+    n_row, n_col = lax.axis_size("row"), lax.axis_size("col")
+    row, col = lax.axis_index("row"), lax.axis_index("col")
+    rows = [{"row": lax.rem(row + d, n_row), "col": col} for d in range(1, n_row)]
+    cols = [{"row": row, "col": lax.rem(col + d, n_col)} for d in range(1, n_col)]
+    greet([(row >= 0, partner) for partner in rows + cols], False)
+    tokens = value_ref.shape[0]
+
+    def value_copy(d, source):
+        return remote(
+            value_ref,
+            strip(out_ref, 0, source, tokens),
+            value_send.at[d],
+            value_recv.at[source],
+            rows[d],
+        )
+
+    def row_copy(d, source):
+        return remote(gains_ref, row_in.at[source], row_send.at[d], row_recv.at[source], rows[d])
+
+    def col_copy(d, source):
+        return remote(held, sums_ref.at[source], col_send.at[d], col_recv.at[source], cols[d])
+
+    for d in range(n_row - 1):
+        row_copy(d, row).start()
+    for d in range(n_row - 1):
+        value_copy(d, row).start()
+    local = pltpu.make_async_copy(value_ref, strip(out_ref, 0, row, tokens), local_sem)
+    local.start()
+    total = gains_ref[...]
+    for d in range(n_row - 1):
+        source = rows[d]["row"]
+        row_copy(d, source).wait_recv()
+        total = total + row_in[source]
+    held[...] = total
+    for d in range(n_col - 1):
+        col_copy(d, col).start()
+    sums_ref[col] = total
+    for d in range(n_row - 1):
+        value_copy(d, rows[d]["row"]).wait_recv()
+        value_copy(d, row).wait_send()
+        row_copy(d, row).wait_send()
+    for d in range(n_col - 1):
+        col_copy(d, cols[d]["col"]).wait_recv()
+        col_copy(d, col).wait_send()
+    local.wait()
+
+
+def kernel_finish(value, gains, number):
+    n_row, n_col = lax.axis_size("row"), lax.axis_size("col")
+    dma = pltpu.SemaphoreType.DMA
+    vmem = pl.BlockSpec(memory_space=pltpu.VMEM)
+    return pl.pallas_call(
+        finish_body,
+        out_shape=[
+            jax.ShapeDtypeStruct((n_row * value.shape[0], value.shape[1]), value.dtype),
+            jax.ShapeDtypeStruct((n_col, *gains.shape), gains.dtype),
+        ],
+        in_specs=[vmem, vmem],
+        out_specs=[vmem, vmem],
+        scratch_shapes=[
+            pltpu.VMEM((n_row, *gains.shape), gains.dtype),
+            pltpu.VMEM(gains.shape, gains.dtype),
+            dma,
+            dma((n_row - 1,)),
+            dma((n_row,)),
+            dma((n_row - 1,)),
+            dma((n_row,)),
+            dma((n_col - 1,)),
+            dma((n_col,)),
+        ],
+        compiler_params=pltpu.CompilerParams(collective_id=number, has_side_effects=True),
+        name=f"finish_{number}",
+    )(value, gains)
+
+
+def total_every(place, partials, small_value, number):
+    blocks, slot_count, tokens = place.shape
+    if kernel_fits(blocks * tokens, partials[0][0].shape[2], len(partials)):
+        return kernel_total(place, partials, small_value, number)
+    capacity = partials[0][0].shape[1] // blocks
     exchanged = lax.all_to_all(small_value, EVERY, split_axis=0, concat_axis=0, tiled=True)
-    return *[every_total(p) for p in partials], exchanged
+    return *[every_total(combine_rows(place, *p, capacity)) for p in partials], exchanged
 
 
 def mixed_fits(col_values):
@@ -1185,11 +1332,20 @@
     return n_row == 4 and (not col_values or (lax.axis_size("col") % 2 == 0 and lines <= 8))
 
 
-def gather_mixed(col_values, dims, flips, row_value, small_value, number):
-    if mixed_fits(col_values):
-        return mixed_gather(col_values, dims, flips, row_value, small_value, number)
-    cols = [lax.all_gather(v, "col", axis=d, tiled=True) for v, d in zip(col_values, dims)]
-    return *cols, token_rows(row_value), every_token(small_value[None])
+def gather(col_values, dims, flips, row_value, every_value, ways, small_value, number):
+    fits = not col_values and every_value is None or lax.axis_size("col") in (4, 6, 8, 10)
+    if lax.axis_size("row") == 4 and fits:
+        return kernel_gather(
+            col_values, dims, flips, row_value, every_value, ways, small_value, number
+        )
+    out = [lax.all_gather(v, "col", axis=d, tiled=True) for v, d in zip(col_values, dims)]
+    if row_value is not None:
+        out.append(token_rows(row_value))
+    if every_value is not None:
+        out.append(every_token(every_value))
+    if small_value is not None:
+        out.append(every_token(small_value[None]))
+    return out
 
 
 def total_mixed(col_values, dims, flips, row_value, number):
@@ -1210,36 +1366,103 @@
     return jnp.where(allowed[None], scores, -1e30)
 
 
-def select_body(group, capacity, place_ref, rows_ref, slots_ref):
+def tokens_body(
+    group,
+    capacity,
+    place_ref,
+    x_ref,
+    g_ref,
+    both_ref,
+    down_ref,
+    xs_ref,
+    gs_ref,
+    hidden_ref,
+    grad_ref,
+    dboth_ref,
+    ddown_ref,
+):
     tokens = place_ref.shape[2]
     for block in range(group):
-        picked = matmul(place_ref[block], rows_ref[block * tokens : (block + 1) * tokens, :])
-        slots_ref[:, block] = picked.astype(BF16).reshape(-1, capacity, picked.shape[-1])
-
-
-def select_rows(place, rows, capacity):
+        rows = slice(block * tokens, (block + 1) * tokens)
+        for source, slots in ((x_ref, xs_ref), (g_ref, gs_ref)):
+            picked = matmul(place_ref[block], source[rows, :])
+            slots[:, block] = picked.astype(BF16).reshape(-1, capacity, picked.shape[-1])
+    half = down_ref.shape[0]
+    both = outer_cols(x_ref[...], both_ref[...])
+    act, slope = silu_parts(both[:, :half])
+    lin = both[:, half:]
+    hidden = (act * lin).astype(BF16)
+    back = outer_cols(g_ref[...], down_ref[...])
+    grads = jnp.concatenate([back * lin * slope, back * act], axis=1).astype(BF16)
+    hidden_ref[...] = hidden
+    grad_ref[...] = grads
+    dboth = inner_rows(grads, x_ref[...])
+    ddown = inner_rows(hidden, g_ref[...])
+
+    @pl.when(pl.program_id(0) == 0)
+    def _():
+        dboth_ref[...] = dboth
+        ddown_ref[...] = ddown
+
+    @pl.when(pl.program_id(0) > 0)
+    def _():
+        dboth_ref[...] += dboth
+        ddown_ref[...] += ddown
+
+
+def run_tokens(place, x_all, g_all, both_weight, down_weight, local_experts):
     blocks, slots, tokens = place.shape
-    width = rows.shape[1]
-    local_experts = slots // capacity
+    capacity = slots // local_experts
+    width = x_all.shape[1]
+    half = down_weight.shape[0]
     group = 4 if blocks % 4 == 0 else 1
-    out = pl.pallas_call(
-        functools.partial(select_body, group, capacity),
+    row_block = pl.BlockSpec((group * tokens, width), lambda i: (i, 0))
+    slot_block = pl.BlockSpec((local_experts, group, capacity, width), lambda i: (0, i, 0, 0))
+    slot_shape = jax.ShapeDtypeStruct((local_experts, blocks, capacity, width), BF16)
+
+    def whole(size):
+        return pl.BlockSpec((size, width), lambda i: (0, 0))
+
+    def hidden_block(size):
+        return pl.BlockSpec((group * tokens, size), lambda i: (i, 0))
+
+    rows = blocks * tokens
+    xs, gs, hidden, grads, dboth, ddown = pl.pallas_call(
+        functools.partial(tokens_body, group, capacity),
         grid=(blocks // group,),
         in_specs=[
             pl.BlockSpec((group, slots, tokens), lambda i: (i, 0, 0)),
-            pl.BlockSpec((group * tokens, width), lambda i: (i, 0)),
+            row_block,
+            row_block,
+            whole(2 * half),
+            whole(half),
         ],
-        out_specs=pl.BlockSpec((local_experts, group, capacity, width), lambda i: (0, i, 0, 0)),
-        out_shape=jax.ShapeDtypeStruct((local_experts, blocks, capacity, width), BF16),
+        out_specs=[
+            slot_block,
+            slot_block,
+            hidden_block(half),
+            hidden_block(2 * half),
+            whole(2 * half),
+            whole(half),
+        ],
+        out_shape=[
+            slot_shape,
+            slot_shape,
+            jax.ShapeDtypeStruct((rows, half), BF16),
+            jax.ShapeDtypeStruct((rows, 2 * half), BF16),
+            jax.ShapeDtypeStruct((2 * half, width), F32),
+            jax.ShapeDtypeStruct((half, width), F32),
+        ],
         compiler_params=pltpu.CompilerParams(vmem_limit_bytes=VMEM_LIMIT),
         cost_estimate=pl.CostEstimate(
-            flops=2 * blocks * slots * tokens * width,
-            bytes_accessed=4 * blocks * tokens * width,
-            transcendentals=0,
+            flops=2 * rows * width * (2 * slots + 6 * half),
+            bytes_accessed=8 * rows * width,
+            transcendentals=rows * half,
         ),
-        name="select_rows",
-    )(place, rows)
-    return out.reshape(local_experts, blocks * capacity, width)
+        name="run_tokens",
+    )(place, x_all, g_all, both_weight, down_weight)
+    shape = (local_experts, blocks * capacity, width)
+    return xs.reshape(shape), gs.reshape(shape), hidden, grads, dboth, ddown
 
 
 def experts_body(
@@ -1397,11 +1620,13 @@
     own_down = lax.dynamic_slice_in_dim(latent_down, own_row * down_cols, down_cols, 1)
     output_rows = output_weight.shape[0]
     query_cols = query_weight.shape[1]
-    query_all, output_down, expand_all, seq_normed, all_routes = gather_mixed(
+    query_all, output_down, expand_all, seq_normed, grad_all, all_routes = gather(
         [query_weight, jnp.concatenate([output_weight, own_down.T], axis=0), latent_up],
         [0, 1, 0],
         [False, False, True],
         normed_one,
+        grad_out.astype(BF16),
+        (0, 0),
         padded_rows(own_routes.astype(F32).T),
         1,
     )
@@ -1409,7 +1634,6 @@
     down_all = output_down[output_rows:]
 
     all_routes = all_routes[:, :TOPK].astype(jnp.int32)
-    grad_all = every_token(grad_out.astype(BF16))
     local_ids = own_col * local_experts + jnp.arange(local_experts)
     named = all_routes[:, :, None, :] == local_ids[None, None, :, None]
     chosen_here = jnp.max(named.astype(BF16), axis=1)
@@ -1418,7 +1642,6 @@
     slot_of = jnp.where(chosen_here > 0, rank.astype(jnp.int32), -1)
     placed = slot_of[:, :, None, :] == jnp.arange(capacity)[None, None, :, None]
     place = placed.astype(BF16).reshape(blocks, local_experts * capacity, own_rows)
-    grad_slots = select_rows(place, grad_all, capacity)
 
     shared_cols = shared_gate.shape[1] // n_col
     shared_send = jnp.stack([shared_gate.T, shared_up.T, shared_down], axis=0)
@@ -1428,12 +1651,15 @@
         .transpose(1, 0, 2, 3)
         .reshape(n_col, 3 * shared_cols, depth)
     )
+    shared_send, all_routes = lax.optimization_barrier((shared_send, all_routes))
     shared_own = (
         lax.all_to_all(shared_send, "col", split_axis=0, concat_axis=0, tiled=True)
         .transpose(1, 0, 2)
         .reshape(3, shared_cols, width)
     )
-    gate_up_own = shared_own[:2].reshape(2 * shared_cols, width)
+    shared_own = jnp.pad(shared_own, ((0, 0), (0, -shared_cols % 128), (0, 0)))
+    shared_held = shared_own.shape[1]
+    gate_up_own = shared_own[:2].reshape(2 * shared_held, width)
     down_own = shared_own[2]
 
     heads_local = query_cols // qk_dim
@@ -1445,7 +1671,10 @@
         ],
         axis=-1,
     ).astype(BF16)
-    latent_all = lax.all_gather(outer_cols(seq_normed, down_all), "row", axis=1, tiled=True)
+    (latent_all,) = gather(
+        [], [], [], outer_cols(down_all, seq_normed), None, None, None, 8
+    )
+    latent_all = latent_all.T
     latent = latent_all[:, :LATENT]
     scale_latent = rms_scale(latent)
     latent_normed = (latent * scale_latent * latent_gain).astype(BF16)
@@ -1467,7 +1696,6 @@
         .astype(BF16)
         .reshape(length, heads_local * VD)
     )
-    heads_out, grad_all = lax.optimization_barrier((heads_out, grad_all))
     (attn_total,) = total_mixed([], [], [], matmul(heads_out, output_all).astype(BF16), 6)
     residual = stream + attn_total
 
@@ -1479,56 +1707,39 @@
     picked = jnp.sum(jnp.where(chosen, logits[:, None, :], 0.0), axis=-1)
     gate_probs = jax.nn.softmax(picked, axis=-1)
 
-    all_normed, all_gates = gather_every(normed_two, padded_rows(gate_probs.T), 2)
+    all_normed, all_gates = gather(
+        [], [], [], None, normed_two, (0, 1), padded_rows(gate_probs.T), 2
+    )
     all_gates = all_gates[:, :TOPK]
     gate_here = jnp.sum(jnp.where(named, all_gates[:, :, None, :], 0.0), axis=1)
     slot_gate = jnp.sum(jnp.where(placed, gate_here[:, :, None, :], 0.0), axis=-1)
     slot_gate = slot_gate.transpose(1, 0, 2).reshape(local_experts, blocks * capacity, 1)
-    normed_slots = select_rows(place, all_normed, capacity)
+    normed_slots, grad_slots, shared_hidden, shared_both_grad, gate_up_part, down_part = run_tokens(
+        place, all_normed, grad_all, gate_up_own, down_own, local_experts
+    )
     out_slots, rows_slots, expert_gate_grad, expert_up_grad, expert_down_grad, slot_dot = (
         run_experts(normed_slots, grad_slots, slot_gate, expert_gate, expert_up, expert_down)
     )
 
-    shared_both = outer_cols(all_normed, gate_up_own)
-    shared_act, shared_slope = silu_parts(shared_both[:, :shared_cols])
-    shared_lin = shared_both[:, shared_cols:]
-    shared_hidden = (shared_act * shared_lin).astype(BF16)
-    shared_hidden_grad = outer_cols(grad_all, down_own)
-    shared_both_grad = jnp.concatenate(
-        [
-            (shared_hidden_grad * shared_lin * shared_slope).astype(BF16),
-            (shared_hidden_grad * shared_act).astype(BF16),
-        ],
-        axis=1,
-    )
     slot_dot = slot_dot.reshape(local_experts, blocks, capacity).transpose(1, 0, 2)
     token_dot = jnp.sum(jnp.where(placed, slot_dot[:, :, :, None], 0.0), axis=2)
     out_total, rows_total, token_dot = total_every(
+        place,
         [
-            combine_rows(place, out_slots, shared_hidden, down_own, capacity),
-            combine_rows(place, rows_slots, shared_both_grad, gate_up_own, capacity),
+            (out_slots, shared_hidden, down_own),
+            (rows_slots, shared_both_grad, gate_up_own),
         ],
         token_dot,
         3,
     )
     layer_out = (residual + out_total).astype(BF16).reshape(1, own_rows, width)
-    gate_up_part = inner_rows(shared_both_grad, all_normed)
-    down_part = inner_rows(shared_hidden, grad_all)
-    shared_back = jnp.concatenate([gate_up_part, down_part], axis=0).astype(BF16)
+    shared_back = jnp.concatenate(
+        [gate_up_part.reshape(2, shared_held, width), down_part[None]], axis=0
+    )[:, :shared_cols].astype(BF16)
     shared_back = (
         shared_back.reshape(3 * shared_cols, n_col, depth).transpose(1, 0, 2)
     )
     shared_back = lax.all_to_all(shared_back, "col", split_axis=0, concat_axis=0, tiled=True)
-    shared_back = (
-        shared_back.reshape(n_col, 3, shared_cols, depth)
-        .transpose(1, 0, 2, 3)
-        .reshape(3, n_col * shared_cols, depth)
-        .astype(F32)
-    )
-    shared_gate_grad = shared_back[0].T
-    shared_up_grad = shared_back[1].T
-    shared_down_grad = shared_back[2]
-
     token_dot = jnp.sum(token_dot.reshape(n_col, n_row, local_experts, own_rows), axis=1)
     token_dot = token_dot.reshape(experts, own_rows).T
     gate_grad = jnp.sum(jnp.where(chosen, token_dot[:, None, :], 0.0), axis=-1)
@@ -1539,10 +1750,12 @@
     second_gain_part = jnp.sum(normed_two_grad * residual * scale_two, axis=0)
     residual_grad = grad_out + rms_back(residual, scale_two, normed_two_grad * second_gain)
 
-    seq_resid, all_logit_grad = gather_mixed(
-        [], [], [], residual_grad.astype(BF16), logit_grad, 4
-    )
-    router_grad = inner_rows(all_normed, all_logit_grad.reshape(-1, experts))
+    seq_resid, all_picked = gather(
+        [], [], [], residual_grad.astype(BF16), None, None, padded_rows(picked_grad.T), 4
+    )
+    all_named = all_routes[:, :, :, None] == expert_ids
+    all_logit_grad = jnp.sum(jnp.where(all_named, all_picked[:, :TOPK, :, None], 0.0), axis=1)
+    router_grad = inner_rows(all_normed, all_logit_grad.astype(BF16).reshape(-1, experts))
     output_part = inner_rows(heads_out, seq_resid)
     heads_grad = outer_cols(seq_resid, output_all).astype(BF16).reshape(length, heads_local, VD)
     recomputed = jnp.exp(masked_scores(queries, attn_keys, allowed, softmax_scale) - log_total)
@@ -1583,10 +1796,10 @@
     expand_part = inner_rows(latent_normed, keyval_grad)
     latent_normed_part = outer_cols(keyval_grad, expand_all)
     rope_part = jnp.sum(key_grad[..., NOPE:], axis=1)
-    latent_normed_grad, rope_raw = (
-        lax.psum(latent_normed_part.astype(BF16), "row").astype(F32),
-        lax.psum(rope_part.astype(BF16), "row").astype(F32),
-    )
+    latent_total = row_sum(
+        jnp.concatenate([latent_normed_part, rope_part], axis=1).astype(BF16), 9
+    ).astype(F32)
+    latent_normed_grad, rope_raw = latent_total[:, :LATENT], latent_total[:, LATENT:]
     rope_grad = unrotate(rope_raw, cosine_table, sine_table)
     latent_gain_part = jnp.sum(
         lax.dynamic_slice_in_dim(
@@ -1601,6 +1814,7 @@
         [output_part.astype(BF16), inner_rows(own_down_grad, seq_normed).astype(BF16)], axis=0
     )
     input_part = outer_cols(query_full, query_all) + matmul(own_down_grad, down_all)
+    input_part, shared_back = lax.optimization_barrier((input_part, shared_back))
     query_grad, output_down_grad, latent_up_grad, normed_one_grad = total_mixed(
         [inner_rows(seq_normed, query_full).astype(BF16), output_down_part, expand_part.astype(BF16)],
         [0, 1, 0],
@@ -1614,11 +1828,19 @@
         residual_grad + rms_back(stream, scale_one, normed_one_grad * first_gain)
     ).reshape(1, own_rows, width)
 
+    shared_back = (
+        shared_back.reshape(n_col, 3, shared_cols, depth)
+        .transpose(1, 0, 2, 3)
+        .reshape(3, n_col * shared_cols, depth)
+        .astype(F32)
+    )
+    shared_gate_grad = shared_back[0].T
+    shared_up_grad = shared_back[1].T
+    shared_down_grad = shared_back[2]
+
     gains = jnp.concatenate([first_gain_part, latent_gain_part, second_gain_part])
     gains = padded_rows(gains.reshape(-1, LATENT // 4))
-    down_total, all_gains = gather_mixed(
-        [], [], [], output_down_grad[output_rows:].astype(BF16), gains, 5
-    )
+    down_total, all_gains = kernel_finish(output_down_grad[output_rows:].astype(BF16), gains, 5)
     latent_down_grad = down_total.astype(F32).T
     gains = jnp.sum(all_gains, axis=0).reshape(-1)
     first_gain_grad = gains[:width]

time: 976 us -> 836 us (0.86)
  waiting for transfers between devices: 133 us -> 3.93 us
  matrix products: 93 us -> 46.8 us
  Pallas kernels: 647 us -> 680 us
  between operations: 15.1 us -> 2 us
    all_gather x2 -> x0, waiting for transfers between devices: 98.6 us -> none  [the longest x1 98.6 us: every_token(): return lax.all_gather(values, EVERY, axis=0, tiled=True)]
    pallas_call x8 -> x7, Pallas kernels: 275 us -> 312 us  [the longest x4 246 us: kernel_gather(): pl.pallas_call(functools.partial(gather_body, lines, tuple(dims), tuple(f...]
    psum x1 -> x0, waiting for transfers between devices: 34 us -> none  [on_device(): lax.psum(latent_normed_part.astype(BF16), 'row').astype(F32)]
    dot_general x7 -> x5, matrix products: 37.7 us -> 13.8 us  [outer_cols(): lax.dot_general(left_side, right_side, COLS_CONTRACT, preferred_element_t...]
    dot_general x7 -> x5, matrix products: 31.1 us -> 12.7 us  [inner_rows(): lax.dot_general(left_side, right_side, ROWS_CONTRACT, preferred_element_t...]
  transfers between devices with their start and end apart: 5 -> 2, of which waited for: 2 -> 1; matrix products, arithmetic and copies ran while one was open for 6% -> 7% of each run, Pallas kernels for 11% -> 13%
where the time goes in v3:
time: 836 us; the launch traced here: 830 us
  Pallas kernels  680 us (81%)
  matrix products  46.8 us (6%)
  other arithmetic  42.1 us (5%)
  local copies, waits for them, and re-layouts  32.9 us (4%)
  starting transfers between devices  21.5 us (3%)
    pallas_call x4, Pallas kernels, kernel_gather(): pl.pallas_call(functools.partial(gather_body, lines, tuple(dims), tuple(f...  246 us
    pallas_call x1, Pallas kernels, kernel_total(): pl.pallas_call(functools.partial(scatter_body, lines, count, small), out_...  182 us
    pallas_call x2, Pallas kernels, mixed_total(): pl.pallas_call(functools.partial(mixed_total_body, lines, tuple(dims), tu...  105 us
    pallas_call x1, Pallas kernels, run_experts(): pl.pallas_call(experts_body, grid=(count, rows // chunk), in_specs=[row_b...  81.2 us
    pallas_call x1, Pallas kernels, run_tokens(): pl.pallas_call(functools.partial(tokens_body, group, capacity), grid=(blo...  36.4 us
  transfers between devices with their start and end apart: 2, of which 1 were waited for; matrix products, arithmetic and copies ran while one was open for 7% of the time, Pallas kernels for 13%

profile of v3, /device:TPU:8, one launch (start us, length us, event | category | flops | bytes accessed | tf_op | source)
XLA Modules:
  0.0 829.6 jit_solution(9326867248894377275)
XLA Ops:
  0.7 1.3 fusion.11
  3.3 2.1 bitcast_convert_fusion.refs_4_
  7.7 131.8 %gather_1.1 = (bf16[2048,768]{1,0:T(8,128)(2,1)}, bf16[656,2048]{1,0:T(8,128)(2,1)}, bf16[512,1024]{1,0:T(8,128)(2,1)}, bf16[512,2048]{1,0:T(8,128)(2,1)}, bf16[...) custom-call(bf16[256,768]{1,0:T(8,128)(2,1)} %refs_0_.1, bf16[656,256]{1,0:T(8,128)(2,1)} %pad_maximum_fusion.10.refs_1_, ...), custom_call_target="tpu_custom_call" | custom-call | tf_op jit(solution)/shard_map/gather_1/pallas_call | solution.py:920
  140.4 2.3 pad_maximum_fusion.2
  142.8 15.8 %all-to-all-start = ((bf16[8,264,256]{2,1,0:T(8,128)(2,1)}), bf16[8,264,256]{2,1,0:T(8,128)(2,1)}, u32[]{:S(2)}, u32[]{:S(2)}) async-start(bf16[8,264,256]{2,1,0:T(8,128)(2,1)} %bitcast.167), calls=%async_computation | async-start | bytes 2162688 | tf_op jit(solution)/shard_map/all_to_all | solution.py:1656
  158.6 1.7 fusion.40
  160.3 2.6 fusion.30.refs_0_
  162.9 12.0 %gather_8.1 = f32[576,512]{1,0:T(8,128)} custom-call(f32[144,512]{1,0:T(8,128)} %fusion.30.refs_0_), custom_call_target="tpu_custom_call" | custom-call | tf_op jit(solution)/shard_map/gather_8/pallas_call | solution.py:920
  174.9 1.7 copy.178
  176.7 1.1 multiply_subtract_fusion
  177.8 1.0 fusion.56
  179.7 3.0 convolution_convert_fusion.5
  182.7 2.4 copy.213
  185.1 1.1 slice.167
  186.2 3.9 fusion.59
  190.3 1.0 fusion.1
  192.4 1.0 copy-done.15
  193.4 1.4 convolution_convert_fusion.7
  195.6 2.6 convolution_convert_fusion.2.refs_0_
  198.2 17.6 %mixed_total_6.1 = f32[128,2048]{1,0:T(8,128)} custom-call(bf16[512,2048]{1,0:T(8,128)(2,1)} %convolution_convert_fusion.2.refs_0_), custom_call_target="tpu_custom_call" | custom-call | tf_op jit(solution)/shard_map/mixed_total_6/pallas_call | solution.py:1156
  215.8 1.5 multiply_reduce_fusion.4
  219.5 81.0 %gather_2.1 = (bf16[4096,2048]{1,0:T(8,128)(2,1)}, f32[32,8,128]{2,1,0:T(8,128)}) custom-call(bf16[128,2048]{1,0:T(8,128)(2,1)} %copy-done.13, f32[8,128]{1,0:T(8,128)} %pad.19.refs_1_), custom_call_target="tpu_custom_call" | custom-call | tf_op jit(solution)/shard_map/gather_2/pallas_call | solution.py:920
  300.9 1.3 fusion.2.place_ref.refs_0_
  302.2 1.1 fusion.22
  304.0 2.4 reshape.382.gate_ref
  306.4 1.5 copy.190
  309.2 1.1 pad_slice_fusion.1
  310.3 36.4 %run_tokens.1 = (bf16[8,32,16,2048]{3,2,1,0:T(8,128)(2,1)}, bf16[8,32,16,2048]{3,2,1,0:T(8,128)(2,1)}, bf16[4096,128]{1,0:T(8,128)(2,1)}, bf16[4096,256]{1,0:T(8...) custom-call(bf16[32,128,128]{2,1,0:T(8,128)(2,1)} %fusion.2.place_ref.refs_0_, ...), custom_call_target="tpu_custom_call" | custom-call | flops 17179869184 | bytes 67108864 | tf_op jit(solution)/shard_map/run_tokens/pallas_call | solution.py:1430
  346.7 81.2 %run_experts.1 = (bf16[8,512,2048]{2,1,0:T(8,128)(2,1)}, bf16[8,512,2048]{2,1,0:T(8,128)(2,1)}, f32[8,352,2048]{2,1,0:T(8,128)}, f32[8,352,2048]{2,1,0:T(8,128)}...) custom-call(bf16[8,512,2048]{2,1,0:T(8,128)(2,1)} %bitcast.198, bf16[8,512,2048]{2,1,0:T(8,128)(2,1)} %bitcast.199, ...), custom_call_target="tpu_custom_call" | custom-call | flops 53150220288 | bytes 170917888 | tf_op jit(solution)/shard_map/run_experts/pallas_call | solution.py:1517
  428.0 2.2 reduce
  430.4 1.6 select_reduce_fusion.1.refs_7_
  431.9 182.1 %scatter_3.1 = (f32[128,2048]{1,0:T(8,128)}, f32[128,2048]{1,0:T(8,128)}, f32[32,8,128]{2,1,0:T(8,128)}) custom-call(bf16[32,128,128]{2,1,0:T(8,128)(2,1)} %fusion.2.place_ref.refs_0_, bf16[8,32,16,2048]{3,2,1,0:T(8,128)(2,1)} %bitcast.165, bf16[8,32,16,2048]{3,2,1,0:T(8,128)(2,1)} %bitcast.166, bf16[4096,128]{1,0:T(8,128)(2,1)} %get-tuple-element.64.refs_3_, ...), custom_call_target="tpu_custom_call" | custom-call | tf_op jit(solution)/shard_map/scatter_3/pallas_call | solution.py:509
  614.0 1.1 bitcast_reduce_fusion
  615.8 2.2 multiply_reduce_fusion
  618.0 1.7 fusion.54
  619.8 21.2 %gather_4.1 = (bf16[512,2048]{1,0:T(8,128)(2,1)}, f32[32,8,128]{2,1,0:T(8,128)}) custom-call(bf16[128,2048]{1,0:T(8,128)(2,1)} %get-tuple-element.90.refs_0_, f32[8,128]{1,0:T(8,128)} %pad.21.refs_1_), custom_call_target="tpu_custom_call" | custom-call | tf_op jit(solution)/shard_map/gather_4/pallas_call | solution.py:920
  641.0 3.7 multiply_reduce_fusion.2
  644.7 2.6 convolution_convert_fusion.1
  647.3 1.4 fusion.9
  648.7 1.8 multiply_convert_fusion
  653.4 1.5 convolution_convert_fusion.8
  655.0 1.9 convolution_convert_fusion.4.refs_2_
  657.2 1.9 pad_maximum_fusion.7.value_ref
  659.1 15.9 %row_sum_9.1 = bf16[512,576]{1,0:T(8,128)(2,1)} custom-call(bf16[512,576]{1,0:T(8,128)(2,1)} %pad_maximum_fusion.7.value_ref), custom_call_target="tpu_custom_call" | custom-call | tf_op jit(solution)/shard_map/row_sum_9/pallas_call | solution.py:1221
  675.0 2.2 slice.175
  677.5 1.1 subtract_convert_fusion.1
  680.2 1.2 copy.202
  681.4 5.7 all-to-all-start.1
  687.1 3.8 fusion.61
  693.7 1.7 pad_maximum_fusion.refs_1_
  695.4 1.6 fusion.38
  697.1 3.5 convolution_add_fusion.refs_3_
  700.6 3.5 convolution_convert_fusion.refs_0_
  704.1 3.8 fusion.26
  708.0 3.9 all-to-all-done.1
  711.9 87.2 %mixed_total_7.1 = (f32[256,768]{1,0:T(8,128)}, f32[656,256]{1,0:T(8,128)}, f32[64,1024]{1,0:T(8,128)}, f32[128,2048]{1,0:T(8,128)}) custom-call(bf16[2048,768]{1,0:T(8,128)(2,1)} %convolution_convert_fusion.refs_0_, bf16[656,2048]{1,0:T(8,128)(2,1)} %pad_maximum_fusion.refs_1_, bf16[512,1024]{1,0:T(8,128)(2,1)} %convolution_convert_fusion.4.refs_2_, ...), custom_call_target="tpu_custom_call" | custom-call | tf_op jit(solution)/shard_map/mixed_total_7/pallas_call | solution.py:1156
  799.1 1.6 slice.244.value_ref
  800.7 1.9 slice.155
  802.6 1.5 fusion.20
  804.7 13.9 %finish_5.1 = (bf16[576,256]{1,0:T(8,128)(2,1)}, f32[8,40,128]{2,1,0:T(8,128)}) custom-call(bf16[144,256]{1,0:T(8,128)(2,1)} %slice.244.value_ref, f32[40,128]{1,0:T(8,128)} %pad.22.gains_ref), custom_call_target="tpu_custom_call" | custom-call | tf_op jit(solution)/shard_map/finish_5/pallas_call | solution.py:1297
  820.7 1.8 convert_bitcast_fusion.1
  822.5 1.4 convert_bitcast_fusion
  824.0 1.4 fusion.55
  826.3 1.4 fusion.17
  (200 shorter events, 25.7 us)
Async XLA Ops:
  0.6 5.3 copy-start
  0.7 6.1 copy-start.6
  0.7 5.3 copy-start.46
  0.7 6.0 copy-start.49
  2.6 136.9 %copy-start.53 = (f32[128]{0:T(128)}, f32[128]{0:T(128)S(1)}, u32[]{:S(2)}) copy-start(f32[128]{0:T(128)S(1)} %get-tuple-element.115) | copy-start | bytes 1540
  5.3 135.1 %copy-start.44 = (bf16[704,256]{1,0:T(8,128)(2,1)S(1)}, bf16[704,256]{1,0:T(8,128)(2,1)}, u32[]{:S(2)}) copy-start(bf16[704,256]{1,0:T(8,128)(2,1)} %param.31) | copy-start | bytes 1081348
  140.4 19.9 %copy-start.10 = (bf16[512,2048]{1,0:T(8,128)(2,1)S(1)}, bf16[512,2048]{1,0:T(8,128)(2,1)}, u32[]{:S(2)}) copy-start(bf16[512,2048]{1,0:T(8,128)(2,1)} %get-tuple-element.52) | copy-start | bytes 6291460
  142.8 163.6 %all-to-all-start = ((bf16[8,264,256]{2,1,0:T(8,128)(2,1)}), bf16[8,264,256]{2,1,0:T(8,128)(2,1)}, u32[]{:S(2)}, u32[]{:S(2)}) async-start(bf16[8,264,256]{2,1,0:T(8,128)(2,1)} %bitcast.167), calls=%async_computation | async-start | bytes 2162688 | tf_op jit(solution)/shard_map/all_to_all | solution.py:1656
  174.9 4.0 copy-start.52
  176.6 3.1 copy-start.2
  176.6 2.5 copy-start.32
  176.6 3.1 copy-start.51
  179.1 13.2 %copy-start.30 = (pred[512,512]{0,1:T(8,128)(4,1)}, pred[512,512]{0,1:T(8,128)(4,1)S(1)}, u32[]{:S(2)}) copy-start(pred[512,512]{0,1:T(8,128)(4,1)S(1)} %fusion.21) | copy-start | bytes 786436
  179.4 10.8 %copy-start.37 = (f32[512,32]{0,1:T(8,128)}, f32[512,32]{0,1:T(8,128)S(1)}, u32[]{:S(2)}) copy-start(f32[512,32]{0,1:T(8,128)S(1)} %copy.183) | copy-start | bytes 196612
  182.6 3.5 copy-start.11
  186.2 4.2 copy-start.21
  190.2 1.2 copy-start.23
  190.3 1.1 copy-start.39
  190.3 1.1 copy-start.41
  190.3 1.1 copy-start.28
  191.4 2.0 copy-start.15
  191.4 2.0 copy-start.19
  193.4 2.2 copy-start.43
  215.8 2.5 copy-start.48
  215.8 2.6 copy-start.27
  217.3 1.0 copy-start.4
  218.5 1.0 copy-start.13
  614.0 4.0 copy-start.5
  614.0 4.0 copy-start.18
  614.0 4.0 copy-start.35
  618.0 23.0 %copy-start.58 = (bf16[4,128,512]{2,1,0:T(8,128)(2,1)S(1)}, bf16[4,128,512]{2,1,0:T(8,128)(2,1)}, u32[]{:S(2)}) copy-start(bf16[4,128,512]{2,1,0:T(8,128)(2,1)} %copy-done.57) | copy-start | bytes 1572868
  641.0 3.7 copy-start.56
  644.7 2.6 copy-start.16
  644.7 2.6 copy-start.31
  647.3 1.4 copy-start.20
  648.7 1.8 copy-start.24
  648.7 1.8 copy-start.40
  648.7 1.8 copy-start.42
  650.5 1.0 copy-start.22
  650.5 1.1 copy-start.29
  652.2 1.2 copy-start.34
  652.4 2.6 copy-start.3
  655.0 1.9 copy-start.38
  675.0 2.2 copy-start.9
  677.2 1.7 copy-start.33
  677.3 1.7 copy-start.7
  677.3 2.3 copy-start.25
  681.4 30.5 %all-to-all-start.1 = ((bf16[8,264,256]{2,1,0:T(8,128)(2,1)}), bf16[8,264,256]{2,1,0:T(8,128)(2,1)}, u32[]{:S(2)}, u32[]{:S(2)}) async-start(bf16[8,264,256]{2,1,0:T(8,128)(2,1)} %copy.202), calls=%async_computation.1 | async-start | bytes 2162688 | tf_op jit(solution)/shard_map/all_to_all | solution.py:1742
  687.1 3.9 copy-start.47
  687.1 4.9 copy-start.8
  691.0 1.6 copy-start.12
  692.0 1.7 copy-start.26
  692.0 12.1 %slice-start = ((s8[16777216]{0:T(1024)(128)(4,1)}), s8[4194304]{0:T(1024)(128)(4,1)S(1)}, s32[]{:S(2)}) async-start(s8[16777216]{0:T(1024)(128)(4,1)} %bitcast.163), calls=%async_computation.2 | async-start | bytes 8388608
  693.7 10.4 %slice-start.1 = ((s8[16777216]{0:T(1024)(128)(4,1)}), s8[4194304]{0:T(1024)(128)(4,1)S(1)}, s32[]{:S(2)}) async-start(s8[16777216]{0:T(1024)(128)(4,1)} %bitcast.163), calls=%async_computation.3 | async-start | bytes 8388608
  697.1 7.1 slice-start.2
  700.6 3.5 slice-start.3
  708.0 94.6 %copy-start.50 = (f32[2048]{0:T(1024)S(1)}, f32[2048]{0:T(1024)}, u32[]{:S(2)}) copy-start(f32[2048]{0:T(1024)} %param.21) | copy-start | bytes 24580
  708.0 94.6 %copy-start.54 = (f32[128]{0:T(128)S(1)}, f32[128]{0:T(128)}, u32[]{:S(2)}) copy-start(f32[128]{0:T(128)} %copy-done.53) | copy-start | bytes 1540
  823.9 1.8 copy-start.14
  823.9 2.3 copy-start.17
  823.9 2.3 copy-start.55
  825.3 2.4 copy-start.36
  825.3 4.0 copy-start.1
  826.2 2.3 copy-start.45
  (1 other events, 0.8 us)

commit v4 on v3

--- a/solution.py
+++ b/solution.py
@@ -198,21 +198,14 @@
     return order
 
 
-def scatter_body(lines, count, small, *refs):
-    place_ref, refs = refs[0], refs[1:]
-    slots, extras, weights = refs[:count], refs[count : 2 * count], refs[2 * count : 3 * count]
-    refs = refs[3 * count :]
-    if small:
-        small_ref, refs = refs[0], refs[1:]
-    outs, refs = refs[:count], refs[count:]
-    if small:
-        small_out, refs = refs[0], refs[1:]
-    own, core_in, wide_in, side_in, up_in, down_in = refs[:6]
-    slot_in, staged, slot_sem, credit = refs[6:10]
-    core_send, core_recv, wide_send, wide_recv, side_send, side_recv = refs[10:16]
-    up_send, up_recv, down_send, down_recv = refs[16:20]
-    refs = refs[3:]
-    wide, core, line, side = places()
+def every_total_plan(lines, ways, spots, place_ref, slots, extras, weights, outs, scratch):
+    count = 1
+    slots, extras, weights, outs = [slots], [extras], [weights], [outs]
+    own, core_in, wide_in, side_in, up_in, down_in = scratch[:6]
+    slot_in, staged, slot_sem, credit = scratch[6:10]
+    core_send, core_recv, wide_send, wide_recv, side_send, side_recv = scratch[10:16]
+    up_send, up_recv, down_send, down_recv = scratch[16:20]
+    wide, core, line, side = spots
     tokens, width = own.shape[1:]
     ring, core_ring = slot_in.shape[0], core_in.shape[0]
     half = tokens // 2
@@ -223,26 +216,17 @@
     below = to_place(wide, core, line - 1, side)
     has_above = line < lines - 1
     has_below = line > 0
-    greet(
-        [
-            (core >= 0, core_mate),
-            (core >= 0, wide_mate),
-            (core >= 0, side_mate),
-            (has_above, above),
-            (has_below, below),
-        ],
-        small,
-    )
     parts = [pl.ds(0, half), pl.ds(half, half)]
 
     def at(a, l, s, w):
         return ((a * lines + l) * 2 + s) * 2 + w
 
     items = [(a, l) for a in range(count) for l in line_order(lines)]
+    corners = [(1 - side, 1 - wide), (1 - side, wide), (side, 1 - wide), (side, wide)]
     blocks = []
     for a, l in items:
-        blocks += [(a, 2 * (l * 4 + j) + 1 - core) for j in range(4)]
-        blocks += [(a, 2 * (l * 4 + j) + core) for j in range(4)]
+        for s, w in corners:
+            blocks += [(a, 2 * at(0, l, s, w) + 1 - core), (a, 2 * at(0, l, s, w) + core)]
 
     def slot_copy(q):
         a, b = blocks[q]
@@ -268,44 +252,27 @@
             core_mate,
         )
 
-    def wide_one(a, l, s):
-        n = (a * lines + l) * 3 + s
+    def spot(a, l, h, j):
+        return ((a * lines + l) * 2 + h) * 2 + j
+
+    def wide_copy(a, l, s, h):
+        n = spot(a, l, h, 0 if ways[h] else s)
         return remote(
-            own.at[at(a, l, s, 1 - wide), parts[0]],
+            own.at[at(a, l, s, 1 - wide), parts[h]],
             wide_in.at[n],
             wide_send.at[n],
             wide_recv.at[n],
             wide_mate,
         )
 
-    def side_one(a, l, w):
-        n = (a * lines + l) * 3 + w
+    def side_copy(a, l, w, h):
+        n = spot(a, l, h, w if ways[h] else 0)
         return remote(
-            own.at[at(a, l, 1 - side, w), parts[1]],
+            own.at[at(a, l, 1 - side, w), parts[h]],
             side_in.at[n],
             side_send.at[n],
             side_recv.at[n],
             side_mate,
-        )
-
-    def side_two(a, l):
-        n = (a * lines + l) * 3 + 2
-        return remote(
-            own.at[at(a, l, 1 - side, wide), parts[0]],
-            side_in.at[n],
-            side_send.at[n],
-            side_recv.at[n],
-            side_mate,
-        )
-
-    def wide_two(a, l):
-        n = (a * lines + l) * 3 + 2
-        return remote(
-            own.at[at(a, l, side, 1 - wide), parts[1]],
-            wide_in.at[n],
-            wide_send.at[n],
-            wide_recv.at[n],
-            wide_mate,
         )
 
     def up_copy(a, l, h):
@@ -331,60 +298,58 @@
     def add(i, rows, other):
         own[i, rows] = (own[i, rows].astype(F32) + other[...].astype(F32)).astype(BF16)
 
-    for q in range(ring - 1):
-        slot_copy(q).start()
-    if small:
-        small_start, small_finish = small_exchange(small_ref, small_out, *refs[17:19], True)
-        small_start()
+    def start():
+        for q in range(ring - 1):
+            slot_copy(q).start()
 
     def stage_one(t):
         a, l = items[t]
-        for j in range(4):
+        for j, (s, w) in enumerate(corners):
             n = t * 4 + j
             if n >= ring:
                 core_copy(n - ring).wait_send()
-            staged[n % ring] = summed(t * 8 + j)
+            staged[n % ring] = summed(t * 8 + 2 * j)
             if n >= core_ring:
                 pl.semaphore_wait(credit, 1)
             core_copy(n).start()
-        for j in range(4):
-            own[a * 4 * lines + l * 4 + j] = summed(t * 8 + 4 + j)
-        for j in range(4):
-            n = t * 4 + j
+            own[at(a, l, s, w)] = summed(t * 8 + 2 * j + 1)
             core_copy(n).wait_recv()
-            add(a * 4 * lines + l * 4 + j, pl.ds(0, tokens), core_in.at[n % core_ring])
+            add(at(a, l, s, w), pl.ds(0, tokens), core_in.at[n % core_ring])
             if n + core_ring < 4 * len(items):
                 pl.semaphore_signal(
                     credit, inc=1, device_id=core_mate, device_id_type=MESH_ID
                 )
+            for h in range(2):
+                if ways[h] and j in (0, 1):
+                    side_copy(a, l, w, h).start()
+                if not ways[h] and j in (0, 2):
+                    wide_copy(a, l, s, h).start()
+
+    def stage_two(a, l):
         for j in range(2):
-            wide_one(a, l, j).start()
-            side_one(a, l, j).start()
-
-    def stage_two(a, l):
-        n = (a * lines + l) * 3
-        for j in range(2):
-            s = 1 - side if j == 0 else side
-            wide_one(a, l, s).wait_recv()
-            add(at(a, l, s, wide), parts[0], wide_in.at[n + s])
-            if j == 0:
-                side_two(a, l).start()
-            w = 1 - wide if j == 0 else wide
-            side_one(a, l, w).wait_recv()
-            add(at(a, l, side, w), parts[1], side_in.at[n + w])
-            if j == 0:
-                wide_two(a, l).start()
+            s = side if j else 1 - side
+            w = wide if j else 1 - wide
+            for h in range(2):
+                if ways[h]:
+                    side_copy(a, l, w, h).wait_recv()
+                    add(at(a, l, side, w), parts[h], side_in.at[spot(a, l, h, w)])
+                    if j == 0:
+                        wide_copy(a, l, side, h).start()
+                else:
+                    wide_copy(a, l, s, h).wait_recv()
+                    add(at(a, l, s, wide), parts[h], wide_in.at[spot(a, l, h, s)])
+                    if j == 0:
+                        side_copy(a, l, wide, h).start()
 
     def stage_three(a, l):
-        n = (a * lines + l) * 3 + 2
         i = at(a, l, side, wide)
         for h in range(2):
-            if h == 0:
-                side_two(a, l).wait_recv()
-                add(i, parts[0], side_in.at[n])
+            if ways[h]:
+                wide_copy(a, l, side, h).wait_recv()
+                add(i, parts[h], wide_in.at[spot(a, l, h, 0)])
             else:
-                wide_two(a, l).wait_recv()
-                add(i, parts[1], wide_in.at[n])
+                side_copy(a, l, wide, h).wait_recv()
+                add(i, parts[h], side_in.at[spot(a, l, h, 0)])
 
             @pl.when(jnp.logical_and(line == 0, l > 0))
             def _(h=h):
@@ -435,95 +400,45 @@
 
         outs[a][...] = own[at(a, line, side, wide)].astype(F32)
 
-    passes = {}
-    for a in range(count):
-        for j in range(lines - 1):
-            after = a * lines + min(2 * j + 2, lines - 1) + 3
-            passes.setdefault(after, []).append(functools.partial(passing, a, j))
-        passes.setdefault(a * lines + lines + 3, []).append(functools.partial(final, a))
-    for step in range(len(items) + 4):
-        if step < len(items):
-            stage_one(step)
-        if 0 <= step - 1 < len(items):
-            stage_two(*items[step - 1])
-        if 0 <= step - 2 < len(items):
-            stage_three(*items[step - 2])
-        for action in passes.get(step, []):
-            action()
-    if small:
-        small_finish()
-    for n in range(4 * len(items) - ring, 4 * len(items)):
-        core_copy(n).wait_send()
-    for a, l in items:
-        for j in range(2):
-            wide_one(a, l, j).wait_send()
-            side_one(a, l, j).wait_send()
-        side_two(a, l).wait_send()
-        wide_two(a, l).wait_send()
-        for h in range(2):
-
-            @pl.when(jnp.logical_and(has_above, line < l))
-            def _(h=h):
-                up_copy(a, l, h).wait_send()
-
-            @pl.when(jnp.logical_and(has_below, line > l))
-            def _(h=h):
-                down_copy(a, l, h).wait_send()
-
-
-def kernel_total(place, partials, small_value, number):
-    n_row, n_col = lax.axis_size("row"), lax.axis_size("col")
-    lines, count = n_col // 2, len(partials)
-    blocks, _, tokens = place.shape
-    local_experts, rows, width = partials[0][0].shape
-    capacity = rows // blocks
-    small = small_value is not None
-    out_shape = [jax.ShapeDtypeStruct((tokens, width), F32)] * count
-    hbm, vmem = pl.BlockSpec(memory_space=pl.ANY), pl.BlockSpec(memory_space=pltpu.VMEM)
-    in_specs = [vmem] + [hbm] * count + [vmem] * (2 * count)
-    operands = [place]
-    operands += [p[0].reshape(local_experts, blocks, capacity, width) for p in partials]
-    operands += [p[1] for p in partials] + [p[2] for p in partials]
-    if small:
-        in_specs.append(vmem)
-        out_shape.append(jax.ShapeDtypeStruct(small_value.shape, small_value.dtype))
-        operands.append(small_value)
-    dma = pltpu.SemaphoreType.DMA
-    scratch = [
-        pltpu.VMEM((count * 4 * lines, tokens, width), BF16),
-        pltpu.VMEM((8, tokens, width), BF16),
-        pltpu.VMEM((count * 3 * lines, tokens // 2, width), BF16),
-        pltpu.VMEM((count * 3 * lines, tokens // 2, width), BF16),
-        pltpu.VMEM((count * 2 * lines, tokens // 2, width), BF16),
-        pltpu.VMEM((count * 2 * lines, tokens // 2, width), BF16),
-        pltpu.VMEM((4, local_experts, capacity, width), BF16),
-        pltpu.VMEM((4, tokens, width), BF16),
-        dma((4,)),
-        pltpu.SemaphoreType.REGULAR,
-        *[dma((count * 4 * lines,))] * 2,
-        *[dma((count * 3 * lines,))] * 4,
-        *[dma((count * 2 * lines,))] * 4,
-    ]
-    if small:
-        scratch += [dma((n_row * n_col,))] * 2
-    return pl.pallas_call(
-        functools.partial(scatter_body, lines, count, small),
-        out_shape=out_shape,
-        in_specs=in_specs,
-        out_specs=[pl.BlockSpec(memory_space=pltpu.VMEM)] * len(out_shape),
-        scratch_shapes=scratch,
-        compiler_params=pltpu.CompilerParams(
-            collective_id=number, has_side_effects=True, vmem_limit_bytes=VMEM_LIMIT
-        ),
-        name=f"scatter_{number}",
-    )(*operands)
-
-
-def kernel_fits(rows, width, count):
-    n_row, n_col = lax.axis_size("row"), lax.axis_size("col")
-    tokens = rows // (n_row * n_col)
-    held = count * n_col * 2 * width * tokens * 13 // 4
-    return n_row == 4 and n_col % 2 == 0 and tokens % 32 == 0 and held < 58 * 1024 * 1024
+    def one(t):
+        stage_one(t)
+
+    def two(t):
+        stage_two(*items[t])
+
+    def three(t):
+        stage_three(*items[t])
+
+    def along(j):
+        passing(0, j)
+
+    def last(_):
+        final(0)
+
+    def finish():
+        for n in range(4 * len(items) - ring, 4 * len(items)):
+            core_copy(n).wait_send()
+        for a, l in items:
+            for h in range(2):
+                for j in range(1 if ways[h] else 2):
+                    wide_copy(a, l, side if ways[h] else j, h).wait_send()
+                for j in range(2 if ways[h] else 1):
+                    side_copy(a, l, j if ways[h] else wide, h).wait_send()
+
+                @pl.when(jnp.logical_and(has_above, line < l))
+                def _(h=h, a=a, l=l):
+                    up_copy(a, l, h).wait_send()
+
+                @pl.when(jnp.logical_and(has_below, line > l))
+                def _(h=h, a=a, l=l):
+                    down_copy(a, l, h).wait_send()
+
+    return start, (one, two, three, along, last), finish
+
+
+def kernel_fits(place_shape, width):
+    blocks, _, tokens = place_shape
+    return tokens % 32 == 0 and 4 * blocks * tokens * width <= 40 * 1024 * 1024
 
 
 def row_mates(wide, core, line, side):
@@ -840,10 +755,61 @@
     return start, step, finish
 
 
+def pick_plan(lines, place_ref, rows_ref, slots_ref, rows_in, slots_out, load_sem, store_sem):
+    ring, tokens = rows_in.shape[:2]
+    blocks = place_ref.shape[0]
+    chunks = lines + 1
+    per_step = -(-blocks // chunks)
+
+    def load(b):
+        return pltpu.make_async_copy(
+            rows_ref.at[pl.ds(pl.multiple_of(b * tokens, tokens), tokens)],
+            rows_in.at[lax.rem(b, ring)],
+            load_sem.at[lax.rem(b, ring)],
+        )
+
+    def store(b):
+        return pltpu.make_async_copy(
+            slots_out.at[lax.rem(b, ring)], slots_ref.at[:, b], store_sem.at[lax.rem(b, ring)]
+        )
+
+    def start():
+        for b in range(ring - 1):
+            load(b).start()
+
+    def step(dist):
+        @pl.loop((dist - 1) * per_step, min(dist * per_step, blocks))
+        def _(b):
+            @pl.when(b + ring - 1 < blocks)
+            def _():
+                load(b + ring - 1).start()
+
+            load(b).wait()
+
+            @pl.when(b >= ring)
+            def _():
+                store(b - ring).wait()
+
+            slot = lax.rem(b, ring)
+            picked = matmul(place_ref[b], rows_in[slot])
+            slots_out[slot] = picked.astype(BF16).reshape(slots_out.shape[1:])
+            store(b).start()
+
+    def finish():
+        for b in range(blocks - ring, blocks):
+            store(b).wait()
+
+    return start, step, finish
+
+
 def gather_body(lines, dims, flips, ways, kinds, *refs):
-    has_row, has_every, has_small = kinds
+    has_row, has_every, has_small, has_pick = kinds
     count = len(dims)
     outputs = count + has_row + has_every + has_small
+    if has_pick:
+        pick_refs = refs[outputs : outputs + 2]
+        pick_refs += refs[2 * outputs + 2 : 2 * outputs + 3] + refs[-4:]
+        refs = refs[:outputs] + refs[outputs + 2 : 2 * outputs + 2] + refs[2 * outputs + 3 : -4]
     ins, outs, sems = refs[:outputs], refs[outputs : 2 * outputs], list(refs[2 * outputs :])
     spots = places()
     wide, core, line, side = spots
@@ -873,6 +839,8 @@
     if has_small:
         small_start, small_finish = small_exchange(ins[at], outs[at], *take(2), False)
         small_start()
+    if has_pick:
+        plans.append(pick_plan(lines, *pick_refs))
     for start, _, _ in plans:
         start()
     for dist in range(1, lines + 2):
@@ -884,7 +852,9 @@
         finish()
 
 
-def kernel_gather(col_values, dims, flips, row_value, every_value, ways, small_value, number):
+def kernel_gather(
+    col_values, dims, flips, row_value, every_value, ways, small_value, number, pick=None
+):
     n_row, n_col = lax.axis_size("row"), lax.axis_size("col")
     lines, count, total = n_col // 2, len(dims), n_row * n_col
     hbm, vmem = pl.BlockSpec(memory_space=pl.ANY), pl.BlockSpec(memory_space=pltpu.VMEM)
@@ -916,7 +886,21 @@
         out_specs.append(vmem)
         out_shape.append(jax.ShapeDtypeStruct((total, *small_value.shape), small_value.dtype))
         scratch += [dma((total,))] * 2
-    kinds = tuple(value is not None for value in (row_value, every_value, small_value))
+    if pick is not None:
+        place, rows, local_experts = pick
+        blocks, slots, tokens = place.shape
+        shape = (local_experts, slots // local_experts, rows.shape[1])
+        operands += [place, rows]
+        in_specs += [vmem, hbm]
+        out_specs.append(hbm)
+        out_shape.append(jax.ShapeDtypeStruct((shape[0], blocks, *shape[1:]), BF16))
+        scratch += [
+            pltpu.VMEM((4, tokens, rows.shape[1]), BF16),
+            pltpu.VMEM((4, *shape), BF16),
+            dma((4,)),
+            dma((4,)),
+        ]
+    kinds = tuple(value is not None for value in (row_value, every_value, small_value, pick))
     return pl.pallas_call(
         functools.partial(gather_body, lines, tuple(dims), tuple(flips), ways, kinds),
         out_shape=out_shape,
@@ -928,7 +912,7 @@
     )(*operands)
 
 
-def mixed_total_body(lines, dims, flips, *refs):
+def mixed_total_plan(lines, dims, flips, spots, refs):
     count = len(dims)
     cols, row_ref, refs = refs[:count], refs[count], refs[count + 1 :]
     col_outs, row_out, refs = refs[:count], refs[count], refs[count + 1 :]
@@ -940,17 +924,13 @@
     row_load, core_send, core_recv, wide_send, wide_recv = refs[:5]
     if count:
         load_sem, side_send, side_recv, up_send, up_recv, down_send, down_recv = refs[5:12]
-    wide, core, line, side = places()
+    wide, core, line, side = spots
     core_mate, wide_mate = row_mates(wide, core, line, side)
     side_mate = to_place(wide, core, line, 1 - side)
     above = to_place(wide, core, line + 1, side)
     below = to_place(wide, core, line - 1, side)
     has_above = line < lines - 1
     has_below = line > 0
-    partners = [(core >= 0, core_mate), (core >= 0, wide_mate)]
-    if count:
-        partners += [(core >= 0, side_mate), (has_above, above), (has_below, below)]
-    greet(partners, False)
     tokens = row_out.shape[0]
 
     def core_copy(w):
@@ -1004,23 +984,6 @@
     def sides(m):
         return (1 - side, side) if flips[m] else (side,)
 
-    for w in range(2):
-        core_copy(w).start()
-        row_loaded(w).start()
-    items = [(m, l) for l in (line_order(lines) if count else []) for m in range(count)]
-    for m, l in items:
-        for s in sides(m):
-            loaded(m, l, s).start()
-        if not flips[m]:
-            side_copy(m, l).start()
-    for j in range(2):
-        w = wide if j else 1 - wide
-        row_loaded(w).wait()
-        core_copy(w).wait_recv()
-        row_own[w] = (row_own[w].astype(F32) + row_core[w].astype(F32)).astype(BF16)
-        if j == 0:
-            wide_copy.start()
-
     def add(m, l, s, other):
         mine = own_at(m, l, s)
         mine[...] = (mine[...].astype(F32) + other.astype(F32)).astype(BF16)
@@ -1086,85 +1049,331 @@
     flipped = [m for m in range(count) if flips[m]]
     straight = [m for m in range(count) if not flips[m]]
     order = line_order(lines)
-    for l in order:
-        for m in flipped:
-            near(m, l)
-    if count:
-        for step in range(lines + 2):
-            if step < lines:
-                for m in straight:
-                    near(m, order[step])
-            if step < lines - 1:
+    def start():
+        for w in range(2):
+            core_copy(w).start()
+            row_loaded(w).start()
+        items = [(m, l) for l in (line_order(lines) if count else []) for m in range(count)]
+        for m, l in items:
+            for s in sides(m):
+                loaded(m, l, s).start()
+            if not flips[m]:
+                side_copy(m, l).start()
+
+    def step_on(step):
+        if step == 0:
+            for j in range(2):
+                w = wide if j else 1 - wide
+                row_loaded(w).wait()
+                core_copy(w).wait_recv()
+                row_own[w] = (row_own[w].astype(F32) + row_core[w].astype(F32)).astype(BF16)
+                if j == 0:
+                    wide_copy.start()
+            for l in order:
                 for m in flipped:
-                    passing(m, step)
-            if step == lines - 1:
-                for m in flipped:
-                    final(m)
-            if 2 <= step < lines + 1:
-                for m in straight:
-                    passing(m, step - 2)
-            if step == lines + 1:
-                for m in straight:
-                    final(m)
-    wide_copy.wait()
-    row_out[...] = row_own[wide].astype(F32) + row_wide[...].astype(F32)
-    for w in range(2):
-        core_copy(w).wait_send()
-    for m in range(count):
-        if flips[m]:
-            side_copy(m, line).wait()
-            add(m, line, side, side_ins[m][0])
-        col_outs[m][...] = own_at(m, line, side)[...].astype(F32)
-        for l in range(lines):
-            if not flips[m]:
-                side_copy(m, l).wait_send()
-            for s in sides(m):
-
-                @pl.when(jnp.logical_and(has_above, line < l))
-                def _(m=m, l=l, s=s):
-                    line_copy(m, l, s, True).wait_send()
-
-                @pl.when(jnp.logical_and(has_below, line > l))
-                def _(m=m, l=l, s=s):
-                    line_copy(m, l, s, False).wait_send()
-
-
-def mixed_total(col_values, dims, flips, row_value, number):
+                    near(m, l)
+        if step == 1:
+            wide_copy.wait_recv()
+            row_out[...] = row_own[wide].astype(F32) + row_wide[...].astype(F32)
+        if not count:
+            return
+        if step < lines:
+            for m in straight:
+                near(m, order[step])
+        if step < lines - 1:
+            for m in flipped:
+                passing(m, step)
+        if step == lines - 1:
+            for m in flipped:
+                final(m)
+        if 2 <= step < lines + 1:
+            for m in straight:
+                passing(m, step - 2)
+        if step == lines + 1:
+            for m in straight:
+                final(m)
+
+    def finish():
+        wide_copy.wait_send()
+        for w in range(2):
+            core_copy(w).wait_send()
+        for m in range(count):
+            if flips[m]:
+                side_copy(m, line).wait()
+                add(m, line, side, side_ins[m][0])
+            col_outs[m][...] = own_at(m, line, side)[...].astype(F32)
+            for l in range(lines):
+                if not flips[m]:
+                    side_copy(m, l).wait_send()
+                for s in sides(m):
+
+                    @pl.when(jnp.logical_and(has_above, line < l))
+                    def _(m=m, l=l, s=s):
+                        line_copy(m, l, s, True).wait_send()
+
+                    @pl.when(jnp.logical_and(has_below, line > l))
+                    def _(m=m, l=l, s=s):
+                        line_copy(m, l, s, False).wait_send()
+
+    def own_rows(m, rows):
+        return own_at(m, line, side).at[rows]
+
+    return start, step_on, finish, lines + 2, own_rows
+
+
+def total_order(lines, stages, mixed_step):
+    one, two, three, along, last = stages
+    order = []
+    lag = 3 if mixed_step else 2
+    late_two = [(two, lines - 1)]
+    for k in range(lines):
+        order.append((one, k))
+        if mixed_step:
+            order.append((mixed_step, k))
+        if k >= lag and lag == 3:
+            order.append((three, k - lag))
+        if k >= 1:
+            order.append((two, k - 1))
+        if k >= lag and lag == 2:
+            order.append((three, k - lag))
+    rest = [(three, k) for k in range(max(0, lines - lag), lines)]
+    if mixed_step:
+        order += rest[:-2] + [(mixed_step, lines)]
+        if lines >= 4:
+            order.append((along, 0))
+        order += rest[-2:-1] + late_two + [(mixed_step, lines + 1)] + rest[-1:]
+    else:
+        order += late_two
+        if lines >= 4:
+            order.append((along, 0))
+        order += rest
+    order += [(along, j) for j in range(1 if lines >= 4 else 0, lines - 1)]
+    return order + [(last, 0)]
+
+
+def last_plan(row_out, scaled_ref, gains_ref, sums_ref, down_ref, scratch):
+    row_in, held, summed = scratch[:3]
+    row_send, row_recv, col_send, col_recv, down_send, down_recv, local_sem = scratch[3:]
+    n_row, n_col = lax.axis_size("row"), lax.axis_size("col")
+    row, col = lax.axis_index("row"), lax.axis_index("col")
+    rows = [{"row": lax.rem(row + d, n_row), "col": col} for d in range(1, n_row)]
+    cols = [{"row": row, "col": lax.rem(col + d, n_col)} for d in range(1, n_col)]
+    size = down_ref.shape[0] // n_row
+
+    def row_copy(d, source):
+        return remote(held, row_in.at[source], row_send.at[d], row_recv.at[source], rows[d])
+
+    def col_copy(d, source):
+        return remote(summed, sums_ref.at[source], col_send.at[d], col_recv.at[source], cols[d])
+
+    def down_copy(d, source, value):
+        return remote(
+            value,
+            strip(down_ref, 0, source, size),
+            down_send.at[d],
+            down_recv.at[source],
+            rows[d],
+        )
+
+    def first():
+        held[...] = gains_ref[...]
+        held[0:1, :] = jnp.sum(row_out[...] * scaled_ref[...], axis=0, keepdims=True)
+        for d in range(n_row - 1):
+            row_copy(d, row).start()
+
+    def second():
+        total = held[...]
+        for d in range(n_row - 1):
+            source = rows[d]["row"]
+            row_copy(d, source).wait_recv()
+            total = total + row_in[source]
+        summed[...] = total
+        sums_ref[col] = total
+        for d in range(n_col - 1):
+            col_copy(d, col).start()
+
+    def finish(value):
+        local = pltpu.make_async_copy(value, strip(down_ref, 0, row, size), local_sem)
+        local.start()
+        for d in range(n_row - 1):
+            down_copy(d, row, value).start()
+        for d in range(n_col - 1):
+            col_copy(d, cols[d]["col"]).wait_recv()
+            col_copy(d, col).wait_send()
+        for d in range(n_row - 1):
+            row_copy(d, row).wait_send()
+            down_copy(d, rows[d]["row"], value).wait_recv()
+            down_copy(d, row, value).wait_send()
+        local.wait()
+
+    return rows + cols, first, second, finish
+
+
+def total_body(lines, dims, flips, ways, kinds, *refs):
+    has_mixed, has_every, has_small, has_last = kinds
+    count = len(dims)
+    spots = places()
+    wide, core, line, side = spots
+    core_mate, wide_mate = row_mates(*spots)
+    partners = [(core >= 0, core_mate), (core >= 0, wide_mate)]
+    if count or has_every:
+        partners += [
+            (core >= 0, to_place(wide, core, line, 1 - side)),
+            (line < lines - 1, to_place(wide, core, line + 1, side)),
+            (line > 0, to_place(wide, core, line - 1, side)),
+        ]
+    refs = list(refs)
+
+    def take(n):
+        taken, refs[:] = refs[:n], refs[n:]
+        return taken
+
+    mixed = (count + 1) * has_mixed
+    mixed_ins, every_ins, small_ins = take(mixed), take(4 * has_every), take(has_small)
+    last_ins = take(2 * has_last)
+    mixed_outs, every_outs, small_outs = take(mixed), take(has_every), take(has_small)
+    if has_last:
+        last_outs = take(2)
+        down_rows = last_outs[1].shape[0] // lax.axis_size("row")
+        peers, last_first, last_second, last_finish = last_plan(
+            mixed_outs[-1], *last_ins, *last_outs, take(10)
+        )
+        partners = [(core >= 0, peer) for peer in peers]
+    greet(partners, has_small)
+    if has_small:
+        small_start, small_finish = small_exchange(*small_ins, *small_outs, *take(2), True)
+        small_start()
+    mixed_step = None
+    if has_every:
+        every_start, stages, every_finish = every_total_plan(
+            lines, ways, spots, *every_ins, *every_outs, take(20)
+        )
+        every_start()
+    if has_mixed:
+        mixed_start, mixed_go, mixed_finish, mixed_steps, own_rows = mixed_total_plan(
+            lines, dims, flips, spots, mixed_ins + mixed_outs + refs
+        )
+        mixed_start()
+
+        def mixed_step(step):
+            mixed_go(step)
+            if has_last and step == 1:
+                last_first()
+            if has_last and step == lines:
+                last_second()
+
+    if has_every:
+        for action, index in total_order(lines, stages, mixed_step):
+            action(index)
+    else:
+        for step in range(mixed_steps):
+            mixed_step(step)
+    if has_last:
+        last_finish(own_rows(1, pl.ds(mixed_outs[1].shape[0] - down_rows, down_rows)))
+    if has_mixed:
+        mixed_finish()
+    if has_every:
+        every_finish()
+    if has_small:
+        small_finish()
+
+
+def kernel_total(
+    col_values, dims, flips, row_value, every_value, ways, small_value, number, last_value=None
+):
     n_row, n_col = lax.axis_size("row"), lax.axis_size("col")
     lines, count = n_col // 2, len(dims)
-    tokens, width = row_value.shape[0] // n_row, row_value.shape[1]
     hbm, vmem = pl.BlockSpec(memory_space=pl.ANY), pl.BlockSpec(memory_space=pltpu.VMEM)
-    blocks = []
-    for value, dim in zip(col_values, dims):
-        shape = list(value.shape)
-        shape[dim] //= n_col
-        blocks.append(tuple(shape))
     dma = pltpu.SemaphoreType.DMA
-    scratch = [
-        pltpu.VMEM((2, tokens, width), BF16),
-        pltpu.VMEM((2, tokens, width), BF16),
-        pltpu.VMEM((tokens, width), BF16),
-    ]
-    doubled = [(lines, 2) if flip else (lines,) for flip in flips]
-    side_held = [(1,) if flip else (lines,) for flip in flips]
-    for lead in (doubled, side_held, doubled, doubled):
-        scratch += [pltpu.VMEM((*d, *shape), BF16) for d, shape in zip(lead, blocks)]
-    scratch += [dma((2,)), dma((2,)), dma((2,)), dma((1,)), dma((1,))]
-    if count:
-        scratch += [dma((2 * count * lines,))] + [dma((count * lines,))] * 2
-        scratch += [dma((2 * count * lines,))] * 4
+    operands, in_specs, out_shape, scratch = [], [], [], []
+    if row_value is not None:
+        operands += [*col_values, row_value]
+        in_specs += [hbm] * (count + 1)
+        blocks = []
+        for value, dim in zip(col_values, dims):
+            shape = list(value.shape)
+            shape[dim] //= n_col
+            blocks.append(tuple(shape))
+        tokens, width = row_value.shape[0] // n_row, row_value.shape[1]
+        out_shape += [jax.ShapeDtypeStruct(shape, F32) for shape in blocks]
+        out_shape.append(jax.ShapeDtypeStruct((tokens, width), F32))
+    every_scratch, small_scratch = [], []
+    if every_value is not None:
+        place, slots, extra, weight = every_value
+        n_blocks, _, tokens = place.shape
+        local_experts, rows, width = slots.shape
+        capacity = rows // n_blocks
+        operands += [place, slots.reshape(local_experts, n_blocks, capacity, width), extra, weight]
+        in_specs += [vmem, hbm, vmem, vmem]
+        out_shape.append(jax.ShapeDtypeStruct((tokens, width), F32))
+        half = (tokens // 2, width)
+        every_scratch = [
+            pltpu.VMEM((4 * lines, tokens, width), BF16),
+            pltpu.VMEM((8, tokens, width), BF16),
+            pltpu.VMEM((4 * lines, *half), BF16),
+            pltpu.VMEM((4 * lines, *half), BF16),
+            pltpu.VMEM((2 * lines, *half), BF16),
+            pltpu.VMEM((2 * lines, *half), BF16),
+            pltpu.VMEM((4, local_experts, capacity, width), BF16),
+            pltpu.VMEM((4, tokens, width), BF16),
+            dma((4,)),
+            pltpu.SemaphoreType.REGULAR,
+            *[dma((4 * lines,))] * 6,
+            *[dma((2 * lines,))] * 4,
+        ]
+    if small_value is not None:
+        operands.append(small_value)
+        in_specs.append(vmem)
+        out_shape.append(jax.ShapeDtypeStruct(small_value.shape, small_value.dtype))
+        small_scratch = [dma((n_row * n_col,))] * 2
+    if last_value is not None:
+        scaled, gains, down_rows = last_value
+        operands += [scaled, gains]
+        in_specs += [vmem, vmem]
+        out_shape += [
+            jax.ShapeDtypeStruct((n_col, *gains.shape), F32),
+            jax.ShapeDtypeStruct((n_row * down_rows, blocks[1][1]), BF16),
+        ]
+        scratch += [
+            pltpu.VMEM((n_row, *gains.shape), F32),
+            pltpu.VMEM(gains.shape, F32),
+            pltpu.VMEM(gains.shape, F32),
+            dma((n_row - 1,)),
+            dma((n_row,)),
+            dma((n_col - 1,)),
+            dma((n_col,)),
+            dma((n_row - 1,)),
+            dma((n_row,)),
+            dma,
+        ]
+    scratch += small_scratch + every_scratch
+    if row_value is not None:
+        tokens, width = row_value.shape[0] // n_row, row_value.shape[1]
+        scratch += [
+            pltpu.VMEM((2, tokens, width), BF16),
+            pltpu.VMEM((2, tokens, width), BF16),
+            pltpu.VMEM((tokens, width), BF16),
+        ]
+        doubled = [(lines, 2) if flip else (lines,) for flip in flips]
+        side_held = [(1,) if flip else (lines,) for flip in flips]
+        for lead in (doubled, side_held, doubled, doubled):
+            scratch += [pltpu.VMEM((*d, *shape), BF16) for d, shape in zip(lead, blocks)]
+        scratch += [dma((2,)), dma((2,)), dma((2,)), dma((1,)), dma((1,))]
+        if count:
+            scratch += [dma((2 * count * lines,))] + [dma((count * lines,))] * 2
+            scratch += [dma((2 * count * lines,))] * 4
+    kinds = tuple(v is not None for v in (row_value, every_value, small_value, last_value))
     return pl.pallas_call(
-        functools.partial(mixed_total_body, lines, tuple(dims), tuple(flips)),
-        out_shape=[jax.ShapeDtypeStruct(shape, F32) for shape in blocks]
-        + [jax.ShapeDtypeStruct((tokens, width), F32)],
-        in_specs=[hbm] * (count + 1),
-        out_specs=[vmem] * (count + 1),
+        functools.partial(total_body, lines, tuple(dims), tuple(flips), ways, kinds),
+        out_shape=out_shape,
+        in_specs=in_specs,
+        out_specs=[vmem] * len(out_shape),
         scratch_shapes=scratch,
         compiler_params=pltpu.CompilerParams(
             collective_id=number, has_side_effects=True, vmem_limit_bytes=VMEM_LIMIT
         ),
-        name=f"mixed_total_{number}",
-    )(*col_values, row_value)
+        name=f"total_{number}",
+    )(*operands)
 
 
 def row_sum_body(value_ref, out_ref, held, core_in, wide_in, *sems):
@@ -1241,102 +1450,13 @@
     )(value)
 
 
-def finish_body(value_ref, gains_ref, out_ref, sums_ref, row_in, held, *sems):
-    local_sem, value_send, value_recv, row_send, row_recv, col_send, col_recv = sems
-    n_row, n_col = lax.axis_size("row"), lax.axis_size("col")
-    row, col = lax.axis_index("row"), lax.axis_index("col")
-    rows = [{"row": lax.rem(row + d, n_row), "col": col} for d in range(1, n_row)]
-    cols = [{"row": row, "col": lax.rem(col + d, n_col)} for d in range(1, n_col)]
-    greet([(row >= 0, partner) for partner in rows + cols], False)
-    tokens = value_ref.shape[0]
-
-    def value_copy(d, source):
-        return remote(
-            value_ref,
-            strip(out_ref, 0, source, tokens),
-            value_send.at[d],
-            value_recv.at[source],
-            rows[d],
-        )
-
-    def row_copy(d, source):
-        return remote(gains_ref, row_in.at[source], row_send.at[d], row_recv.at[source], rows[d])
-
-    def col_copy(d, source):
-        return remote(held, sums_ref.at[source], col_send.at[d], col_recv.at[source], cols[d])
-
-    for d in range(n_row - 1):
-        row_copy(d, row).start()
-    for d in range(n_row - 1):
-        value_copy(d, row).start()
-    local = pltpu.make_async_copy(value_ref, strip(out_ref, 0, row, tokens), local_sem)
-    local.start()
-    total = gains_ref[...]
-    for d in range(n_row - 1):
-        source = rows[d]["row"]
-        row_copy(d, source).wait_recv()
-        total = total + row_in[source]
-    held[...] = total
-    for d in range(n_col - 1):
-        col_copy(d, col).start()
-    sums_ref[col] = total
-    for d in range(n_row - 1):
-        value_copy(d, rows[d]["row"]).wait_recv()
-        value_copy(d, row).wait_send()
-        row_copy(d, row).wait_send()
-    for d in range(n_col - 1):
-        col_copy(d, cols[d]["col"]).wait_recv()
-        col_copy(d, col).wait_send()
-    local.wait()
-
-
-def kernel_finish(value, gains, number):
-    n_row, n_col = lax.axis_size("row"), lax.axis_size("col")
-    dma = pltpu.SemaphoreType.DMA
-    vmem = pl.BlockSpec(memory_space=pltpu.VMEM)
-    return pl.pallas_call(
-        finish_body,
-        out_shape=[
-            jax.ShapeDtypeStruct((n_row * value.shape[0], value.shape[1]), value.dtype),
-            jax.ShapeDtypeStruct((n_col, *gains.shape), gains.dtype),
-        ],
-        in_specs=[vmem, vmem],
-        out_specs=[vmem, vmem],
-        scratch_shapes=[
-            pltpu.VMEM((n_row, *gains.shape), gains.dtype),
-            pltpu.VMEM(gains.shape, gains.dtype),
-            dma,
-            dma((n_row - 1,)),
-            dma((n_row,)),
-            dma((n_row - 1,)),
-            dma((n_row,)),
-            dma((n_col - 1,)),
-            dma((n_col,)),
-        ],
-        compiler_params=pltpu.CompilerParams(collective_id=number, has_side_effects=True),
-        name=f"finish_{number}",
-    )(value, gains)
-
-
-def total_every(place, partials, small_value, number):
-    blocks, slot_count, tokens = place.shape
-    if kernel_fits(blocks * tokens, partials[0][0].shape[2], len(partials)):
-        return kernel_total(place, partials, small_value, number)
-    capacity = partials[0][0].shape[1] // blocks
-    exchanged = lax.all_to_all(small_value, EVERY, split_axis=0, concat_axis=0, tiled=True)
-    return *[every_total(combine_rows(place, *p, capacity)) for p in partials], exchanged
-
-
-def mixed_fits(col_values):
-    n_row, lines = lax.axis_size("row"), lax.axis_size("col") // 2
-    return n_row == 4 and (not col_values or (lax.axis_size("col") % 2 == 0 and lines <= 8))
-
-
-def gather(col_values, dims, flips, row_value, every_value, ways, small_value, number):
+def gather(
+    col_values, dims, flips, row_value, every_value, ways, small_value, number, pick=None
+):
     fits = not col_values and every_value is None or lax.axis_size("col") in (4, 6, 8, 10)
     if lax.axis_size("row") == 4 and fits:
         return kernel_gather(
-            col_values, dims, flips, row_value, every_value, ways, small_value, number
+            col_values, dims, flips, row_value, every_value, ways, small_value, number, pick
         )
     out = [lax.all_gather(v, "col", axis=d, tiled=True) for v, d in zip(col_values, dims)]
     if row_value is not None:
@@ -1345,13 +1465,66 @@
         out.append(every_token(every_value))
     if small_value is not None:
         out.append(every_token(small_value[None]))
+    if pick is not None:
+        out.append(pick_rows(*pick))
     return out
 
 
-def total_mixed(col_values, dims, flips, row_value, number):
-    if mixed_fits(col_values):
-        return mixed_total(col_values, dims, flips, row_value, number)
-    return *[col_total(v, d) for v, d in zip(col_values, dims)], row_total(row_value)
+def pick_body(capacity, place_ref, rows_ref, slots_ref):
+    picked = matmul(place_ref[0], rows_ref[...]).astype(BF16)
+    slots_ref[:, 0] = picked.reshape(-1, capacity, picked.shape[-1])
+
+
+def pick_rows(place, rows, local_experts):
+    blocks, slots, tokens = place.shape
+    capacity, width = slots // local_experts, rows.shape[1]
+    return pl.pallas_call(
+        functools.partial(pick_body, capacity),
+        grid=(blocks,),
+        in_specs=[
+            pl.BlockSpec((1, slots, tokens), lambda i: (i, 0, 0)),
+            pl.BlockSpec((tokens, width), lambda i: (i, 0)),
+        ],
+        out_specs=pl.BlockSpec((local_experts, 1, capacity, width), lambda i: (0, i, 0, 0)),
+        out_shape=jax.ShapeDtypeStruct((local_experts, blocks, capacity, width), BF16),
+        name="pick_rows",
+    )(place, rows)
+
+
+def total(
+    col_values, dims, flips, row_value, every_value, ways, small_value, number, last_value=None
+):
+    fits = lax.axis_size("row") == 4
+    if col_values or every_value is not None:
+        fits = fits and lax.axis_size("col") in (4, 6, 8, 10)
+    if every_value is not None:
+        fits = fits and kernel_fits(every_value[0].shape, every_value[1].shape[2])
+    if fits:
+        return kernel_total(
+            col_values,
+            dims,
+            flips,
+            row_value,
+            every_value,
+            ways,
+            small_value,
+            number,
+            last_value,
+        )
+    out = [col_total(v, d) for v, d in zip(col_values, dims)]
+    if row_value is not None:
+        out.append(row_total(row_value))
+    if every_value is not None:
+        capacity = every_value[1].shape[1] // every_value[0].shape[0]
+        out.append(every_total(combine_rows(*every_value, capacity)))
+    if small_value is not None:
+        out.append(lax.all_to_all(small_value, EVERY, split_axis=0, concat_axis=0, tiled=True))
+    if last_value is not None:
+        scaled, gains, down_rows = last_value
+        part = jnp.sum(out[len(dims)] * scaled, axis=0)
+        out.append(lax.psum(gains.at[0].set(part), EVERY)[None])
+        out.append(token_rows(out[1][-down_rows:].astype(BF16)))
+    return out
 
 
 def padded_rows(values):
@@ -1375,7 +1548,6 @@
     both_ref,
     down_ref,
     xs_ref,
-    gs_ref,
     hidden_ref,
     grad_ref,
     dboth_ref,
@@ -1384,9 +1556,8 @@
     tokens = place_ref.shape[2]
     for block in range(group):
         rows = slice(block * tokens, (block + 1) * tokens)
-        for source, slots in ((x_ref, xs_ref), (g_ref, gs_ref)):
-            picked = matmul(place_ref[block], source[rows, :])
-            slots[:, block] = picked.astype(BF16).reshape(-1, capacity, picked.shape[-1])
+        picked = matmul(place_ref[block], x_ref[rows, :])
+        xs_ref[:, block] = picked.astype(BF16).reshape(-1, capacity, picked.shape[-1])
     half = down_ref.shape[0]
     both = outer_cols(x_ref[...], both_ref[...])
     act, slope = silu_parts(both[:, :half])
@@ -1427,7 +1598,7 @@
         return pl.BlockSpec((group * tokens, size), lambda i: (i, 0))
 
     rows = blocks * tokens
-    xs, gs, hidden, grads, dboth, ddown = pl.pallas_call(
+    xs, hidden, grads, dboth, ddown = pl.pallas_call(
         functools.partial(tokens_body, group, capacity),
         grid=(blocks // group,),
         in_specs=[
@@ -1439,14 +1610,12 @@
         ],
         out_specs=[
             slot_block,
-            slot_block,
             hidden_block(half),
             hidden_block(2 * half),
             whole(2 * half),
             whole(half),
         ],
         out_shape=[
-            slot_shape,
             slot_shape,
             jax.ShapeDtypeStruct((rows, half), BF16),
             jax.ShapeDtypeStruct((rows, 2 * half), BF16),
@@ -1455,26 +1624,75 @@
         ],
         compiler_params=pltpu.CompilerParams(vmem_limit_bytes=VMEM_LIMIT),
         cost_estimate=pl.CostEstimate(
-            flops=2 * rows * width * (2 * slots + 6 * half),
+            flops=2 * rows * width * (slots + 6 * half),
             bytes_accessed=8 * rows * width,
             transcendentals=rows * half,
         ),
         name="run_tokens",
     )(place, x_all, g_all, both_weight, down_weight)
-    shape = (local_experts, blocks * capacity, width)
-    return xs.reshape(shape), gs.reshape(shape), hidden, grads, dboth, ddown
+    xs = xs.reshape(local_experts, blocks * capacity, width)
+    return xs, hidden, grads, dboth, ddown
 
 
 def experts_body(
-    x_ref, g_ref, gate_ref, wg_ref, wu_ref, wd_ref, y_ref, r_ref, dg_ref, du_ref, dd_ref, gg_ref
+    x_ref,
+    g_ref,
+    gate_ref,
+    wg_ref,
+    wu_ref,
+    wd_ref,
+    y_ref,
+    r_ref,
+    dg_ref,
+    du_ref,
+    dd_ref,
+    gg_ref,
+    both,
+    down,
+    load_sem,
 ):
-    first = pl.program_id(1) == 0
+    expert, part = pl.program_id(0), pl.program_id(1)
+    size = wd_ref.shape[1]
+    held = down.shape[1]
+    width = x_ref.shape[2]
+    slot = lax.rem(expert, 2)
+
+    def loads(e):
+        into = lax.rem(e, 2)
+        return [
+            pltpu.make_async_copy(wg_ref.at[e], both.at[into, pl.ds(0, size)], load_sem.at[into, 0]),
+            pltpu.make_async_copy(
+                wu_ref.at[e], both.at[into, pl.ds(held, size)], load_sem.at[into, 1]
+            ),
+            pltpu.make_async_copy(wd_ref.at[e], down.at[into, pl.ds(0, size)], load_sem.at[into, 2]),
+        ]
+
+    @pl.when(jnp.logical_and(expert == 0, part == 0))
+    def _():
+        if held > size:
+            gap = jnp.zeros((2, held - size, width), BF16)
+            both[:, size:held] = gap
+            both[:, held + size :] = gap
+            down[:, size:] = gap
+        for copy in loads(expert):
+            copy.start()
+
+    @pl.when(part == 0)
+    def _():
+        for copy in loads(expert):
+            copy.wait()
+
+        @pl.when(expert + 1 < pl.num_programs(0))
+        def _():
+            for copy in loads(expert + 1):
+                copy.start()
+
     x = x_ref[0]
     g = g_ref[0]
     gate = gate_ref[0]
-    pre = outer_cols(x, wg_ref[0])
-    lin = outer_cols(x, wu_ref[0])
-    back = outer_cols(g, wd_ref[0])
+    pre_lin = outer_cols(x, both[slot])
+    pre, lin = pre_lin[:, :held], pre_lin[:, held:]
+    back = outer_cols(g, down[slot])
     act, slope = silu_parts(pre)
     hidden = act * lin
     gg_ref[0] = jnp.sum(hidden * back, axis=-1, keepdims=True)
@@ -1482,17 +1700,16 @@
     back = back * gate
     pre_grad = (back * lin * slope).astype(BF16)
     lin_grad = (back * act).astype(BF16)
-    width = x_ref.shape[2]
+    grads = jnp.concatenate([pre_grad, lin_grad], axis=1)
+    first = part == 0
     chunk = 512 if width % 512 == 0 else width
     for start in range(0, width, chunk):
         cols = slice(start, start + chunk)
-        y_ref[0, :, cols] = matmul(hidden, wd_ref[0, :, cols]).astype(BF16)
-        r_ref[0, :, cols] = (
-            matmul(pre_grad, wg_ref[0, :, cols]) + matmul(lin_grad, wu_ref[0, :, cols])
-        ).astype(BF16)
-        d_gate = inner_rows(pre_grad, x_ref[0, :, cols])
-        d_up = inner_rows(lin_grad, x_ref[0, :, cols])
-        d_down = inner_rows(hidden, g_ref[0, :, cols])
+        y_ref[0, :, cols] = matmul(hidden, down[slot, :, cols]).astype(BF16)
+        r_ref[0, :, cols] = matmul(grads, both[slot, :, cols]).astype(BF16)
+        d_gate = inner_rows(pre_grad[:, :size], x_ref[0, :, cols])
+        d_up = inner_rows(lin_grad[:, :size], x_ref[0, :, cols])
+        d_down = inner_rows(hidden[:, :size], g_ref[0, :, cols])
 
         @pl.when(first)
         def _():
@@ -1510,14 +1727,16 @@
 def run_experts(x_slots, g_slots, gates, w_gate, w_up, w_down):
     count, rows, width = x_slots.shape
     hidden = w_down.shape[1]
+    held = hidden + -hidden % 128
     chunk = 512 if rows % 512 == 0 else rows
+    hbm = pl.BlockSpec(memory_space=pl.ANY)
     row_block = pl.BlockSpec((1, chunk, width), lambda e, r: (e, r, 0))
     col_block = pl.BlockSpec((1, chunk, 1), lambda e, r: (e, r, 0))
     out_block = pl.BlockSpec((1, hidden, width), lambda e, r: (e, 0, 0))
     y, r, d_gate, d_up, d_down, dots = pl.pallas_call(
         experts_body,
         grid=(count, rows // chunk),
-        in_specs=[row_block, row_block, col_block, out_block, out_block, out_block],
+        in_specs=[row_block, row_block, col_block, hbm, hbm, hbm],
         out_specs=[row_block, row_block, out_block, out_block, out_block, col_block],
         out_shape=[
             jax.ShapeDtypeStruct((count, rows, width), BF16),
@@ -1526,6 +1745,11 @@
             jax.ShapeDtypeStruct((count, hidden, width), F32),
             jax.ShapeDtypeStruct((count, hidden, width), F32),
             jax.ShapeDtypeStruct((count, rows, 1), F32),
+        ],
+        scratch_shapes=[
+            pltpu.VMEM((2, 2 * held, width), BF16),
+            pltpu.VMEM((2, held, width), BF16),
+            pltpu.SemaphoreType.DMA((2, 3)),
         ],
         compiler_params=pltpu.CompilerParams(vmem_limit_bytes=VMEM_LIMIT),
         cost_estimate=pl.CostEstimate(
@@ -1696,7 +1920,9 @@
         .astype(BF16)
         .reshape(length, heads_local * VD)
     )
-    (attn_total,) = total_mixed([], [], [], matmul(heads_out, output_all).astype(BF16), 6)
+    (attn_total,) = total(
+        [], [], [], matmul(heads_out, output_all).astype(BF16), None, None, None, 6
+    )
     residual = stream + attn_total
 
     scale_two = rms_scale(residual)
@@ -1707,14 +1933,23 @@
     picked = jnp.sum(jnp.where(chosen, logits[:, None, :], 0.0), axis=-1)
     gate_probs = jax.nn.softmax(picked, axis=-1)
 
-    all_normed, all_gates = gather(
-        [], [], [], None, normed_two, (0, 1), padded_rows(gate_probs.T), 2
-    )
+    all_normed, all_gates, grad_slots = gather(
+        [],
+        [],
+        [],
+        None,
+        normed_two,
+        (0, 1),
+        padded_rows(gate_probs.T),
+        2,
+        (place, grad_all, local_experts),
+    )
+    grad_slots = grad_slots.reshape(local_experts, blocks * capacity, width)
     all_gates = all_gates[:, :TOPK]
     gate_here = jnp.sum(jnp.where(named, all_gates[:, :, None, :], 0.0), axis=1)
     slot_gate = jnp.sum(jnp.where(placed, gate_here[:, :, None, :], 0.0), axis=-1)
     slot_gate = slot_gate.transpose(1, 0, 2).reshape(local_experts, blocks * capacity, 1)
-    normed_slots, grad_slots, shared_hidden, shared_both_grad, gate_up_part, down_part = run_tokens(
+    normed_slots, shared_hidden, shared_both_grad, gate_up_part, down_part = run_tokens(
         place, all_normed, grad_all, gate_up_own, down_own, local_experts
     )
     out_slots, rows_slots, expert_gate_grad, expert_up_grad, expert_down_grad, slot_dot = (
@@ -1723,16 +1958,16 @@
 
     slot_dot = slot_dot.reshape(local_experts, blocks, capacity).transpose(1, 0, 2)
     token_dot = jnp.sum(jnp.where(placed, slot_dot[:, :, :, None], 0.0), axis=2)
-    out_total, rows_total, token_dot = total_every(
-        place,
-        [
-            (out_slots, shared_hidden, down_own),
-            (rows_slots, shared_both_grad, gate_up_own),
-        ],
+    rows_total, token_dot = total(
+        [],
+        [],
+        [],
+        None,
+        (place, rows_slots, shared_both_grad, gate_up_own),
+        (0, 1),
         token_dot,
         3,
     )
-    layer_out = (residual + out_total).astype(BF16).reshape(1, own_rows, width)
     shared_back = jnp.concatenate(
         [gate_up_part.reshape(2, shared_held, width), down_part[None]], axis=0
     )[:, :shared_cols].astype(BF16)
@@ -1815,15 +2050,35 @@
     )
     input_part = outer_cols(query_full, query_all) + matmul(own_down_grad, down_all)
     input_part, shared_back = lax.optimization_barrier((input_part, shared_back))
-    query_grad, output_down_grad, latent_up_grad, normed_one_grad = total_mixed(
+    gains = jnp.stack(
+        [
+            jnp.zeros_like(second_gain_part),
+            second_gain_part,
+            jnp.pad(latent_gain_part, (0, width - LATENT)),
+        ]
+    )
+    gains = padded_rows(gains)
+    (
+        query_grad,
+        output_down_grad,
+        latent_up_grad,
+        normed_one_grad,
+        out_total,
+        all_gains,
+        down_total,
+    ) = total(
         [inner_rows(seq_normed, query_full).astype(BF16), output_down_part, expand_part.astype(BF16)],
         [0, 1, 0],
         [False, False, True],
         input_part.astype(BF16),
+        (place, out_slots, shared_hidden, down_own),
+        (0, 0),
+        None,
         7,
-    )
+        (stream * scale_one, gains, down_cols),
+    )
+    layer_out = (residual + out_total).astype(BF16).reshape(1, own_rows, width)
     output_grad = output_down_grad[:output_rows]
-    first_gain_part = jnp.sum(normed_one_grad * stream * scale_one, axis=0)
     input_grad = (
         residual_grad + rms_back(stream, scale_one, normed_one_grad * first_gain)
     ).reshape(1, own_rows, width)
@@ -1838,14 +2093,10 @@
     shared_up_grad = shared_back[1].T
     shared_down_grad = shared_back[2]
 
-    gains = jnp.concatenate([first_gain_part, latent_gain_part, second_gain_part])
-    gains = padded_rows(gains.reshape(-1, LATENT // 4))
-    down_total, all_gains = kernel_finish(output_down_grad[output_rows:].astype(BF16), gains, 5)
     latent_down_grad = down_total.astype(F32).T
-    gains = jnp.sum(all_gains, axis=0).reshape(-1)
-    first_gain_grad = gains[:width]
-    latent_gain_grad = gains[width : width + LATENT]
-    second_gain_grad = gains[width + LATENT : 2 * width + LATENT]
+    gains = jnp.sum(all_gains, axis=0)
+    first_gain_grad, second_gain_grad = gains[0], gains[1]
+    latent_gain_grad = gains[2, :LATENT]
     return (
         layer_out,
         input_grad,

time: 836 us -> 809 us (0.968)
  Pallas kernels: 680 us -> 656 us
    pallas_call x4 -> x3, Pallas kernels: 301 us -> 282 us  [kernel_total(): pl.pallas_call(functools.partial(total_body, lines, tuple(dims), tuple(fl...]
  transfers between devices with their start and end apart: 2 -> 2, of which waited for: 1 -> 1; matrix products, arithmetic and copies ran while one was open for 7% -> 7% of each run, Pallas kernels for 13% -> 14%
where the time goes in v4:
time: 809 us; the launch traced here: 803 us
  Pallas kernels  656 us (81%)
  matrix products  46.8 us (6%)
  other arithmetic  41.5 us (5%)
  local copies, waits for them, and re-layouts  31.1 us (4%)
  starting transfers between devices  21.6 us (3%)
    pallas_call x3, Pallas kernels, kernel_total(): pl.pallas_call(functools.partial(total_body, lines, tuple(dims), tuple(fl...  282 us
    pallas_call x4, Pallas kernels, kernel_gather(): pl.pallas_call(functools.partial(gather_body, lines, tuple(dims), tuple(f...  251 us
    pallas_call x1, Pallas kernels, run_experts(): pl.pallas_call(experts_body, grid=(count, rows // chunk), in_specs=[row_b...  75.7 us
    pallas_call x1, Pallas kernels, run_tokens(): pl.pallas_call(functools.partial(tokens_body, group, capacity), grid=(blo...  30.5 us
    pallas_call x1, Pallas kernels, row_sum(): pl.pallas_call(row_sum_body, out_shape=jax.ShapeDtypeStruct(value.shape,...  16.5 us
  transfers between devices with their start and end apart: 2, of which 1 were waited for; matrix products, arithmetic and copies ran while one was open for 7% of the time, Pallas kernels for 14%

profile of v4, /device:TPU:8, one launch (start us, length us, event | category | flops | bytes accessed | tf_op | source)
XLA Modules:
  0.0 802.9 jit_solution(14541609394799636755)
XLA Ops:
  0.7 1.3 fusion.11
  3.2 2.1 bitcast_convert_fusion.refs_4_
  6.7 1.3 convert_multiply_fusion.2
  8.0 131.8 %gather_1.1 = (bf16[2048,768]{1,0:T(8,128)(2,1)}, bf16[656,2048]{1,0:T(8,128)(2,1)}, bf16[512,1024]{1,0:T(8,128)(2,1)}, bf16[512,2048]{1,0:T(8,128)(2,1)}, bf16[...) custom-call(bf16[256,768]{1,0:T(8,128)(2,1)} %refs_0_.1, bf16[656,256]{1,0:T(8,128)(2,1)} %pad_maximum_fusion.10.refs_1_, ...), custom_call_target="tpu_custom_call" | custom-call | tf_op jit(solution)/shard_map/gather_1/pallas_call | solution.py:904
  140.8 2.3 pad_maximum_fusion.2
  143.1 15.8 %all-to-all-start = ((bf16[8,264,256]{2,1,0:T(8,128)(2,1)}), bf16[8,264,256]{2,1,0:T(8,128)(2,1)}, u32[]{:S(2)}, u32[]{:S(2)}) async-start(bf16[8,264,256]{2,1,0:T(8,128)(2,1)} %bitcast.166), calls=%async_computation | async-start | bytes 2162688 | tf_op jit(solution)/shard_map/all_to_all | solution.py:1880
  158.9 1.7 fusion.36
  160.6 2.6 fusion.26.refs_0_
  163.3 12.0 %gather_8.1 = f32[576,512]{1,0:T(8,128)} custom-call(f32[144,512]{1,0:T(8,128)} %fusion.26.refs_0_), custom_call_target="tpu_custom_call" | custom-call | tf_op jit(solution)/shard_map/gather_8/pallas_call | solution.py:904
  175.2 1.7 copy.178
  177.0 1.1 multiply_subtract_fusion
  178.1 1.1 fusion.52
  180.0 3.0 convolution_convert_fusion.5
  183.0 2.4 copy.213
  185.4 1.1 slice.150
  186.5 3.9 fusion.56
  190.7 1.0 fusion.1
  192.7 1.0 copy-done.15
  193.8 1.4 convolution_convert_fusion.7
  195.9 2.6 convolution_convert_fusion.2.refs_0_
  198.6 17.6 %total_6.1 = f32[128,2048]{1,0:T(8,128)} custom-call(bf16[512,2048]{1,0:T(8,128)(2,1)} %convolution_convert_fusion.2.refs_0_), custom_call_target="tpu_custom_call" | custom-call | tf_op jit(solution)/shard_map/total_6/pallas_call | solution.py:1366
  216.1 1.5 multiply_reduce_fusion.4
  220.2 1.3 fusion.2.refs_2_.place_ref.refs_0_.refs_4_
  221.5 84.8 %gather_2.1 = (bf16[4096,2048]{1,0:T(8,128)(2,1)}, f32[32,8,128]{2,1,0:T(8,128)}, bf16[8,32,16,2048]{3,2,1,0:T(8,128)(2,1)}) custom-call(bf16[128,2048]{1,0:T(8,128)(2,1)} %copy-done.14, f32[8,128]{1,0:T(8,128)} %pad.23.refs_1_, bf16[32,128,128]{2,1,0:T(8,128)(2,1)} %fusion.2.refs_2_.place_ref.refs_0_.refs_4_, bf16[4096,2048]{1,0:T(8,128)(2,1)} %get-tuple-element.56.refs_3_.g_ref), custom_call_target="tpu_custom_call" | custom-call | tf_op jit(solution)/shard_map/gather_2/pallas_call | solution.py:904
  306.2 1.1 fusion.18
  308.0 2.4 reshape.374.gate_ref
  310.5 1.5 copy.190
  313.3 1.1 pad_slice_fusion.1
  314.3 30.5 %run_tokens.1 = (bf16[8,32,16,2048]{3,2,1,0:T(8,128)(2,1)}, bf16[4096,128]{1,0:T(8,128)(2,1)}, bf16[4096,256]{1,0:T(8,128)(2,1)}, f32[256,2048]{1,0:T(8,128)}, f32[128,2048]{1,0:T(8,128)}) custom-call(bf16[32,128,128]{2,1,0:T(8,128)(2,1)} %fusion.2.refs_2_.place_ref.refs_0_.refs_4_, bf16[4096,2048]{1,0:T(8,128)(2,1)} %get-tuple-element.57.x_ref, ...), custom_call_target="tpu_custom_call" | custom-call | flops 15032385536 | bytes 67108864 | tf_op jit(solution)/shard_map/run_tokens/pallas_call | solution.py:1601
  344.8 75.7 %run_experts.1 = (bf16[8,512,2048]{2,1,0:T(8,128)(2,1)}, bf16[8,512,2048]{2,1,0:T(8,128)(2,1)}, f32[8,352,2048]{2,1,0:T(8,128)}, f32[8,352,2048]{2,1,0:T(8,128)}...) custom-call(bf16[8,512,2048]{2,1,0:T(8,128)(2,1)} %bitcast.203, bf16[8,512,2048]{2,1,0:T(8,128)(2,1)} %bitcast.198, ...), custom_call_target="tpu_custom_call" | custom-call | flops 53150220288 | bytes 170917888 | tf_op jit(solution)/shard_map/run_experts/pallas_call | solution.py:1736
  420.6 2.2 reduce
  423.0 1.6 select_reduce_fusion.1.refs_4_
  424.5 105.2 %total_3.1 = (f32[128,2048]{1,0:T(8,128)}, f32[32,8,128]{2,1,0:T(8,128)}) custom-call(bf16[32,128,128]{2,1,0:T(8,128)(2,1)} %fusion.2.refs_2_.place_ref.refs_0_.refs_4_, bf16[8,32,16,2048]{3,2,1,0:T(8,128)(2,1)} %bitcast.165, bf16[4096,256]{1,0:T(8,128)(2,1)} %get-tuple-element.63.refs_2_, bf16[256,2048]{1,0:T(8,128)(2,1)} %bitcast.170, ...), custom_call_target="tpu_custom_call" | custom-call | tf_op jit(solution)/shard_map/total_3/pallas_call | solution.py:1366
  529.7 1.1 bitcast_reduce_fusion
  531.5 2.2 multiply_reduce_fusion
  533.7 1.5 fusion.50
  535.2 22.5 %gather_4.1 = (bf16[512,2048]{1,0:T(8,128)(2,1)}, f32[32,8,128]{2,1,0:T(8,128)}) custom-call(bf16[128,2048]{1,0:T(8,128)(2,1)} %get-tuple-element.88.refs_0_, f32[8,128]{1,0:T(8,128)} %pad.25.refs_1_), custom_call_target="tpu_custom_call" | custom-call | tf_op jit(solution)/shard_map/gather_4/pallas_call | solution.py:904
  557.8 3.7 multiply_reduce_fusion.2
  561.5 2.6 convolution_convert_fusion.1
  564.1 1.4 fusion.9
  565.5 1.8 multiply_convert_fusion
  569.2 1.0 copy-done.35
  570.2 1.5 convolution_convert_fusion.8
  571.8 1.9 convolution_convert_fusion.4.refs_2_
  574.0 1.9 pad_maximum_fusion.7.value_ref
  575.9 16.5 %row_sum_9.1 = bf16[512,576]{1,0:T(8,128)(2,1)} custom-call(bf16[512,576]{1,0:T(8,128)(2,1)} %pad_maximum_fusion.7.value_ref), custom_call_target="tpu_custom_call" | custom-call | tf_op jit(solution)/shard_map/row_sum_9/pallas_call | solution.py:1430
  592.4 2.2 slice.158
  595.0 1.1 subtract_convert_fusion.1
  597.6 1.3 copy.202
  598.9 5.8 all-to-all-start.1
  604.8 3.8 fusion.58
  608.6 1.3 fusion.34
  611.6 1.7 pad_maximum_fusion.refs_1_
  613.4 1.1 select_reduce_fusion
  615.1 3.5 convolution_add_fusion.refs_3_
  618.6 3.5 convolution_convert_fusion.refs_0_
  622.1 3.8 fusion.22
  625.9 3.5 all-to-all-done.1
  629.5 159.8 %total_7.1 = (f32[256,768]{1,0:T(8,128)}, f32[656,256]{1,0:T(8,128)}, f32[64,1024]{1,0:T(8,128)}, f32[128,2048]{1,0:T(8,128)}, f32[128,2048]{1,0:T(8,128)}, /*in...) custom-call(bf16[2048,768]{1,0:T(8,128)(2,1)} %convolution_convert_fusion.refs_0_, ...), custom_call_target="tpu_custom_call" | custom-call | tf_op jit(solution)/shard_map/total_7/pallas_call | solution.py:1366
  789.2 1.2 reduce_sum.218
  791.6 1.4 fusion.16
  794.7 1.4 convert_bitcast_fusion
  796.2 1.4 fusion.51
  799.1 1.7 fusion.15
  (206 shorter events, 24.2 us)
Async XLA Ops:
  0.6 5.3 copy-start
  0.7 6.0 copy-start.7
  0.7 5.3 copy-start.49
  0.7 6.0 copy-start.52
  2.6 5.5 copy-start.56
  6.7 134.0 %copy-start.46 = (bf16[704,256]{1,0:T(8,128)(2,1)S(1)}, bf16[704,256]{1,0:T(8,128)(2,1)}, u32[]{:S(2)}) copy-start(bf16[704,256]{1,0:T(8,128)(2,1)} %param.31) | copy-start | bytes 1081348
  140.8 19.9 %copy-start.11 = (bf16[512,2048]{1,0:T(8,128)(2,1)S(1)}, bf16[512,2048]{1,0:T(8,128)(2,1)}, u32[]{:S(2)}) copy-start(bf16[512,2048]{1,0:T(8,128)(2,1)} %get-tuple-element.52) | copy-start | bytes 6291460
  143.1 167.4 %all-to-all-start = ((bf16[8,264,256]{2,1,0:T(8,128)(2,1)}), bf16[8,264,256]{2,1,0:T(8,128)(2,1)}, u32[]{:S(2)}, u32[]{:S(2)}) async-start(bf16[8,264,256]{2,1,0:T(8,128)(2,1)} %bitcast.166), calls=%async_computation | async-start | bytes 2162688 | tf_op jit(solution)/shard_map/all_to_all | solution.py:1880
  175.2 4.0 copy-start.55
  176.9 3.1 copy-start.2
  176.9 2.5 copy-start.33
  177.0 3.1 copy-start.54
  179.5 13.3 %copy-start.31 = (pred[512,512]{0,1:T(8,128)(4,1)}, pred[512,512]{0,1:T(8,128)(4,1)S(1)}, u32[]{:S(2)}) copy-start(pred[512,512]{0,1:T(8,128)(4,1)S(1)} %fusion.17) | copy-start | bytes 786436
  179.7 10.8 %copy-start.38 = (f32[512,32]{0,1:T(8,128)}, f32[512,32]{0,1:T(8,128)S(1)}, u32[]{:S(2)}) copy-start(f32[512,32]{0,1:T(8,128)S(1)} %copy.183) | copy-start | bytes 196612
  183.0 3.5 copy-start.12
  186.5 4.2 copy-start.22
  190.5 1.2 copy-start.24
  190.6 1.1 copy-start.40
  190.6 1.1 copy-start.42
  191.8 2.0 copy-start.15
  191.8 2.0 copy-start.20
  193.8 2.2 copy-start.44
  216.1 2.5 copy-start.51
  216.1 2.7 copy-start.28
  218.8 2.6 copy-start.14
  529.7 4.0 copy-start.5
  529.7 4.0 copy-start.17
  533.7 24.1 %copy-start.61 = (bf16[4,128,512]{2,1,0:T(8,128)(2,1)S(1)}, bf16[4,128,512]{2,1,0:T(8,128)(2,1)}, u32[]{:S(2)}) copy-start(bf16[4,128,512]{2,1,0:T(8,128)(2,1)} %copy-done.60) | copy-start | bytes 1572868
  557.8 3.7 copy-start.59
  561.5 2.6 copy-start.16
  561.5 2.6 copy-start.32
  564.1 1.4 copy-start.21
  565.5 1.8 copy-start.25
  565.5 1.8 copy-start.41
  565.5 1.8 copy-start.43
  567.3 1.1 copy-start.30
  569.0 1.2 copy-start.35
  569.2 2.6 copy-start.3
  571.8 2.0 copy-start.39
  592.4 2.3 copy-start.10
  594.7 1.7 copy-start.34
  594.8 1.7 copy-start.8
  594.8 2.3 copy-start.26
  598.9 30.5 %all-to-all-start.1 = ((bf16[8,264,256]{2,1,0:T(8,128)(2,1)}), bf16[8,264,256]{2,1,0:T(8,128)(2,1)}, u32[]{:S(2)}, u32[]{:S(2)}) async-start(bf16[8,264,256]{2,1,0:T(8,128)(2,1)} %copy.202), calls=%async_computation.1 | async-start | bytes 2162688 | tf_op jit(solution)/shard_map/all_to_all | solution.py:1977
  604.7 5.2 copy-start.9
  608.6 1.7 copy-start.13
  609.9 1.7 copy-start.27
  609.9 12.2 %slice-start = ((s8[16777216]{0:T(1024)(128)(4,1)}), s8[4194304]{0:T(1024)(128)(4,1)S(1)}, s32[]{:S(2)}) async-start(s8[16777216]{0:T(1024)(128)(4,1)} %bitcast.162), calls=%async_computation.2 | async-start | bytes 8388608
  610.3 3.0 copy-start.50
  611.6 10.5 %slice-start.1 = ((s8[16777216]{0:T(1024)(128)(4,1)}), s8[4194304]{0:T(1024)(128)(4,1)S(1)}, s32[]{:S(2)}) async-start(s8[16777216]{0:T(1024)(128)(4,1)} %bitcast.162), calls=%async_computation.3 | async-start | bytes 8388608
  615.1 7.0 slice-start.2
  618.6 3.5 slice-start.3
  629.5 162.1 %copy-start.53 = (f32[2048]{0:T(1024)S(1)}, f32[2048]{0:T(1024)}, u32[]{:S(2)}) copy-start(f32[2048]{0:T(1024)} %param.21) | copy-start | bytes 24580
  789.2 3.8 copy-start.45
  789.2 4.7 copy-start.47
  796.1 1.7 copy-start.6
  796.2 2.3 copy-start.18
  796.2 2.6 copy-start.19
  796.2 2.9 copy-start.36
  796.2 2.9 copy-start.57
  796.2 2.9 copy-start.58
  799.1 1.8 copy-start.37
  799.1 2.6 copy-start.48
  799.1 3.3 copy-start.1
  (4 other events, 4.0 us)

commit v5 on v4

--- a/solution.py
+++ b/solution.py
@@ -838,11 +838,12 @@
         at += 1
     if has_small:
         small_start, small_finish = small_exchange(ins[at], outs[at], *take(2), False)
-        small_start()
     if has_pick:
         plans.append(pick_plan(lines, *pick_refs))
     for start, _, _ in plans:
         start()
+    if has_small:
+        small_start()
     for dist in range(1, lines + 2):
         for _, step, _ in plans:
             step(dist)
@@ -1177,7 +1178,10 @@
 
     def first():
         held[...] = gains_ref[...]
-        held[0:1, :] = jnp.sum(row_out[...] * scaled_ref[...], axis=0, keepdims=True)
+        part = jnp.sum(row_out[...] * scaled_ref[...], axis=0, keepdims=True)
+        piece = part.shape[1] // 4
+        for i in range(4):
+            held[i : i + 1, 0:piece] = part[:, i * piece : (i + 1) * piece]
         for d in range(n_row - 1):
             row_copy(d, row).start()
 
@@ -1192,11 +1196,15 @@
         for d in range(n_col - 1):
             col_copy(d, col).start()
 
-    def finish(value):
-        local = pltpu.make_async_copy(value, strip(down_ref, 0, row, size), local_sem)
-        local.start()
+    def local(value):
+        return pltpu.make_async_copy(value, strip(down_ref, 0, row, size), local_sem)
+
+    def third(value):
+        local(value).start()
         for d in range(n_row - 1):
             down_copy(d, row, value).start()
+
+    def finish(value):
         for d in range(n_col - 1):
             col_copy(d, cols[d]["col"]).wait_recv()
             col_copy(d, col).wait_send()
@@ -1204,9 +1212,9 @@
             row_copy(d, row).wait_send()
             down_copy(d, rows[d]["row"], value).wait_recv()
             down_copy(d, row, value).wait_send()
-        local.wait()
-
-    return rows + cols, first, second, finish
+        local(value).wait()
+
+    return rows + cols, first, second, third, finish
 
 
 def total_body(lines, dims, flips, ways, kinds, *refs):
@@ -1235,14 +1243,13 @@
     if has_last:
         last_outs = take(2)
         down_rows = last_outs[1].shape[0] // lax.axis_size("row")
-        peers, last_first, last_second, last_finish = last_plan(
+        peers, last_first, last_second, last_third, last_finish = last_plan(
             mixed_outs[-1], *last_ins, *last_outs, take(10)
         )
         partners = [(core >= 0, peer) for peer in peers]
     greet(partners, has_small)
     if has_small:
         small_start, small_finish = small_exchange(*small_ins, *small_outs, *take(2), True)
-        small_start()
     mixed_step = None
     if has_every:
         every_start, stages, every_finish = every_total_plan(
@@ -1254,6 +1261,9 @@
             lines, dims, flips, spots, mixed_ins + mixed_outs + refs
         )
         mixed_start()
+
+        def down_value():
+            return own_rows(1, pl.ds(mixed_outs[1].shape[0] - down_rows, down_rows))
 
         def mixed_step(step):
             mixed_go(step)
@@ -1261,15 +1271,21 @@
                 last_first()
             if has_last and step == lines:
                 last_second()
+            if has_last and step == lines + 1:
+                last_third(down_value())
 
     if has_every:
-        for action, index in total_order(lines, stages, mixed_step):
+        for number, (action, index) in enumerate(total_order(lines, stages, mixed_step)):
             action(index)
+            if has_small and number == 0:
+                small_start()
     else:
+        if has_small:
+            small_start()
         for step in range(mixed_steps):
             mixed_step(step)
     if has_last:
-        last_finish(own_rows(1, pl.ds(mixed_outs[1].shape[0] - down_rows, down_rows)))
+        last_finish(down_value())
     if has_mixed:
         mixed_finish()
     if has_every:
@@ -1521,8 +1537,9 @@
         out.append(lax.all_to_all(small_value, EVERY, split_axis=0, concat_axis=0, tiled=True))
     if last_value is not None:
         scaled, gains, down_rows = last_value
-        part = jnp.sum(out[len(dims)] * scaled, axis=0)
-        out.append(lax.psum(gains.at[0].set(part), EVERY)[None])
+        part = jnp.sum(out[len(dims)] * scaled, axis=0).reshape(4, -1)
+        part = jnp.pad(part, ((0, 4), (0, gains.shape[1] - part.shape[1])))
+        out.append(lax.psum(gains + part, EVERY)[None])
         out.append(token_rows(out[1][-down_rows:].astype(BF16)))
     return out
 
@@ -2050,14 +2067,13 @@
     )
     input_part = outer_cols(query_full, query_all) + matmul(own_down_grad, down_all)
     input_part, shared_back = lax.optimization_barrier((input_part, shared_back))
-    gains = jnp.stack(
+    gains = jnp.concatenate(
         [
-            jnp.zeros_like(second_gain_part),
-            second_gain_part,
-            jnp.pad(latent_gain_part, (0, width - LATENT)),
-        ]
-    )
-    gains = padded_rows(gains)
+            jnp.pad(second_gain_part.reshape(4, -1), ((4, 0), (0, 0))),
+            jnp.pad(latent_gain_part.reshape(4, -1), ((0, 4), (0, 0))),
+        ],
+        axis=1,
+    )
     (
         query_grad,
         output_down_grad,
@@ -2095,8 +2111,9 @@
 
     latent_down_grad = down_total.astype(F32).T
     gains = jnp.sum(all_gains, axis=0)
-    first_gain_grad, second_gain_grad = gains[0], gains[1]
-    latent_gain_grad = gains[2, :LATENT]
+    first_gain_grad = gains[:4, : width // 4].reshape(-1)
+    second_gain_grad = gains[4:, : width // 4].reshape(-1)
+    latent_gain_grad = gains[:4, width // 4 :].reshape(-1)
     return (
         layer_out,
         input_grad,

time: 809 us -> 801 us (level)
  Pallas kernels: 656 us -> 644 us
  matrix products: 46.8 us -> 55.3 us
    pallas_call x3, Pallas kernels: 282 us -> 271 us  [kernel_total(): pl.pallas_call(functools.partial(total_body, lines, tuple(dims), tuple(fl...]
  transfers between devices with their start and end apart: 2 -> 2, of which waited for: 1 -> 0; matrix products, arithmetic and copies ran while one was open for 7% -> 8% of each run, Pallas kernels for 14% -> 14%
where the time goes in v5:
time: 801 us; the launch traced here: 796 us
  Pallas kernels  644 us (80%)
  matrix products  55.3 us (7%)
  other arithmetic  41.3 us (5%)
  local copies, waits for them, and re-layouts  31.7 us (4%)
  starting transfers between devices  21.4 us (3%)
    pallas_call x3, Pallas kernels, kernel_total(): pl.pallas_call(functools.partial(total_body, lines, tuple(dims), tuple(fl...  271 us
    pallas_call x4, Pallas kernels, kernel_gather(): pl.pallas_call(functools.partial(gather_body, lines, tuple(dims), tuple(f...  250 us
    pallas_call x1, Pallas kernels, run_experts(): pl.pallas_call(experts_body, grid=(count, rows // chunk), in_specs=[row_b...  75.7 us
    pallas_call x1, Pallas kernels, run_tokens(): pl.pallas_call(functools.partial(tokens_body, group, capacity), grid=(blo...  30.5 us
    dot_general x5, matrix products, inner_rows(): lax.dot_general(left_side, right_side, ROWS_CONTRACT, preferred_element_t...  18.4 us
    pallas_call x1, Pallas kernels, row_sum(): pl.pallas_call(row_sum_body, out_shape=jax.ShapeDtypeStruct(value.shape,...  16.6 us
  transfers between devices with their start and end apart: 2, of which 0 were waited for; matrix products, arithmetic and copies ran while one was open for 8% of the time, Pallas kernels for 14%

profile of v5, /device:TPU:8, one launch (start us, length us, event | category | flops | bytes accessed | tf_op | source)
XLA Modules:
  0.0 795.8 jit_solution(12961949676388812731)
XLA Ops:
  0.7 1.3 fusion.11
  3.3 2.1 bitcast_convert_fusion.refs_4_
  6.8 1.3 convert_multiply_fusion.2
  8.1 131.6 %gather_1.1 = (bf16[2048,768]{1,0:T(8,128)(2,1)}, bf16[656,2048]{1,0:T(8,128)(2,1)}, bf16[512,1024]{1,0:T(8,128)(2,1)}, bf16[512,2048]{1,0:T(8,128)(2,1)}, bf16[...) custom-call(bf16[256,768]{1,0:T(8,128)(2,1)} %refs_0_.1, bf16[656,256]{1,0:T(8,128)(2,1)} %pad_maximum_fusion.10.refs_1_, ...), custom_call_target="tpu_custom_call" | custom-call | tf_op jit(solution)/shard_map/gather_1/pallas_call | solution.py:905
  139.7 0.9 slice_convert_fusion.3
  140.6 2.3 pad_maximum_fusion.2
  143.0 15.8 %all-to-all-start = ((bf16[8,264,256]{2,1,0:T(8,128)(2,1)}), bf16[8,264,256]{2,1,0:T(8,128)(2,1)}, u32[]{:S(2)}, u32[]{:S(2)}) async-start(bf16[8,264,256]{2,1,0:T(8,128)(2,1)} %bitcast.167), calls=%async_computation | async-start | bytes 2162688 | tf_op jit(solution)/shard_map/all_to_all | solution.py:1897
  158.8 1.7 fusion.36
  160.5 2.6 fusion.26.refs_0_
  163.1 11.8 %gather_8.1 = f32[576,512]{1,0:T(8,128)} custom-call(f32[144,512]{1,0:T(8,128)} %fusion.26.refs_0_), custom_call_target="tpu_custom_call" | custom-call | tf_op jit(solution)/shard_map/gather_8/pallas_call | solution.py:905
  175.0 1.7 copy.178
  176.7 1.1 multiply_subtract_fusion
  177.8 1.1 fusion.52
  179.8 3.0 convolution_convert_fusion.5
  182.8 2.4 copy.213
  185.2 1.1 slice.150
  186.3 3.9 fusion.55
  190.5 1.0 fusion.1
  191.6 0.9 exponential_reduce_fusion
  192.5 1.0 copy-done.16
  193.6 1.4 convolution_convert_fusion.7
  195.7 2.6 convolution_convert_fusion.2.refs_0_
  198.3 17.5 %total_6.1 = f32[128,2048]{1,0:T(8,128)} custom-call(bf16[512,2048]{1,0:T(8,128)(2,1)} %convolution_convert_fusion.2.refs_0_), custom_call_target="tpu_custom_call" | custom-call | tf_op jit(solution)/shard_map/total_6/pallas_call | solution.py:1382
  215.9 1.5 multiply_reduce_fusion.4
  217.4 1.0 copy-done.4
  219.9 1.3 fusion.2.refs_2_.place_ref.refs_0_.refs_4_
  221.2 84.6 %gather_2.1 = (bf16[4096,2048]{1,0:T(8,128)(2,1)}, f32[32,8,128]{2,1,0:T(8,128)}, bf16[8,32,16,2048]{3,2,1,0:T(8,128)(2,1)}) custom-call(bf16[128,2048]{1,0:T(8,128)(2,1)} %copy-done.15, f32[8,128]{1,0:T(8,128)} %pad.23.refs_1_, bf16[32,128,128]{2,1,0:T(8,128)(2,1)} %fusion.2.refs_2_.place_ref.refs_0_.refs_4_, bf16[4096,2048]{1,0:T(8,128)(2,1)} %get-tuple-element.56.refs_3_.g_ref), custom_call_target="tpu_custom_call" | custom-call | tf_op jit(solution)/shard_map/gather_2/pallas_call | solution.py:905
  305.8 1.1 fusion.18
  307.6 2.4 reshape.394.gate_ref
  310.0 1.5 copy.190
  312.8 1.1 pad_slice_fusion.1
  313.9 30.5 %run_tokens.1 = (bf16[8,32,16,2048]{3,2,1,0:T(8,128)(2,1)}, bf16[4096,128]{1,0:T(8,128)(2,1)}, bf16[4096,256]{1,0:T(8,128)(2,1)}, f32[256,2048]{1,0:T(8,128)}, f32[128,2048]{1,0:T(8,128)}) custom-call(bf16[32,128,128]{2,1,0:T(8,128)(2,1)} %fusion.2.refs_2_.place_ref.refs_0_.refs_4_, bf16[4096,2048]{1,0:T(8,128)(2,1)} %get-tuple-element.57.x_ref, ...), custom_call_target="tpu_custom_call" | custom-call | flops 15032385536 | bytes 67108864 | tf_op jit(solution)/shard_map/run_tokens/pallas_call | solution.py:1618
  344.4 75.7 %run_experts.1 = (bf16[8,512,2048]{2,1,0:T(8,128)(2,1)}, bf16[8,512,2048]{2,1,0:T(8,128)(2,1)}, f32[8,352,2048]{2,1,0:T(8,128)}, f32[8,352,2048]{2,1,0:T(8,128)}...) custom-call(bf16[8,512,2048]{2,1,0:T(8,128)(2,1)} %bitcast.202, bf16[8,512,2048]{2,1,0:T(8,128)(2,1)} %bitcast.197, ...), custom_call_target="tpu_custom_call" | custom-call | flops 53150220288 | bytes 170917888 | tf_op jit(solution)/shard_map/run_experts/pallas_call | solution.py:1753
  420.1 2.2 reduce
  422.5 1.6 select_reduce_fusion.1.refs_4_
  424.1 106.1 %total_3.1 = (f32[128,2048]{1,0:T(8,128)}, f32[32,8,128]{2,1,0:T(8,128)}) custom-call(bf16[32,128,128]{2,1,0:T(8,128)(2,1)} %fusion.2.refs_2_.place_ref.refs_0_.refs_4_, bf16[8,32,16,2048]{3,2,1,0:T(8,128)(2,1)} %bitcast.166, bf16[4096,256]{1,0:T(8,128)(2,1)} %get-tuple-element.63.refs_2_, bf16[256,2048]{1,0:T(8,128)(2,1)} %bitcast.171, ...), custom_call_target="tpu_custom_call" | custom-call | tf_op jit(solution)/shard_map/total_3/pallas_call | solution.py:1382
  530.2 1.1 bitcast_reduce_fusion
  532.0 2.2 multiply_reduce_fusion
  534.2 1.5 fusion.50
  535.7 22.2 %gather_4.1 = (bf16[512,2048]{1,0:T(8,128)(2,1)}, f32[32,8,128]{2,1,0:T(8,128)}) custom-call(bf16[128,2048]{1,0:T(8,128)(2,1)} %get-tuple-element.88.refs_0_, f32[8,128]{1,0:T(8,128)} %pad.25.refs_1_), custom_call_target="tpu_custom_call" | custom-call | tf_op jit(solution)/shard_map/gather_4/pallas_call | solution.py:905
  558.0 3.7 multiply_reduce_fusion.2
  561.7 2.6 convolution_convert_fusion.1
  564.3 1.4 fusion.9
  565.7 1.7 multiply_convert_fusion
  571.4 1.9 convolution_convert_fusion.4.refs_2_
  573.5 1.0 copy.201
  575.3 16.6 %row_sum_9.1 = bf16[512,576]{1,0:T(8,128)(2,1)} custom-call(bf16[512,576]{1,0:T(8,128)(2,1)} %pad_maximum_fusion.7.value_ref), custom_call_target="tpu_custom_call" | custom-call | tf_op jit(solution)/shard_map/row_sum_9/pallas_call | solution.py:1446
  591.9 2.3 slice.158
  594.5 1.1 subtract_convert_fusion.1
  597.2 1.2 copy.202
  598.4 5.5 all-to-all-start.1
  604.0 6.1 fusion.57
  610.1 1.0 select_reduce_fusion
  613.1 1.7 pad_maximum_fusion.refs_1_
  614.7 1.1 fusion.34
  616.5 4.8 convolution_add_fusion.refs_3_
  621.3 3.5 convolution_convert_fusion.refs_0_
  624.8 9.6 %fusion.22 = f32[2048,64]{0,1:T(8,128)} fusion(bf16[4096,2048]{1,0:T(8,128)(2,1)} %get-tuple-element.57.x_ref, bf16[32,128,64]{1,2,0:T(8,128)(2,1)S(1)} %select_reduce_fusion), kind=kOutput, calls=%fused_computation.83 | convolution fusion | flops 1073741824 | bytes 17825792 | tf_op jit(solution)/shard_map/dot_general | solution.py:27
  634.4 147.5 %total_7.1 = (f32[256,768]{1,0:T(8,128)}, f32[656,256]{1,0:T(8,128)}, f32[64,1024]{1,0:T(8,128)}, f32[128,2048]{1,0:T(8,128)}, f32[128,2048]{1,0:T(8,128)}, /*in...) custom-call(bf16[2048,768]{1,0:T(8,128)(2,1)} %convolution_convert_fusion.refs_0_, bf16[656,2048]{1,0:T(8,128)(2,1)} %pad_maximum_fusion.refs_1_, ...), custom_call_target="tpu_custom_call" | custom-call | tf_op jit(solution)/shard_map/total_7/pallas_call | solution.py:1382
  781.9 1.0 reduce_sum.218
  783.5 1.4 fusion.16
  787.9 1.4 convert_bitcast_fusion
  789.3 1.4 fusion.51
  792.3 1.7 fusion.15
  (203 shorter events, 25.0 us)
Async XLA Ops:
  0.6 5.3 copy-start
  0.7 6.1 copy-start.7
  0.7 5.3 copy-start.52
  0.7 6.1 copy-start.55
  2.6 5.5 copy-start.59
  6.8 133.8 %copy-start.49 = (bf16[704,256]{1,0:T(8,128)(2,1)S(1)}, bf16[704,256]{1,0:T(8,128)(2,1)}, u32[]{:S(2)}) copy-start(bf16[704,256]{1,0:T(8,128)(2,1)} %param.31) | copy-start | bytes 1081348
  140.6 19.9 %copy-start.11 = (bf16[512,2048]{1,0:T(8,128)(2,1)S(1)}, bf16[512,2048]{1,0:T(8,128)(2,1)}, u32[]{:S(2)}) copy-start(bf16[512,2048]{1,0:T(8,128)(2,1)} %get-tuple-element.52) | copy-start | bytes 6291460
  143.0 167.0 %all-to-all-start = ((bf16[8,264,256]{2,1,0:T(8,128)(2,1)}), bf16[8,264,256]{2,1,0:T(8,128)(2,1)}, u32[]{:S(2)}, u32[]{:S(2)}) async-start(bf16[8,264,256]{2,1,0:T(8,128)(2,1)} %bitcast.167), calls=%async_computation | async-start | bytes 2162688 | tf_op jit(solution)/shard_map/all_to_all | solution.py:1897
  175.0 4.0 copy-start.58
  176.7 3.1 copy-start.2
  176.7 2.6 copy-start.34
  176.7 3.1 copy-start.57
  179.2 13.3 %copy-start.32 = (pred[512,512]{0,1:T(8,128)(4,1)}, pred[512,512]{0,1:T(8,128)(4,1)S(1)}, u32[]{:S(2)}) copy-start(pred[512,512]{0,1:T(8,128)(4,1)S(1)} %fusion.17) | copy-start | bytes 786436
  179.5 10.8 %copy-start.41 = (f32[512,32]{0,1:T(8,128)}, f32[512,32]{0,1:T(8,128)S(1)}, u32[]{:S(2)}) copy-start(f32[512,32]{0,1:T(8,128)S(1)} %copy.183) | copy-start | bytes 196612
  182.8 3.5 copy-start.12
  186.3 4.2 copy-start.23
  190.3 1.2 copy-start.25
  190.4 1.1 copy-start.43
  190.4 1.1 copy-start.45
  190.5 1.1 copy-start.30
  191.6 2.0 copy-start.16
  191.6 2.0 copy-start.21
  193.6 2.2 copy-start.47
  215.8 2.5 copy-start.54
  215.9 2.7 copy-start.29
  218.5 2.6 copy-start.15
  530.2 4.0 copy-start.5
  530.2 4.0 copy-start.18
  534.2 23.8 %copy-start.64 = (bf16[4,128,512]{2,1,0:T(8,128)(2,1)S(1)}, bf16[4,128,512]{2,1,0:T(8,128)(2,1)}, u32[]{:S(2)}) copy-start(bf16[4,128,512]{2,1,0:T(8,128)(2,1)} %copy-done.63) | copy-start | bytes 1572868
  558.0 3.7 copy-start.62
  561.7 2.6 copy-start.17
  561.7 2.6 copy-start.33
  564.3 1.4 copy-start.22
  565.7 1.8 copy-start.26
  565.7 1.8 copy-start.44
  565.7 1.8 copy-start.46
  567.5 1.1 copy-start.31
  569.2 1.3 copy-start.36
  570.0 1.4 copy-start.3
  571.4 1.9 copy-start.42
  591.9 2.3 copy-start.10
  594.2 1.7 copy-start.35
  594.3 1.7 copy-start.8
  594.3 2.3 copy-start.27
  598.4 36.0 %all-to-all-start.1 = ((bf16[8,264,256]{2,1,0:T(8,128)(2,1)}), bf16[8,264,256]{2,1,0:T(8,128)(2,1)}, u32[]{:S(2)}, u32[]{:S(2)}) async-start(bf16[8,264,256]{2,1,0:T(8,128)(2,1)} %copy.202), calls=%async_computation.1 | async-start | bytes 2162688 | tf_op jit(solution)/shard_map/all_to_all | solution.py:1994
  604.0 6.2 copy-start.39
  604.0 6.1 copy-start.53
  604.0 7.1 copy-start.9
  610.1 1.6 copy-start.13
  611.4 1.7 copy-start.28
  616.5 4.8 copy-start.14
  616.5 4.8 copy-start.40
  634.4 149.1 %copy-start.56 = (f32[2048]{0:T(1024)S(1)}, f32[2048]{0:T(1024)}, u32[]{:S(2)}) copy-start(f32[2048]{0:T(1024)} %param.21) | copy-start | bytes 24580
  781.9 4.3 copy-start.48
  781.9 5.1 copy-start.50
  789.3 1.7 copy-start.6
  789.3 2.3 copy-start.19
  789.3 2.6 copy-start.20
  789.3 2.9 copy-start.37
  789.3 2.9 copy-start.60
  789.3 2.9 copy-start.61
  792.2 1.8 copy-start.38
  792.2 2.6 copy-start.51
  792.2 3.3 copy-start.1
  (3 other events, 2.9 us)

commit v6 on v5

--- a/solution.py
+++ b/solution.py
@@ -1249,7 +1249,9 @@
         partners = [(core >= 0, peer) for peer in peers]
     greet(partners, has_small)
     if has_small:
-        small_start, small_finish = small_exchange(*small_ins, *small_outs, *take(2), True)
+        small_start, small_finish = small_exchange(
+            *small_ins, *small_outs, *take(2), len(small_ins[0].shape) == 3
+        )
     mixed_step = None
     if has_every:
         every_start, stages, every_finish = every_total_plan(
@@ -1340,7 +1342,8 @@
     if small_value is not None:
         operands.append(small_value)
         in_specs.append(vmem)
-        out_shape.append(jax.ShapeDtypeStruct(small_value.shape, small_value.dtype))
+        lead = () if small_value.ndim == 3 else (n_row * n_col,)
+        out_shape.append(jax.ShapeDtypeStruct((*lead, *small_value.shape), small_value.dtype))
         small_scratch = [dma((n_row * n_col,))] * 2
     if last_value is not None:
         scaled, gains, down_rows = last_value
@@ -1533,7 +1536,9 @@
     if every_value is not None:
         capacity = every_value[1].shape[1] // every_value[0].shape[0]
         out.append(every_total(combine_rows(*every_value, capacity)))
-    if small_value is not None:
+    if small_value is not None and small_value.ndim == 2:
+        out.append(every_token(small_value[None]))
+    elif small_value is not None:
         out.append(lax.all_to_all(small_value, EVERY, split_axis=0, concat_axis=0, tiled=True))
     if last_value is not None:
         scaled, gains, down_rows = last_value
@@ -2002,12 +2007,7 @@
     second_gain_part = jnp.sum(normed_two_grad * residual * scale_two, axis=0)
     residual_grad = grad_out + rms_back(residual, scale_two, normed_two_grad * second_gain)
 
-    seq_resid, all_picked = gather(
-        [], [], [], residual_grad.astype(BF16), None, None, padded_rows(picked_grad.T), 4
-    )
-    all_named = all_routes[:, :, :, None] == expert_ids
-    all_logit_grad = jnp.sum(jnp.where(all_named, all_picked[:, :TOPK, :, None], 0.0), axis=1)
-    router_grad = inner_rows(all_normed, all_logit_grad.astype(BF16).reshape(-1, experts))
+    (seq_resid,) = gather([], [], [], residual_grad.astype(BF16), None, None, None, 4)
     output_part = inner_rows(heads_out, seq_resid)
     heads_grad = outer_cols(seq_resid, output_all).astype(BF16).reshape(length, heads_local, VD)
     recomputed = jnp.exp(masked_scores(queries, attn_keys, allowed, softmax_scale) - log_total)
@@ -2080,6 +2080,7 @@
         latent_up_grad,
         normed_one_grad,
         out_total,
+        all_picked,
         all_gains,
         down_total,
     ) = total(
@@ -2089,7 +2090,7 @@
         input_part.astype(BF16),
         (place, out_slots, shared_hidden, down_own),
         (0, 0),
-        None,
+        padded_rows(picked_grad.T),
         7,
         (stream * scale_one, gains, down_cols),
     )
@@ -2109,6 +2110,9 @@
     shared_up_grad = shared_back[1].T
     shared_down_grad = shared_back[2]
 
+    all_named = all_routes[:, :, :, None] == expert_ids
+    all_logit_grad = jnp.sum(jnp.where(all_named, all_picked[:, :TOPK, :, None], 0.0), axis=1)
+    router_grad = inner_rows(all_normed, all_logit_grad.astype(BF16).reshape(-1, experts))
     latent_down_grad = down_total.astype(F32).T
     gains = jnp.sum(all_gains, axis=0)
     first_gain_grad = gains[:4, : width // 4].reshape(-1)

time: 801 us -> 802 us (level)
  transfers between devices with their start and end apart: 2 -> 2, of which waited for: 0 -> 1; matrix products, arithmetic and copies ran while one was open for 8% -> 6% of each run, Pallas kernels for 14% -> 14%
where the time goes in v6:
time: 802 us; the launch traced here: 796 us
  Pallas kernels  641 us (80%)
  matrix products  49.7 us (6%)
  other arithmetic  44.2 us (6%)
  local copies, waits for them, and re-layouts  31.2 us (4%)
  starting transfers between devices  21.5 us (3%)
    pallas_call x3, Pallas kernels, kernel_total(): pl.pallas_call(functools.partial(total_body, lines, tuple(dims), tuple(fl...  273 us
    pallas_call x4, Pallas kernels, kernel_gather(): pl.pallas_call(functools.partial(gather_body, lines, tuple(dims), tuple(f...  245 us
    pallas_call x1, Pallas kernels, run_experts(): pl.pallas_call(experts_body, grid=(count, rows // chunk), in_specs=[row_b...  75.7 us
    pallas_call x1, Pallas kernels, run_tokens(): pl.pallas_call(functools.partial(tokens_body, group, capacity), grid=(blo...  30.5 us
    dot_general x5, matrix products, inner_rows(): lax.dot_general(left_side, right_side, ROWS_CONTRACT, preferred_element_t...  18.5 us
    pallas_call x1, Pallas kernels, row_sum(): pl.pallas_call(row_sum_body, out_shape=jax.ShapeDtypeStruct(value.shape,...  16.6 us
  transfers between devices with their start and end apart: 2, of which 1 were waited for; matrix products, arithmetic and copies ran while one was open for 6% of the time, Pallas kernels for 14%

profile of v6, /device:TPU:8, one launch (start us, length us, event | category | flops | bytes accessed | tf_op | source)
XLA Modules:
  0.0 796.1 jit_solution(9799109030929508825)
XLA Ops:
  0.7 1.3 fusion.11
  3.3 2.1 bitcast_convert_fusion.refs_4_
  6.7 1.3 convert_multiply_fusion.2
  8.1 131.6 %gather_1.1 = (bf16[2048,768]{1,0:T(8,128)(2,1)}, bf16[656,2048]{1,0:T(8,128)(2,1)}, bf16[512,1024]{1,0:T(8,128)(2,1)}, bf16[512,2048]{1,0:T(8,128)(2,1)}, bf16[...) custom-call(bf16[256,768]{1,0:T(8,128)(2,1)} %refs_0_.1, bf16[656,256]{1,0:T(8,128)(2,1)} %pad_maximum_fusion.10.refs_1_, ...), custom_call_target="tpu_custom_call" | custom-call | tf_op jit(solution)/shard_map/gather_1/pallas_call | solution.py:905
  140.6 2.3 pad_maximum_fusion.2
  142.9 15.8 %all-to-all-start = ((bf16[8,264,256]{2,1,0:T(8,128)(2,1)}), bf16[8,264,256]{2,1,0:T(8,128)(2,1)}, u32[]{:S(2)}, u32[]{:S(2)}) async-start(bf16[8,264,256]{2,1,0:T(8,128)(2,1)} %bitcast.167), calls=%async_computation | async-start | bytes 2162688 | tf_op jit(solution)/shard_map/all_to_all | solution.py:1902
  158.8 1.7 fusion.36
  160.5 2.6 fusion.26.refs_0_
  163.1 11.8 %gather_8.1 = f32[576,512]{1,0:T(8,128)} custom-call(f32[144,512]{1,0:T(8,128)} %fusion.26.refs_0_), custom_call_target="tpu_custom_call" | custom-call | tf_op jit(solution)/shard_map/gather_8/pallas_call | solution.py:905
  174.9 1.7 copy.178
  176.6 1.1 multiply_subtract_fusion
  177.8 1.1 fusion.52
  179.7 3.0 convolution_convert_fusion.5
  182.7 2.5 copy.213
  185.1 1.1 slice.150
  186.2 3.9 fusion.55
  190.4 1.0 fusion.1
  192.4 1.0 copy-done.13
  193.5 1.4 convolution_convert_fusion.7
  195.6 2.6 convolution_convert_fusion.2.refs_0_
  198.3 17.5 %total_6.1 = f32[128,2048]{1,0:T(8,128)} custom-call(bf16[512,2048]{1,0:T(8,128)(2,1)} %convolution_convert_fusion.2.refs_0_), custom_call_target="tpu_custom_call" | custom-call | tf_op jit(solution)/shard_map/total_6/pallas_call | solution.py:1385
  215.8 1.5 multiply_reduce_fusion.4
  217.3 1.0 copy-done.4
  219.8 1.3 fusion.2.refs_2_.place_ref.refs_0_.refs_4_
  221.2 84.6 %gather_2.1 = (bf16[4096,2048]{1,0:T(8,128)(2,1)}, f32[32,8,128]{2,1,0:T(8,128)}, bf16[8,32,16,2048]{3,2,1,0:T(8,128)(2,1)}) custom-call(bf16[128,2048]{1,0:T(8,128)(2,1)} %copy-done.12, f32[8,128]{1,0:T(8,128)} %pad.23.refs_1_, bf16[32,128,128]{2,1,0:T(8,128)(2,1)} %fusion.2.refs_2_.place_ref.refs_0_.refs_4_, bf16[4096,2048]{1,0:T(8,128)(2,1)} %get-tuple-element.55.refs_3_.g_ref), custom_call_target="tpu_custom_call" | custom-call | tf_op jit(solution)/shard_map/gather_2/pallas_call | solution.py:905
  305.8 1.1 fusion.18
  307.6 2.4 reshape.394.gate_ref
  310.0 1.5 copy.190
  312.8 1.1 pad_slice_fusion.1
  313.9 30.5 %run_tokens.1 = (bf16[8,32,16,2048]{3,2,1,0:T(8,128)(2,1)}, bf16[4096,128]{1,0:T(8,128)(2,1)}, bf16[4096,256]{1,0:T(8,128)(2,1)}, f32[256,2048]{1,0:T(8,128)}, f32[128,2048]{1,0:T(8,128)}) custom-call(bf16[32,128,128]{2,1,0:T(8,128)(2,1)} %fusion.2.refs_2_.place_ref.refs_0_.refs_4_, bf16[4096,2048]{1,0:T(8,128)(2,1)} %get-tuple-element.56.x_ref, ...), custom_call_target="tpu_custom_call" | custom-call | flops 15032385536 | bytes 67108864 | tf_op jit(solution)/shard_map/run_tokens/pallas_call | solution.py:1623
  344.4 75.7 %run_experts.1 = (bf16[8,512,2048]{2,1,0:T(8,128)(2,1)}, bf16[8,512,2048]{2,1,0:T(8,128)(2,1)}, f32[8,352,2048]{2,1,0:T(8,128)}, f32[8,352,2048]{2,1,0:T(8,128)}...) custom-call(bf16[8,512,2048]{2,1,0:T(8,128)(2,1)} %bitcast.202, bf16[8,512,2048]{2,1,0:T(8,128)(2,1)} %bitcast.197, ...), custom_call_target="tpu_custom_call" | custom-call | flops 53150220288 | bytes 170917888 | tf_op jit(solution)/shard_map/run_experts/pallas_call | solution.py:1758
  420.1 2.2 reduce
  422.5 1.6 select_reduce_fusion.1.refs_4_
  424.1 106.1 %total_3.1 = (f32[128,2048]{1,0:T(8,128)}, f32[32,8,128]{2,1,0:T(8,128)}) custom-call(bf16[32,128,128]{2,1,0:T(8,128)(2,1)} %fusion.2.refs_2_.place_ref.refs_0_.refs_4_, bf16[8,32,16,2048]{3,2,1,0:T(8,128)(2,1)} %bitcast.165, bf16[4096,256]{1,0:T(8,128)(2,1)} %get-tuple-element.62.refs_2_, bf16[256,2048]{1,0:T(8,128)(2,1)} %bitcast.171, ...), custom_call_target="tpu_custom_call" | custom-call | tf_op jit(solution)/shard_map/total_3/pallas_call | solution.py:1385
  530.2 1.1 bitcast_reduce_fusion
  531.4 2.2 multiply_reduce_fusion
  533.6 1.5 fusion.50
  535.1 16.5 %gather_4.1 = bf16[512,2048]{1,0:T(8,128)(2,1)} custom-call(bf16[128,2048]{1,0:T(8,128)(2,1)} %get-tuple-element.86.refs_0_), custom_call_target="tpu_custom_call" | custom-call | tf_op jit(solution)/shard_map/gather_4/pallas_call | solution.py:905
  551.7 3.7 multiply_reduce_fusion.2
  555.4 2.6 convolution_convert_fusion.1
  558.0 1.4 fusion.9
  559.4 1.7 multiply_convert_fusion
  564.8 1.0 copy-done.15
  567.6 16.6 %row_sum_9.1 = bf16[512,576]{1,0:T(8,128)(2,1)} custom-call(bf16[512,576]{1,0:T(8,128)(2,1)} %pad_maximum_fusion.7.value_ref), custom_call_target="tpu_custom_call" | custom-call | tf_op jit(solution)/shard_map/row_sum_9/pallas_call | solution.py:1449
  584.2 2.3 slice.158
  586.8 2.1 subtract_convert_fusion.1
  589.6 1.2 copy.202
  590.8 5.7 all-to-all-start.1
  597.5 1.0 pad_maximum_fusion.6
  598.6 1.3 fusion.34
  601.9 1.7 pad_maximum_fusion.refs_1_
  603.6 1.9 convolution_convert_fusion.4.refs_2_
  605.5 1.8 fusion.57
  607.3 3.3 convolution_add_fusion.refs_3_
  610.7 3.5 convolution_convert_fusion.refs_0_
  614.1 6.8 all-to-all-done.1
  621.0 149.7 %total_7.1 = (f32[256,768]{1,0:T(8,128)}, f32[656,256]{1,0:T(8,128)}, f32[64,1024]{1,0:T(8,128)}, f32[128,2048]{1,0:T(8,128)}, f32[128,2048]{1,0:T(8,128)}, /*in...) custom-call(bf16[2048,768]{1,0:T(8,128)(2,1)} %convolution_convert_fusion.refs_0_, ...), custom_call_target="tpu_custom_call" | custom-call | tf_op jit(solution)/shard_map/total_7/pallas_call | solution.py:1385
  770.7 0.9 reduce_sum.218
  772.2 1.4 fusion.16
  774.9 1.8 select_reduce_fusion
  776.7 9.8 %fusion.22 = f32[2048,64]{0,1:T(8,128)} fusion(bf16[4096,2048]{1,0:T(8,128)(2,1)} %get-tuple-element.56.x_ref, bf16[32,128,64]{1,2,0:T(8,128)(2,1)S(1)} %select_reduce_fusion), kind=kOutput, calls=%fused_computation.83 | convolution fusion | flops 1073741824 | bytes 17825792 | tf_op jit(solution)/shard_map/dot_general | solution.py:27
  788.2 1.4 convert_bitcast_fusion
  789.6 1.4 fusion.51
  792.6 1.7 fusion.15
  (201 shorter events, 26.2 us)
Async XLA Ops:
  0.6 5.3 copy-start
  0.7 6.1 copy-start.7
  0.7 5.3 copy-start.52
  0.7 6.0 copy-start.54
  2.6 5.5 copy-start.58
  6.7 133.8 %copy-start.49 = (bf16[704,256]{1,0:T(8,128)(2,1)S(1)}, bf16[704,256]{1,0:T(8,128)(2,1)}, u32[]{:S(2)}) copy-start(bf16[704,256]{1,0:T(8,128)(2,1)} %param.31) | copy-start | bytes 1081348
  140.6 19.9 %copy-start.9 = (bf16[512,2048]{1,0:T(8,128)(2,1)S(1)}, bf16[512,2048]{1,0:T(8,128)(2,1)}, u32[]{:S(2)}) copy-start(bf16[512,2048]{1,0:T(8,128)(2,1)} %get-tuple-element.51) | copy-start | bytes 6291460
  142.9 167.1 %all-to-all-start = ((bf16[8,264,256]{2,1,0:T(8,128)(2,1)}), bf16[8,264,256]{2,1,0:T(8,128)(2,1)}, u32[]{:S(2)}, u32[]{:S(2)}) async-start(bf16[8,264,256]{2,1,0:T(8,128)(2,1)} %bitcast.167), calls=%async_computation | async-start | bytes 2162688 | tf_op jit(solution)/shard_map/all_to_all | solution.py:1902
  174.9 4.0 copy-start.57
  176.6 3.1 copy-start.2
  176.6 2.5 copy-start.36
  176.6 3.1 copy-start.56
  179.1 13.3 %copy-start.34 = (pred[512,512]{0,1:T(8,128)(4,1)}, pred[512,512]{0,1:T(8,128)(4,1)S(1)}, u32[]{:S(2)}) copy-start(pred[512,512]{0,1:T(8,128)(4,1)S(1)} %fusion.17) | copy-start | bytes 786436
  179.4 10.8 %copy-start.41 = (f32[512,32]{0,1:T(8,128)}, f32[512,32]{0,1:T(8,128)S(1)}, u32[]{:S(2)}) copy-start(f32[512,32]{0,1:T(8,128)S(1)} %copy.183) | copy-start | bytes 196612
  182.7 3.6 copy-start.10
  186.2 4.2 copy-start.23
  190.2 1.2 copy-start.25
  190.3 1.1 copy-start.43
  190.3 1.1 copy-start.45
  190.4 1.1 copy-start.32
  191.5 2.0 copy-start.13
  191.5 2.0 copy-start.20
  193.5 2.2 copy-start.47
  215.8 2.5 copy-start.53
  215.8 2.7 copy-start.31
  217.3 1.0 copy-start.4
  218.5 2.6 copy-start.12
  530.2 3.4 copy-start.5
  530.2 3.4 copy-start.17
  535.1 16.6 %copy-start.63 = (bf16[4,128,512]{2,1,0:T(8,128)(2,1)S(1)}, bf16[4,128,512]{2,1,0:T(8,128)(2,1)}, u32[]{:S(2)}) copy-start(bf16[4,128,512]{2,1,0:T(8,128)(2,1)} %copy-done.62) | copy-start | bytes 1572868
  551.7 3.7 copy-start.22
  555.4 2.6 copy-start.14
  555.4 2.6 copy-start.35
  558.0 1.4 copy-start.21
  559.3 1.8 copy-start.26
  559.4 1.8 copy-start.44
  559.4 1.8 copy-start.46
  561.2 1.0 copy-start.24
  561.2 1.1 copy-start.33
  563.1 2.7 copy-start.38
  564.8 1.0 copy-start.15
  584.2 2.3 copy-start.8
  584.2 2.4 copy-start.3
  586.5 2.4 copy-start.37
  586.6 2.4 copy-start.28
  590.8 30.2 %all-to-all-start.1 = ((bf16[8,264,256]{2,1,0:T(8,128)(2,1)}), bf16[8,264,256]{2,1,0:T(8,128)(2,1)}, u32[]{:S(2)}, u32[]{:S(2)}) async-start(bf16[8,264,256]{2,1,0:T(8,128)(2,1)} %copy.202), calls=%async_computation.1 | async-start | bytes 2162688 | tf_op jit(solution)/shard_map/all_to_all | solution.py:1999
  596.5 1.0 copy-start.27
  596.5 3.3 copy-start.11
  596.5 3.3 copy-start.30
  598.6 3.3 copy-start.29
  601.9 1.7 copy-start.16
  603.6 1.9 copy-start.61
  621.0 151.2 %copy-start.55 = (f32[2048]{0:T(1024)S(1)}, f32[2048]{0:T(1024)}, u32[]{:S(2)}) copy-start(f32[2048]{0:T(1024)} %param.21) | copy-start | bytes 24580
  776.7 9.8 %copy-start.48 = (f32[656,256]{1,0:T(8,128)S(1)}, f32[656,256]{1,0:T(8,128)}, u32[]{:S(2)}) copy-start(f32[656,256]{1,0:T(8,128)} %get-tuple-element.77) | copy-start | bytes 2015236
  776.7 10.6 %copy-start.50 = (bf16[576,256]{1,0:T(8,128)(2,1)S(1)}, bf16[576,256]{1,0:T(8,128)(2,1)}, u32[]{:S(2)}) copy-start(bf16[576,256]{1,0:T(8,128)(2,1)} %get-tuple-element.75) | copy-start | bytes 884740
  789.6 1.7 copy-start.6
  789.6 2.3 copy-start.18
  789.6 2.6 copy-start.19
  789.6 2.9 copy-start.39
  789.6 2.9 copy-start.59
  789.6 2.9 copy-start.60
  792.5 1.8 copy-start.40
  792.5 2.6 copy-start.51
  792.6 3.3 copy-start.1
  (2 other events, 1.6 us)
